TPU v7x, 128 devices: a whole 4x4x4 slice. The times are simulated.
128 devices in a mesh: dp: 64 (over x, y, z_lo, core), section: 2 (over z_hi).
Axes of the slice: x: 4, y: 4, z: 4 (z_hi: 2, z_lo: 2; z = z_hi * 2 + z_lo), core: 2. Of those that a mesh axis runs over, the one named last changes fastest.
Arguments:
- samples: bfloat16 [512, 512], P('dp'), may hold values from -16 to 16
- targets: bfloat16 [512, 512], P('dp'), may hold values from -16 to 16
- jacobian_targets: bfloat16 [512, 128, 512], P('dp'), may hold values from -0.1796875 to 0.1796875
- directions: int32 [512, 128], P('dp'), may hold values from 0 to 511
- plan: int32 [64, 8], P('dp'), may hold values from 0 to 7, each once within a row
- weights: bfloat16 [2, 512, 8192], P('section'), may hold values from -1 to 1
Outputs:
- gradients: float32 [2, 512, 8192], P('section', 'dp')
Inputs may be any that keep to these rules, and one draw needn't show every extreme that they name: `plan`: each row is a permutation of 0 to 7.
All inputs are finite; a program needn't handle non-finite values.
Results may differ from a plain program's by a relative error of at most 0.0034.
Values may be sent and summed in bfloat16 or wider, within the bound.
No kernel may reach another device: no remote copies, remote signals or barrier semaphores. Data moves between devices by JAX's collectives and lax.ppermute only.
A program may use at most 128 MiB of HBM per device.

v0:
```python
import jax
import jax.numpy as jnp
from jax import lax
from jax.sharding import Mesh
from jax.sharding import PartitionSpec as P

MICRO = 4
BATCH = 1
DP = ("dp_0", "dp_1", "dp_2", "dp_3")


jacobian_weight = 32.0


def partner(block, axis, distance):
    count = lax.axis_size(axis)
    route = []
    for low in range(count):
        high = low | 1 << distance
        if high != low and high < count:
            route += [(low, high), (high, low)]
    return lax.ppermute(block, axis, route)


def sent_to_all(shard, axis):
    copies = jnp.broadcast_to(shard, (lax.axis_size(axis), *shard.shape))
    return lax.all_to_all(copies, axis, split_axis=0, concat_axis=0, tiled=True)


def of_everyone(shard, axis):
    return sent_to_all(shard, axis).sum(axis=0)


def packed_total(arrays, axis):
    ends = [0]
    for a in arrays:
        ends.append(ends[-1] + a.size)
    subtotal = of_everyone(jnp.concatenate([a.ravel() for a in arrays]), axis)
    return tuple((subtotal[b:e].reshape(a.shape) for a, b, e in zip(arrays, ends, ends[1:])))


def cut_along(shard, dim, length):
    before, after = (shard.shape[:dim], shard.shape[dim + 1 :])
    return jnp.moveaxis(shard.reshape(*before, length, -1, *after), dim, 0)


def scatter_pairs(shard, chips, core, dim):
    sizes = (lax.axis_size(chips), lax.axis_size(core))
    tiles = cut_along(shard, dim, sizes[0] * sizes[1])
    inside = tiles.shape[1:]
    tiles = tiles.reshape(*sizes, *inside).swapaxes(0, 1).reshape(-1, *inside)
    tiles = lax.psum_scatter(tiles, core, scatter_dimension=0, tiled=True)
    return lax.psum_scatter(tiles, chips, scatter_dimension=0, tiled=True)[0]


def contract_rows(left, right):
    return lax.dot_general(
        left, right, (((0,), (0,)), ((), ())), preferred_element_type=jnp.float32
    )


def against_rows(left, right):
    return lax.dot_general(
        left, right, (((1,), (1,)), ((), ())), preferred_element_type=jnp.float32
    )


def encoder_parts(inputs, chosen_dirs, w_first):
    linear = jnp.dot(inputs, w_first, preferred_element_type=jnp.float32)
    squash = jax.nn.sigmoid(linear)
    first_slope = squash * (1.0 + linear * (1.0 - squash))
    second_slope = squash * (1.0 - squash) * (2.0 + linear * (1.0 - 2.0 * squash))
    picked = jnp.take(w_first, chosen_dirs, axis=0)
    return (linear, squash, first_slope, second_slope, picked)


def encoder_forward(encoded):
    linear, squash, first_slope, second_slope, picked = encoded
    hidden = (linear * squash).astype(jnp.bfloat16)
    tangent = (first_slope[:, None, :] * picked.astype(jnp.float32)).astype(jnp.bfloat16)
    return (hidden, tangent)


def encoder_backward(inputs, chosen_dirs, encoded, cotangent, cotangent_tangent, reduced):
    linear, squash, first_slope, second_slope, picked = encoded
    projected = jnp.sum(cotangent_tangent.astype(jnp.float32) * picked.astype(jnp.float32), axis=1)
    grad_pre = (cotangent.astype(jnp.float32) * first_slope + second_slope * projected).astype(
        jnp.bfloat16
    )
    grad_picked = (cotangent_tangent.astype(jnp.float32) * first_slope[:, None, :]).astype(
        jnp.bfloat16
    )
    columns = grad_pre.shape[1]
    onehot = (
        chosen_dirs.reshape(-1)[:, None] == jnp.arange(reduced, dtype=jnp.int32)[None, :]
    ).astype(jnp.bfloat16)
    return contract_rows(inputs, grad_pre) + contract_rows(onehot, grad_picked.reshape(-1, columns))


def shards(samples, targets, jacobian_targets, directions, plan, weights):
    section_index = lax.axis_index("section")
    weight = weights[0]
    reduced, columns = weight.shape
    order_row = plan[0]

    def batch_slots(micro_index):
        return lax.dynamic_slice_in_dim(order_row, micro_index * BATCH, BATCH)

    def encoder_rows(micro_index):
        chosen = batch_slots(micro_index)
        return (jnp.take(samples, chosen, axis=0), jnp.take(directions, chosen, axis=0))

    def decoder_rows(micro_index):
        chosen = batch_slots(micro_index)
        return (jnp.take(targets, chosen, axis=0), jnp.take(jacobian_targets, chosen, axis=0))

    half = columns // 2
    keep_part = lax.dynamic_slice_in_dim(weight, section_index * half, half, 1)
    give_part = lax.dynamic_slice_in_dim(weight, (1 - section_index) * half, half, 1)
    other_part = partner(give_part, "section", 0)
    w_first, w_last = lax.cond(
        section_index == 0, lambda: (keep_part, other_part), lambda: (other_part, keep_part)
    )
    cleared_half = jnp.zeros((reduced, half), jnp.float32)

    def advance(current, carried):
        first_total, last_total = carried
        inputs, chosen_dirs = encoder_rows(current)
        target_rows, jacobian_rows = decoder_rows(current)
        encoded = encoder_parts(inputs, chosen_dirs, w_first)
        hidden, tangent = encoder_forward(encoded)
        flattened = tangent.reshape(-1, half)
        output, jacobian = packed_total(
            (against_rows(hidden, w_last), against_rows(flattened, w_last)), "section"
        )
        misfit = (output - target_rows.astype(jnp.float32)).astype(jnp.bfloat16)
        jac_misfit = (
            jacobian_weight * (jacobian - jacobian_rows.reshape(jacobian.shape).astype(jnp.float32))
        ).astype(jnp.bfloat16)
        grad_last = contract_rows(misfit, hidden) + contract_rows(jac_misfit, flattened)
        cotangent = jnp.dot(misfit, w_last, preferred_element_type=jnp.float32).astype(jnp.bfloat16)
        cotangent_tangent = jnp.dot(jac_misfit, w_last, preferred_element_type=jnp.float32).astype(
            jnp.bfloat16
        )
        cotangent_tangent = cotangent_tangent.reshape(tangent.shape)
        grad_first = encoder_backward(
            inputs, chosen_dirs, encoded, cotangent, cotangent_tangent, reduced
        )
        return (first_total + grad_first, last_total + grad_last)

    first_total, last_total = lax.fori_loop(0, MICRO, advance, (cleared_half, cleared_half))
    stacked = jnp.stack([first_total, last_total])
    row_sums = scatter_pairs(stacked, ("dp_0", "dp_1", "dp_2"), "dp_3", 1)
    result = lax.all_to_all(row_sums, "section", split_axis=0, concat_axis=2, tiled=True)
    return result


def solution(mesh):
    torus = Mesh(
        mesh.devices.reshape(4, 4, 2, 2, mesh.shape["section"]),
        ("dp_0", "dp_1", "dp_2", "dp_3", "section"),
    )
    return jax.shard_map(
        shards,
        mesh=torus,
        in_specs=(
            P(DP, None),
            P(DP, None),
            P(DP, None, None),
            P(DP, None),
            P(DP, None),
            P("section", None, None),
        ),
        out_specs=P("section", DP, None),
        check_vma=False,
    )
```

profile of v0, /device:TPU:1, one launch (start us, length us, event | category | flops | bytes accessed | tf_op | source)
XLA Modules:
  0.0 571.4 jit_solution(5117243101292586576)
XLA Ops:
  6.5 7.8 %dynamic-slice_bitcast_fusion = (bf16[512,4096]{1,0:T(8,128)(2,1)}, bf16[512,4096]{1,0:T(8,128)(2,1)}) fusion(bf16[1,512,8192]{2,1,0:T(8,128)(2,1)} %param.17, s32[]{:T(128)S(6)} %select_n.137, s32[]{:T(128)S(6)} %select_n.136), kind=kLoop, calls=%fused_computation.49 | loop fusion | bytes 16777224 | tf_op jit(solution)/shard_map/dynamic_slice | solution.py:118
  14.4 4.4 collective-permute-start
  18.8 90.6 %collective-permute-done = bf16[512,4096]{1,0:T(8,128)(2,1)} collective-permute-done((bf16[512,4096]{1,0:T(8,128)(2,1)}, bf16[512,4096]{1,0:T(8,128)(2,1)}, u32[]{:S(2)}, u32[]{:S(2)}) %collective-permute-start) | collective-permute-done | bytes 4194336 | tf_op jit(solution)/shard_map/ppermute | solution.py:22
  109.4 6.9 %conditional.1 = (bf16[512,4096]{1,0:T(8,128)(2,1)S(1)}, bf16[512,4096]{1,0:T(8,128)(2,1)}) conditional(s32[]{:T(128)} %convert_element_type.116, (bf16[512,4096]{1,0:T(8,128)(2,1)}, bf16[512,4096]{1,0:T(8,128)(2,1)}) %tuple.26, (bf16[512,4096]{1,0:T(8,128)(2,1)}, bf16[512,4096]{1,0:T(8,128)(2,1)}) %tuple.27), branch_computations={%region_0.0_spmd, %region_1.0_spmd} | conditional | bytes 16777232 | solution.py:121
  109.4 2.2 copy.19
  111.6 4.7 copy.20
  116.3 1.9 copy-done.2
  118.2 200.7 %while.19 = (s32[]{:T(128)}, f32[512,4096]{1,0:T(8,128)}, f32[512,4096]{1,0:T(8,128)}, s32[8]{0:T(128)S(1)}, bf16[8,512]{1,0:T(8,128)(2,1)S(1)}, /*index=5*/bf16...) while((s32[]{:T(128)}, f32[512,4096]{1,0:T(8,128)}, ...), condition=%wide.region_5.7_spmd.clone, body=%wide.region_2.6_spmd.clone.sunk | while | flops 2186210560 | bytes 104153424 | solution.py:151
  121.5 2.8 fusion.70
  124.4 4.9 gather_fusion
  129.3 3.5 fusion.72
  135.6 3.5 all-to-all-start
  139.1 8.3 %all-to-all-done = f32[2,1,66048]{2,1,0:T(1,128)S(1)} async-done(((f32[2,1,66048]{2,1,0:T(1,128)}), f32[2,1,66048]{2,1,0:T(1,128)S(1)}, u32[]{:S(2)}, u32[]{:S(2)}) %all-to-all-start) | async-done | bytes 528416 | tf_op jit(solution)/shard_map/while/body/eval_jaxpr/all_to_all | solution.py:27
  149.2 3.1 fusion.75
  152.2 1.8 fusion.73
  154.1 5.8 %select_add_fusion.5 = f32[512,4096]{1,0:T(8,128)} fusion(f32[512,4096]{1,0:T(8,128)} %get-tuple-element.391, f32[4096]{0:T(1024)S(1)} %get-tuple-element.367, f32[512]{0:T(512)S(1)} %convert.45, pred[]{:T(512)S(6)} %compare.6, f32[4096]{0:T(1024)S(1)} %get-tuple-element.361, bf16[128,4096]{1,0:T(8,128)(2,1)S(1)} %gather_fusion, ...), kind=kOutput, calls=%fused_computation.1.clone.1 | convolution fusion | flops 547684352 | bytes 18254976 | tf_op jit(solution)/shard_map/while/body/eval_jaxpr/dot_general | solution.py:57
  159.9 4.9 select_add_fusion.4
  168.1 2.8 fusion.70
  171.0 4.9 gather_fusion
  175.9 3.5 fusion.72
  182.2 3.5 all-to-all-start
  185.7 7.5 %all-to-all-done = f32[2,1,66048]{2,1,0:T(1,128)S(1)} async-done(((f32[2,1,66048]{2,1,0:T(1,128)}), f32[2,1,66048]{2,1,0:T(1,128)S(1)}, u32[]{:S(2)}, u32[]{:S(2)}) %all-to-all-start) | async-done | bytes 528416 | tf_op jit(solution)/shard_map/while/body/eval_jaxpr/all_to_all | solution.py:27
  195.0 3.1 fusion.75
  198.0 1.8 fusion.73
  199.9 8.3 %select_add_fusion.5 = f32[512,4096]{1,0:T(8,128)} fusion(f32[512,4096]{1,0:T(8,128)} %get-tuple-element.391, f32[4096]{0:T(1024)S(1)} %get-tuple-element.367, f32[512]{0:T(512)S(1)} %convert.45, pred[]{:T(512)S(6)} %compare.6, f32[4096]{0:T(1024)S(1)} %get-tuple-element.361, bf16[128,4096]{1,0:T(8,128)(2,1)S(1)} %gather_fusion, ...), kind=kOutput, calls=%fused_computation.1.clone.1 | convolution fusion | flops 547684352 | bytes 18254976 | tf_op jit(solution)/shard_map/while/body/eval_jaxpr/dot_general | solution.py:57
  208.2 8.3 %select_add_fusion.4 = f32[512,4096]{1,0:T(8,128)} fusion(f32[512,4096]{1,0:T(8,128)} %get-tuple-element.390, f32[4096]{0:T(1024)S(1)} %fusion.76, f32[512]{0:T(512)S(1)} %convert.44, pred[]{:T(512)S(6)} %compare.6, f32[128,4096]{1,0:T(8,128)S(1)} %get-tuple-element.366, f32[4096]{0:T(1024)S(1)} %get-tuple-element.361, s32[128]{0:T(128)S(1)} %bitcast.110), kind=kOutput, calls=%fused_computation.2.clone.1 | convolution fusion | flops 546373632 | bytes 18909696 | tf_op jit(solution)/shard_map/while/body/eval_jaxpr/dot_general | solution.py:57
  219.8 2.8 fusion.70
  222.7 4.9 gather_fusion
  227.7 3.5 fusion.72
  233.9 3.5 all-to-all-start
  237.4 6.9 %all-to-all-done = f32[2,1,66048]{2,1,0:T(1,128)S(1)} async-done(((f32[2,1,66048]{2,1,0:T(1,128)}), f32[2,1,66048]{2,1,0:T(1,128)S(1)}, u32[]{:S(2)}, u32[]{:S(2)}) %all-to-all-start) | async-done | bytes 528416 | tf_op jit(solution)/shard_map/while/body/eval_jaxpr/all_to_all | solution.py:27
  246.1 3.1 fusion.75
  251.0 8.3 %select_add_fusion.5 = f32[512,4096]{1,0:T(8,128)} fusion(f32[512,4096]{1,0:T(8,128)} %get-tuple-element.391, f32[4096]{0:T(1024)S(1)} %get-tuple-element.367, f32[512]{0:T(512)S(1)} %convert.45, pred[]{:T(512)S(6)} %compare.6, f32[4096]{0:T(1024)S(1)} %get-tuple-element.361, bf16[128,4096]{1,0:T(8,128)(2,1)S(1)} %gather_fusion, ...), kind=kOutput, calls=%fused_computation.1.clone.1 | convolution fusion | flops 547684352 | bytes 18254976 | tf_op jit(solution)/shard_map/while/body/eval_jaxpr/dot_general | solution.py:57
  259.4 8.3 %select_add_fusion.4 = f32[512,4096]{1,0:T(8,128)} fusion(f32[512,4096]{1,0:T(8,128)} %get-tuple-element.390, f32[4096]{0:T(1024)S(1)} %fusion.76, f32[512]{0:T(512)S(1)} %convert.44, pred[]{:T(512)S(6)} %compare.6, f32[128,4096]{1,0:T(8,128)S(1)} %get-tuple-element.366, f32[4096]{0:T(1024)S(1)} %get-tuple-element.361, s32[128]{0:T(128)S(1)} %bitcast.110), kind=kOutput, calls=%fused_computation.2.clone.1 | convolution fusion | flops 546373632 | bytes 18909696 | tf_op jit(solution)/shard_map/while/body/eval_jaxpr/dot_general | solution.py:57
  271.0 2.8 fusion.70
  273.9 4.9 gather_fusion
  278.8 3.5 fusion.72
  285.1 3.5 all-to-all-start
  288.6 6.9 %all-to-all-done = f32[2,1,66048]{2,1,0:T(1,128)S(1)} async-done(((f32[2,1,66048]{2,1,0:T(1,128)}), f32[2,1,66048]{2,1,0:T(1,128)S(1)}, u32[]{:S(2)}, u32[]{:S(2)}) %all-to-all-start) | async-done | bytes 528416 | tf_op jit(solution)/shard_map/while/body/eval_jaxpr/all_to_all | solution.py:27
  297.3 3.1 fusion.75
  300.3 1.8 fusion.73
  302.2 8.3 %select_add_fusion.5 = f32[512,4096]{1,0:T(8,128)} fusion(f32[512,4096]{1,0:T(8,128)} %get-tuple-element.391, f32[4096]{0:T(1024)S(1)} %get-tuple-element.367, f32[512]{0:T(512)S(1)} %convert.45, pred[]{:T(512)S(6)} %compare.6, f32[4096]{0:T(1024)S(1)} %get-tuple-element.361, bf16[128,4096]{1,0:T(8,128)(2,1)S(1)} %gather_fusion, ...), kind=kOutput, calls=%fused_computation.1.clone.1 | convolution fusion | flops 547684352 | bytes 18254976 | tf_op jit(solution)/shard_map/while/body/eval_jaxpr/dot_general | solution.py:57
  310.6 8.3 %select_add_fusion.4 = f32[512,4096]{1,0:T(8,128)} fusion(f32[512,4096]{1,0:T(8,128)} %get-tuple-element.390, f32[4096]{0:T(1024)S(1)} %fusion.76, f32[512]{0:T(512)S(1)} %convert.44, pred[]{:T(512)S(6)} %compare.6, f32[128,4096]{1,0:T(8,128)S(1)} %get-tuple-element.366, f32[4096]{0:T(1024)S(1)} %get-tuple-element.361, s32[128]{0:T(128)S(1)} %bitcast.110), kind=kOutput, calls=%fused_computation.2.clone.1 | convolution fusion | flops 546373632 | bytes 18909696 | tf_op jit(solution)/shard_map/while/body/eval_jaxpr/dot_general | solution.py:57
  318.9 6.6 %pad_maximum_fusion.1 = f32[2,64,8,4096]{3,2,1,0:T(8,128)S(1)} fusion(f32[1,64,8,4096]{3,2,1,0:T(8,128)} %bitcast.99, f32[1,64,8,4096]{3,2,1,0:T(8,128)} %bitcast.3), kind=kLoop, calls=%fused_computation.48 | loop fusion | flops 4194304 | bytes 33554432 | tf_op jit(solution)/shard_map/stack | solution.py:152
  325.5 6.0 %copy.10 = f32[32,2,2,8,4096]{4,3,2,0,1:T(8,128)} copy(f32[32,2,2,8,4096]{4,3,1,0,2:T(8,128)S(1)} %bitcast.101) | data formatting | bytes 33554432 | tf_op jit(solution)/shard_map/reshape | solution.py:51
  331.6 31.9 %reduce-scatter.3.cloned.1.call-done = f32[32,2,8,4096]{3,2,1,0:T(8,128)} async-done(((f32[64,2,8,4096]{3,2,1,0:T(8,128)}), f32[32,2,8,4096]{3,2,1,0:T(8,128)}) %reduce-scatter.3.cloned.1.call-update) | async-done | bytes 8388624 | tf_op jit(solution)/shard_map/reduce_scatter | solution.py:52
  363.5 191.4 %reduce-scatter.5.cloned.1.call-done = f32[1,2,8,4096]{3,2,1,0:T(8,128)} async-done(((f32[32,2,8,4096]{3,2,1,0:T(8,128)}), f32[1,2,8,4096]{3,2,1,0:T(8,128)}) %reduce-scatter.5.cloned.1.call-update) | async-done | bytes 262160 | tf_op jit(solution)/shard_map/reduce_scatter | solution.py:53
  554.9 9.0 %all_to_all.30 = f32[2,8,4096]{2,1,0:T(8,128)S(1)} all-to-all(f32[2,8,4096]{2,1,0:T(8,128)} %bitcast.107), channel_id=1, replica_groups=mesh['dp_0'=4,'dp_1'=4,'dp_2'=2,'dp_3'=2,'section'=2] {'section'}, dimensions={0} | all-to-all | bytes 524288 | tf_op jit(solution)/shard_map/all_to_all | solution.py:154
  (101 shorter events, 25.8 us)
Async XLA Ops:
  6.5 357.0 %reduce-scatter.3.cloned.1.call-start = ((), (), s32[]{:S(2)}) async-start(), calls=%async_computation.4 | async-start | bytes 25165824 | tf_op jit(solution)/shard_map/reduce_scatter | solution.py:52
  14.4 95.0 %collective-permute-start = (bf16[512,4096]{1,0:T(8,128)(2,1)}, bf16[512,4096]{1,0:T(8,128)(2,1)}, u32[]{:S(2)}, u32[]{:S(2)}) collective-permute-start(bf16[512,4096]{1,0:T(8,128)(2,1)} %get-tuple-element.287), channel_id=1, source_target_pairs={{0,1},{1,0},{2,3},{3,2},{4,5},{5,4},{6,7},{7,6},{8,9},{9,8},{10,11... | collective-permute-start | bytes 12582920 | tf_op jit(solution)/shard_map/ppermute | solution.py:22
  109.4 8.8 %copy-start.3 = (bf16[8,512]{1,0:T(8,128)(2,1)S(1)}, bf16[8,512]{1,0:T(8,128)(2,1)}, u32[]{:S(2)}) copy-start(bf16[8,512]{1,0:T(8,128)(2,1)} %param.12) | copy-start | bytes 24580
  109.4 8.8 %copy-start.4 = (s32[1,8]{1,0:T(1,128)S(1)}, s32[1,8]{1,0:T(1,128)}, u32[]{:S(2)}) copy-start(s32[1,8]{1,0:T(1,128)} %param.16) | copy-start | bytes 100
  116.3 1.9 copy-start.2
  129.3 3.5 copy-start
  135.6 11.9 %all-to-all-start = ((f32[2,1,66048]{2,1,0:T(1,128)}), f32[2,1,66048]{2,1,0:T(1,128)S(1)}, u32[]{:S(2)}, u32[]{:S(2)}) async-start(f32[2,1,66048]{2,1,0:T(1,128)} %broadcast_in_dim.163), calls=%async_computation | async-start | bytes 1056768 | tf_op jit(solution)/shard_map/while/body/eval_jaxpr/all_to_all | solution.py:27
  148.3 4.0 copy-start.1
  175.9 3.5 copy-start
  182.2 11.0 %all-to-all-start = ((f32[2,1,66048]{2,1,0:T(1,128)}), f32[2,1,66048]{2,1,0:T(1,128)S(1)}, u32[]{:S(2)}, u32[]{:S(2)}) async-start(f32[2,1,66048]{2,1,0:T(1,128)} %broadcast_in_dim.163), calls=%async_computation | async-start | bytes 1056768 | tf_op jit(solution)/shard_map/while/body/eval_jaxpr/all_to_all | solution.py:27
  194.1 4.0 copy-start.1
  227.6 3.5 copy-start
  233.9 10.4 %all-to-all-start = ((f32[2,1,66048]{2,1,0:T(1,128)}), f32[2,1,66048]{2,1,0:T(1,128)S(1)}, u32[]{:S(2)}, u32[]{:S(2)}) async-start(f32[2,1,66048]{2,1,0:T(1,128)} %broadcast_in_dim.163), calls=%async_computation | async-start | bytes 1056768 | tf_op jit(solution)/shard_map/while/body/eval_jaxpr/all_to_all | solution.py:27
  245.2 4.0 copy-start.1
  278.8 3.5 copy-start
  285.1 10.4 %all-to-all-start = ((f32[2,1,66048]{2,1,0:T(1,128)}), f32[2,1,66048]{2,1,0:T(1,128)S(1)}, u32[]{:S(2)}, u32[]{:S(2)}) async-start(f32[2,1,66048]{2,1,0:T(1,128)} %broadcast_in_dim.163), calls=%async_computation | async-start | bytes 1056768 | tf_op jit(solution)/shard_map/while/body/eval_jaxpr/all_to_all | solution.py:27
  296.4 4.0 copy-start.1
  331.5 223.4 %reduce-scatter.5.cloned.1.call-start = ((), (), s32[]{:S(2)}) async-start(), calls=%async_computation.5 | async-start | bytes 8650752 | tf_op jit(solution)/shard_map/reduce_scatter | solution.py:53
Sparse Core Ops, SparseCore 0:
  331.6 31.8 reduce-scatter.2
  365.9 188.9 reduce-scatter.4
where the time goes:
time: 575 us; the launch traced here: 571 us
  waiting for transfers between devices  344 us (60%)
  matrix products  112 us (19%)
  local copies, waits for them, and re-layouts  50.5 us (9%)
  starting transfers between devices  18.4 us (3%)
  other arithmetic  16.2 us (3%)
  between operations  13.4 us (2%)
  blocking collectives  8.96 us (2%)
  loops' own time  8.37 us (1%)
    reduce_scatter x1, waiting for transfers between devices, scatter_pairs(): return lax.psum_scatter(tiles, chips, scatter_dimension=0, tiled=True)[0]  191 us
    ppermute x1, waiting for transfers between devices, partner(): return lax.ppermute(block, axis, route)  90.6 us
    dot_general x8, matrix products, contract_rows(): lax.dot_general(left, right, (((0,), (0,)), ((), ())), preferred_element_...  60.7 us
    reduce_scatter x1, waiting for transfers between devices, scatter_pairs(): tiles = lax.psum_scatter(tiles, core, scatter_dimension=0, tiled=True)  31.9 us
    all_to_all x4, waiting for transfers between devices, sent_to_all(): return lax.all_to_all(copies, axis, split_axis=0, concat_axis=0, tiled=True)  29.7 us
    dot_general x8, matrix products, against_rows(): lax.dot_general(left, right, (((1,), (1,)), ((), ())), preferred_element_...  20.3 us
    gather x4, local copies, waits for them, and re-layouts, encoder_parts(): picked = jnp.take(w_first, chosen_dirs, axis=0)  19.7 us
    all_to_all x4, starting transfers between devices, sent_to_all(): return lax.all_to_all(copies, axis, split_axis=0, concat_axis=0, tiled=True)  14 us
  transfers between devices with their start and end apart: 7, of which 7 were waited for; matrix products, arithmetic and copies ran while one was open for 0% of the time, Pallas kernels for 0%

commit v1 on v0

v1 whole, which is shorter than its diff:
```python
import jax
import jax.numpy as jnp
from jax import lax
from jax.experimental import pallas as pl
from jax.experimental.pallas import tpu as pltpu
from jax.sharding import Mesh
from jax.sharding import PartitionSpec as P

AXES = ("x", "y", "zl", "core", "zh")
DP = ("x", "y", "zl", "core")
Z = ("zl", "zh")
MICRO = 4
REDUCED = 512
COLS = 1024
TANGENTS = 128
CHUNK = 2 * TANGENTS + 16
BLOCK = 256
jacobian_weight = 32.0
f32 = jnp.float32
bf16 = jnp.bfloat16


def z_index(z):
    return (z % 2) * 2 + z // 2


def z_shift(block, d):
    return lax.ppermute(block, Z, [(z_index(z), z_index((z + d) % 4)) for z in range(4)])


def ring_shift(block, axis, d):
    return lax.ppermute(block, axis, [(i, (i + d) % 4) for i in range(4)])


def core_swap(block):
    return lax.ppermute(block, "core", [(0, 1), (1, 0)])


def slopes(linear):
    squash = jax.nn.sigmoid(linear)
    first = squash * (1.0 + linear * (1.0 - squash))
    second = squash * (1.0 - squash) * (2.0 + linear * (1.0 - 2.0 * squash))
    return linear * squash, first, second


def per_row(top, first):
    return jnp.concatenate(
        [top[:TANGENTS] * first[0:1], top[TANGENTS : 2 * TANGENTS] * first[1:2]], axis=0
    )


def forward_kernel(place, rows, own, other, out, w_first, w_last):
    @pl.when(pl.program_id(0) == 0)
    def _():
        layer = place[1]
        w_first[...] = jnp.where(layer == 0, own[...], other[...])
        w_last[...] = jnp.where(layer == 0, other[...], own[...])

    picked = jnp.dot(rows[0], w_first[...], preferred_element_type=f32)
    hidden, first, _ = slopes(picked[2 * TANGENTS :])
    tangent = jnp.concatenate([per_row(picked, first), hidden], axis=0).astype(bf16)
    total = lax.dot_general(
        tangent, w_last[...], (((1,), (1,)), ((), ())), preferred_element_type=f32
    )
    out[0] = total.astype(out.dtype)


def forward(place, rows, weight, other, dtype):
    count = rows.shape[0]
    return pl.pallas_call(
        forward_kernel,
        grid_spec=pltpu.PrefetchScalarGridSpec(
            num_scalar_prefetch=1,
            grid=(count,),
            in_specs=[
                pl.BlockSpec((1, CHUNK, REDUCED), lambda i, place: (i, 0, 0)),
                pl.BlockSpec((REDUCED, COLS), lambda i, place: (0, place[0])),
                pl.BlockSpec((REDUCED, COLS), lambda i, place: (0, 0)),
            ],
            out_specs=pl.BlockSpec((1, CHUNK, REDUCED), lambda i, place: (i, 0, 0)),
            scratch_shapes=[
                pltpu.VMEM((REDUCED, COLS), bf16),
                pltpu.VMEM((REDUCED, COLS), bf16),
            ],
        ),
        out_shape=jax.ShapeDtypeStruct((count, CHUNK, REDUCED), dtype),
        compiler_params=pltpu.CompilerParams(dimension_semantics=("arbitrary",)),
        cost_estimate=pl.CostEstimate(
            flops=4 * count * CHUNK * REDUCED * COLS,
            bytes_accessed=4 * REDUCED * COLS,
            transcendentals=0,
        ),
    )(place, rows, weight, other)


def backward_kernel(place, rows, *refs):
    misfits = refs[:8]
    own, other, last_out, first_out, rows_t, misfit_t, tangents, cotangents = refs[8:]

    @pl.when(pl.program_id(0) == 0)
    def _():
        for k in range(8 * CHUNK // 128):
            rows_t[:, k * 128 : (k + 1) * 128] = rows[k * 128 : (k + 1) * 128, :].T
        whole = jnp.concatenate([m[...] for m in misfits], axis=0)
        for k in range(8 * CHUNK // 128):
            misfit_t[:, k * 128 : (k + 1) * 128] = whole[k * 128 : (k + 1) * 128, :].T

    layer = place[1]
    w_first = jnp.where(layer == 0, own[...], other[...])
    w_last = jnp.where(layer == 0, other[...], own[...])
    for c in range(8):
        span = pl.ds(c * CHUNK, CHUNK)
        picked = jnp.dot(rows[span, :], w_first, preferred_element_type=f32)
        hidden, first, second = slopes(picked[2 * TANGENTS :])
        tangents[span, :] = jnp.concatenate([per_row(picked, first), hidden], axis=0).astype(bf16)
        back = jnp.dot(misfits[c][...], w_last, preferred_element_type=f32)
        back = back.astype(bf16).astype(f32)
        joint = back[: 2 * TANGENTS] * picked[: 2 * TANGENTS]
        projected = jnp.concatenate(
            [
                jnp.sum(joint[:TANGENTS], axis=0, keepdims=True),
                jnp.sum(joint[TANGENTS:], axis=0, keepdims=True),
                jnp.zeros((14, BLOCK), f32),
            ],
            axis=0,
        )
        before = back[2 * TANGENTS :] * first + second * projected
        cotangents[span, :] = jnp.concatenate([per_row(back, first), before], axis=0).astype(bf16)
    last_out[...] = jnp.dot(misfit_t[...], tangents[...], preferred_element_type=f32).astype(bf16)
    first_out[...] = jnp.dot(rows_t[...], cotangents[...], preferred_element_type=f32).astype(bf16)


def backward(place, rows, misfits, weight, other):
    steps = COLS // BLOCK
    total = 8 * CHUNK
    return pl.pallas_call(
        backward_kernel,
        grid_spec=pltpu.PrefetchScalarGridSpec(
            num_scalar_prefetch=1,
            grid=(steps,),
            in_specs=[
                pl.BlockSpec((total, REDUCED), lambda j, place: (0, 0)),
                *[pl.BlockSpec((CHUNK, REDUCED), lambda j, place: (0, 0)) for _ in range(8)],
                pl.BlockSpec((REDUCED, BLOCK), lambda j, place: (0, place[0] * steps + j)),
                pl.BlockSpec((REDUCED, BLOCK), lambda j, place: (0, j)),
            ],
            out_specs=[
                pl.BlockSpec((REDUCED, BLOCK), lambda j, place: (0, j)),
                pl.BlockSpec((REDUCED, BLOCK), lambda j, place: (0, j)),
            ],
            scratch_shapes=[
                pltpu.VMEM((REDUCED, total), bf16),
                pltpu.VMEM((REDUCED, total), bf16),
                pltpu.VMEM((total, BLOCK), bf16),
                pltpu.VMEM((total, BLOCK), bf16),
            ],
        ),
        out_shape=[jax.ShapeDtypeStruct((REDUCED, COLS), bf16)] * 2,
        compiler_params=pltpu.CompilerParams(dimension_semantics=("arbitrary",)),
        cost_estimate=pl.CostEstimate(
            flops=8 * total * REDUCED * COLS, bytes_accessed=4 * REDUCED * COLS, transcendentals=0
        ),
    )(place, rows, *misfits, weight, other)


def ring_sum(chunks, at, axis):
    def piece(i):
        return lax.dynamic_index_in_dim(chunks, i % 4, 0, keepdims=False)

    got = [ring_shift(piece(at + d), axis, d) for d in (1, 3, 2)]
    total = piece(at).astype(f32)
    for g in got:
        total = total + g.astype(f32)
    return total


def shards(samples, targets, jacobian_targets, directions, plan, weights):
    at_x, at_y = lax.axis_index("x"), lax.axis_index("y")
    zl, core, zh = lax.axis_index("zl"), lax.axis_index("core"), lax.axis_index("zh")
    z = zh * 2 + zl
    weight = weights[0]
    mine = (zl * 2 + core) * 2 + zh
    theirs = ((1 - zl) * 2 + core) * 2 + (1 - zh)
    place = jnp.stack([mine, zh]).astype(jnp.int32)

    give = lax.dynamic_slice_in_dim(weight, theirs * COLS, COLS, 1)
    other = z_shift_partner(give)

    order = plan[0, :MICRO]
    inputs = jnp.take(samples, order, axis=0).astype(f32)
    chosen = jnp.take(directions, order, axis=0).astype(f32)
    small = lax.all_gather(jnp.concatenate([inputs, chosen], axis=1), ("zl", "core"))
    small = small.reshape(2, 2, 2, 2, REDUCED + TANGENTS).transpose(1, 2, 0, 3, 4)
    small = small.reshape(2, 4, 2, REDUCED + TANGENTS)
    small = jnp.where(core == 0, small, small[::-1])
    small = lax.dynamic_slice_in_dim(jnp.concatenate([small, small], axis=1), z, 4, 1)
    small = small.reshape(8, 2, REDUCED + TANGENTS)
    chosen = small[:, :, REDUCED:].reshape(8, 2 * TANGENTS).astype(jnp.int32)
    onehot = (chosen[:, :, None] == jnp.arange(REDUCED, dtype=jnp.int32)).astype(bf16)
    inputs = jnp.pad(small[:, :, :REDUCED].astype(bf16), ((0, 0), (0, 14), (0, 0)))
    rows = jnp.concatenate([onehot, inputs], axis=1)

    own_order = lax.dynamic_slice_in_dim(order, zh * 2, 2)
    target_rows = jnp.take(targets, own_order, axis=0).astype(f32)
    target_jac = jnp.take(jacobian_targets, own_order, axis=0).reshape(2 * TANGENTS, REDUCED)
    wanted = jnp.concatenate(
        [target_jac.astype(f32), jnp.pad(target_rows, ((0, 14), (0, 0)))], axis=0
    )

    sent = forward(place, rows[4:], weight, other, bf16)
    from_core = core_swap(sent)
    kept = forward(place, rows[:4], weight, other, f32)
    partial = kept + from_core.astype(f32)
    sending = partial[1:].astype(bf16)
    got = [z_shift(sending[d - 1], d) for d in (1, 3, 2)]
    total = partial[0]
    for g in got:
        total = total + g.astype(f32)
    scale = jnp.where(jnp.arange(CHUNK)[:, None] < 2 * TANGENTS, jacobian_weight, 1.0)
    misfit = (scale * (total - wanted)).astype(bf16)
    near = [misfit] + [z_shift(misfit, 4 - d) for d in (1, 2, 3)]
    far = [core_swap(m) for m in near]
    grad_last, grad_first = backward(
        place, rows.reshape(8 * CHUNK, REDUCED), near + far, weight, other
    )

    last = ring_sum(grad_last.reshape(4, 128, COLS), at_x, "x").astype(bf16)
    by_y = grad_first.reshape(4, 4, 32, COLS).transpose(1, 0, 2, 3)
    first = ring_sum(by_y, at_y, "y").astype(bf16)
    last = ring_sum(last.reshape(4, 32, COLS), at_y, "y")
    first = ring_sum(first, at_x, "x")

    both = jnp.stack([first.reshape(2, 2, 8, COLS), last.reshape(2, 2, 8, COLS)], axis=2)
    result = lax.all_to_all(
        both.reshape(8, 8, COLS), ("zl", "core", "zh"), split_axis=0, concat_axis=0, tiled=True
    )
    return result.transpose(1, 0, 2).reshape(1, 8, 8 * COLS)


def z_shift_partner(block):
    return lax.ppermute(block, Z, [(t, 3 - t) for t in range(4)])


def solution(mesh):
    torus = Mesh(mesh.devices.reshape(4, 4, 2, 2, 2), AXES)
    return jax.shard_map(
        shards,
        mesh=torus,
        in_specs=(
            P(DP, None),
            P(DP, None),
            P(DP, None, None),
            P(DP, None),
            P(DP, None),
            P("zh", None, None),
        ),
        out_specs=P("zh", DP, None),
        check_vma=False,
    )
```

time: 575 us -> 146 us (0.25)
  waiting for transfers between devices: 344 us -> 42.4 us
  matrix products: 112 us -> 0 us
  local copies, waits for them, and re-layouts: 50.5 us -> 11.2 us
  Pallas kernels: 0 us -> 29.2 us
  starting transfers between devices: 18.4 us -> 35 us
  between operations: 13.4 us -> 0.27 us
  blocking collectives: 8.96 us -> 18.1 us
  loops' own time: 8.37 us -> 0 us
  other arithmetic: 16.2 us -> 9.41 us
    reduce_scatter x2 -> x0, waiting for transfers between devices: 223 us -> none  [the longest x1 191 us: scatter_pairs(): return lax.psum_scatter(tiles, chips, scatter_dimension=0, tiled=True)[0]]
    dot_general x28 -> x0, matrix products: 112 us -> none  [the longest x8 60.7 us: contract_rows(): lax.dot_general(left, right, (((0,), (0,)), ((), ())), preferred_element_...]
    ppermute x1 -> x24, waiting for transfers between devices: 90.6 us -> 42.4 us  [the longest x6 20.1 us: z_shift(): lax.ppermute(block, Z, [(z_index(z), z_index((z + d) % 4)) for z in range...]
    ppermute x1 -> x24, starting transfers between devices: 4.41 us -> 35 us  [the longest x12 16.9 us: ring_shift(): return lax.ppermute(block, axis, [(i, (i + d) % 4) for i in range(4)])]
    all_to_all x4 -> x0, waiting for transfers between devices: 29.7 us -> none  [sent_to_all(): return lax.all_to_all(copies, axis, split_axis=0, concat_axis=0, tiled=True)]
    pallas_call x0 -> x3, Pallas kernels: none -> 29.2 us  [the longest x1 15.6 us: backward(): pl.pallas_call(backward_kernel, grid_spec=pltpu.PrefetchScalarGridSpec(nu...]
    gather x4, local copies, waits for them, and re-layouts: 19.7 us -> 3.64 us  [the longest x1 1.27 us: shards(): inputs = jnp.take(samples, order, axis=0).astype(f32)]
    all_to_all x4 -> x0, starting transfers between devices: 14 us -> none  [sent_to_all(): return lax.all_to_all(copies, axis, split_axis=0, concat_axis=0, tiled=True)]
  transfers between devices with their start and end apart: 7 -> 24, of which waited for: 7 -> 14; matrix products, arithmetic and copies ran while one was open for 0% -> 8% of each run, Pallas kernels for 0% -> 5%
where the time goes in v1:
time: 146 us
  waiting for transfers between devices  42.4 us (29%)
  starting transfers between devices  35 us (24%)
  Pallas kernels  29.2 us (20%)
  blocking collectives  18.1 us (12%)
  local copies, waits for them, and re-layouts  11.2 us (8%)
  other arithmetic  9.41 us (6%)
    ppermute x6, waiting for transfers between devices, z_shift(): lax.ppermute(block, Z, [(z_index(z), z_index((z + d) % 4)) for z in range...  20.1 us
    ppermute x12, starting transfers between devices, ring_shift(): return lax.ppermute(block, axis, [(i, (i + d) % 4) for i in range(4)])  16.9 us
    pallas_call x1, Pallas kernels, backward(): pl.pallas_call(backward_kernel, grid_spec=pltpu.PrefetchScalarGridSpec(nu...  15.6 us
    pallas_call x2, Pallas kernels, forward(): pl.pallas_call(forward_kernel, grid_spec=pltpu.PrefetchScalarGridSpec(num...  13.6 us
    all_to_all x1, blocking collectives, shards(): lax.all_to_all(both.reshape(8, 8, COLS), ('zl', 'core', 'zh'), split_axis...  12.1 us
    ppermute x12, waiting for transfers between devices, ring_shift(): return lax.ppermute(block, axis, [(i, (i + d) % 4) for i in range(4)])  11 us
    ppermute x1, waiting for transfers between devices, z_shift_partner(): return lax.ppermute(block, Z, [(t, 3 - t) for t in range(4)])  9.8 us
    ppermute x6, starting transfers between devices, z_shift(): lax.ppermute(block, Z, [(z_index(z), z_index((z + d) % 4)) for z in range...  6.9 us
  transfers between devices with their start and end apart: 24, of which 14 were waited for; matrix products, arithmetic and copies ran while one was open for 8% of the time, Pallas kernels for 5%

profile of v1, /device:TPU:1, one launch (start us, length us, event | category | flops | bytes accessed | tf_op | source)
XLA Modules:
  0.0 145.6 jit_solution(16501909685937072058)
XLA Ops:
  0.0 1.4 dynamic-slice_bitcast_fusion
  1.4 4.7 %collective-permute-start = (bf16[512,1024]{1,0:T(8,128)(2,1)S(1)}, bf16[512,1024]{1,0:T(8,128)(2,1)}, u32[]{:S(2)}, u32[]{:S(2)}) collective-permute-start(bf16[512,1024]{1,0:T(8,128)(2,1)S(1)} %dynamic-slice_bitcast_fusion), channel_id=1, source_target_pairs={{0,5},{1,4},{4,1},{5,0},{2,7},{3,6},{6,3},{7,2},{8,13},{9,12},{12,... | collective-permute-start | bytes 3145736 | tf_op jit(solution)/shard_map/ppermute | solution.py:241
  6.0 0.7 fusion.24
  6.7 0.7 compare_and_fusion.1
  7.4 1.3 gather_fusion
  8.6 1.2 gather_fusion.1
  10.0 6.0 %all-gather.1 = f32[4,4,640]{2,1,0:T(4,128)S(1)} all-gather(f32[1,4,640]{2,1,0:T(4,128)S(1)} %maximum_bitcast_fusion), channel_id=2, replica_groups=mesh['x'=4,'y'=4,'zl'=2,'core'=2,'zh'=2] {'zl','core'}, dimensions={0}, use_global_device_ids=true | all-gather | bytes 51200 | tf_op jit(solution)/shard_map/all_gather | solution.py:192
  16.2 0.6 pad_add_fusion.place
  17.6 1.6 %fusion.27 = (bf16[4,272,512]{2,1,0:T(8,128)(2,1)}, bf16[4,272,512]{2,1,0:T(8,128)(2,1)}) fusion(bf16[8,272,512]{2,1,0:T(8,128)(2,1)S(1)} %fusion.2), kind=kLoop, calls=%fused_computation.80 | loop fusion | bytes 4456448 | tf_op jit(solution)/shard_map/slice | solution.py:210
  19.2 9.8 %collective-permute-done.other.refs_9_ = bf16[512,1024]{1,0:T(8,128)(2,1)} collective-permute-done((bf16[512,1024]{1,0:T(8,128)(2,1)S(1)}, bf16[512,1024]{1,0:T(8,128)(2,1)}, u32[]{:S(2)}, u32[]{:S(2)}) %collective-permute-start) | collective-permute-done | bytes 1048608 | tf_op jit(solution)/shard_map/ppermute | solution.py:241
  29.0 6.8 %shard_map.65 = bf16[4,272,512]{2,1,0:T(8,128)(2,1)} custom-call(s32[2]{0:T(128)} %pad_add_fusion.place, bf16[4,272,512]{2,1,0:T(8,128)(2,1)} %get-tuple-element.11.rows, bf16[512,8192]{1,0:T(8,128)(2,1)} %bitcast.98, bf16[512,1024]{1,0:T(8,128)(2,1)} %collective-permute-done.other.refs_9_), custom_call_target="tpu_custom_call" | custom-call | flops 2281701376 | bytes 2097152 | tf_op jit(solution)/shard_map/pallas_call | solution.py:70
  35.8 1.3 collective-permute-start.1
  37.8 0.7 broadcast_select_fusion
  38.5 6.8 %shard_map.64 = f32[4,272,512]{2,1,0:T(8,128)} custom-call(s32[2]{0:T(128)} %pad_add_fusion.place, bf16[4,272,512]{2,1,0:T(8,128)(2,1)} %get-tuple-element.12.rows, bf16[512,8192]{1,0:T(8,128)(2,1)} %bitcast.99, bf16[512,1024]{1,0:T(8,128)(2,1)} %collective-permute-done.other.refs_9_), custom_call_target="tpu_custom_call" | custom-call | flops 2281701376 | bytes 2097152 | tf_op jit(solution)/shard_map/pallas_call | solution.py:70
  45.3 2.3 %fusion.26 = (bf16[4,272,512]{2,1,0:T(8,128)(2,1)S(1)}, f32[4,272,512]{2,1,0:T(8,128)S(1)}) fusion(f32[4,272,512]{2,1,0:T(8,128)} %shard_map.64, bf16[4,272,512]{2,1,0:T(8,128)(2,1)} %collective-permute-done.1), kind=kLoop, calls=%fused_computation.79 | loop fusion | flops 1671168 | bytes 6684672 | tf_op jit(solution)/shard_map/convert.7
  47.7 0.9 slice_bitcast_fusion.3
  48.6 2.7 %collective-permute-start.3 = (bf16[272,512]{1,0:T(8,128)(2,1)}, bf16[272,512]{1,0:T(8,128)(2,1)}, u32[]{:S(2)}, u32[]{:S(2)}) collective-permute-start(bf16[272,512]{1,0:T(8,128)(2,1)} %get-tuple-element.15), channel_id=1, source_target_pairs={{0,5},{4,0},{1,4},{5,1},{2,7},{6,2},{3,6},{7,3},{8,13},{12,8},{9,1... | collective-permute-start | bytes 835592 | tf_op jit(solution)/shard_map/ppermute | solution.py:28
  51.3 1.2 collective-permute-start.4
  53.7 4.6 %collective-permute-done.2 = bf16[272,512]{1,0:T(8,128)(2,1)} collective-permute-done((bf16[272,512]{1,0:T(8,128)(2,1)}, bf16[272,512]{1,0:T(8,128)(2,1)}, u32[]{:S(2)}, u32[]{:S(2)}) %collective-permute-start.2) | collective-permute-done | bytes 278560 | tf_op jit(solution)/shard_map/ppermute | solution.py:28
  58.3 4.8 %collective-permute-done.3 = bf16[272,512]{1,0:T(8,128)(2,1)} collective-permute-done((bf16[272,512]{1,0:T(8,128)(2,1)}, bf16[272,512]{1,0:T(8,128)(2,1)}, u32[]{:S(2)}, u32[]{:S(2)}) %collective-permute-start.3) | collective-permute-done | bytes 278560 | tf_op jit(solution)/shard_map/ppermute | solution.py:28
  63.1 2.3 %collective-permute-done.4 = bf16[272,512]{1,0:T(8,128)(2,1)} collective-permute-done((bf16[272,512]{1,0:T(8,128)(2,1)}, bf16[272,512]{1,0:T(8,128)(2,1)}, u32[]{:S(2)}, u32[]{:S(2)}) %collective-permute-start.4) | collective-permute-done | bytes 278560 | tf_op jit(solution)/shard_map/ppermute | solution.py:28
  65.5 1.3 fusion.8.refs_0_
  66.9 1.8 %collective-permute-start.7 = (bf16[272,512]{1,0:T(8,128)(2,1)S(1)}, bf16[272,512]{1,0:T(8,128)(2,1)S(1)}, u32[]{:S(2)}, u32[]{:S(2)}) collective-permute-start(bf16[272,512]{1,0:T(8,128)(2,1)S(1)} %fusion.8.refs_0_), channel_id=1, source_target_pairs={{0,4},{4,1},{1,5},{5,0},{2,6},{6,3},{3,7},{7,2},{8,12},{12,9},{9,1... | collective-permute-start | bytes 835592 | tf_op jit(solution)/shard_map/ppermute | solution.py:28
  68.7 1.2 collective-permute-start.5
  69.9 1.7 %collective-permute-start.8 = (bf16[272,512]{1,0:T(8,128)(2,1)S(1)}, bf16[272,512]{1,0:T(8,128)(2,1)S(1)}, u32[]{:S(2)}, u32[]{:S(2)}) collective-permute-start(bf16[272,512]{1,0:T(8,128)(2,1)S(1)} %fusion.8.refs_0_), channel_id=1, source_target_pairs={{0,2},{2,0},{1,3},{3,1},{4,6},{6,4},{5,7},{7,5},{8,10},{10,8},{9,1... | collective-permute-start | bytes 835592 | tf_op jit(solution)/shard_map/ppermute | solution.py:36
  71.6 4.2 %collective-permute-done.6.refs_2_ = bf16[272,512]{1,0:T(8,128)(2,1)S(1)} collective-permute-done((bf16[272,512]{1,0:T(8,128)(2,1)S(1)}, bf16[272,512]{1,0:T(8,128)(2,1)S(1)}, u32[]{:S(2)}, u32[]{:S(2)}) %collective-permute-start.6) | collective-permute-done | bytes 278560 | tf_op jit(solution)/shard_map/ppermute | solution.py:28
  75.8 3.0 %collective-permute-start.10 = (bf16[272,512]{1,0:T(8,128)(2,1)S(1)}, bf16[272,512]{1,0:T(8,128)(2,1)S(1)}, u32[]{:S(2)}, u32[]{:S(2)}) collective-permute-start(bf16[272,512]{1,0:T(8,128)(2,1)S(1)} %collective-permute-done.6.refs_2_), channel_id=1, source_target_pairs={{0,2},{2,0},{1,3},{3,1},{4,6},{6,4},{5,7},{7,5},{8,10},{10,8},{9,1... | collective-permute-start | bytes 835592 | tf_op jit(solution)/shard_map/ppermute | solution.py:36
  78.8 4.1 %collective-permute-done.7.refs_3_ = bf16[272,512]{1,0:T(8,128)(2,1)S(1)} collective-permute-done((bf16[272,512]{1,0:T(8,128)(2,1)S(1)}, bf16[272,512]{1,0:T(8,128)(2,1)S(1)}, u32[]{:S(2)}, u32[]{:S(2)}) %collective-permute-start.7) | collective-permute-done | bytes 278560 | tf_op jit(solution)/shard_map/ppermute | solution.py:28
  83.5 1.1 collective-permute-done.11.refs_7_
  85.7 15.6 %shard_map.66 = (bf16[512,1024]{1,0:T(8,128)(2,1)}, bf16[512,1024]{1,0:T(8,128)(2,1)}) custom-call(s32[2]{0:T(128)} %pad_add_fusion.place, bf16[2176,512]{1,0:T(8,128)(2,1)} %bitcast.101, bf16[272,512]{1,0:T(8,128)(2,1)} %copy-done.3, bf16[272,512]{1,0:T(8,128)(2,1)} %copy-done.7, bf16[272,512]{1,0:T(8,128)(2,1)} %copy-done.5, bf16[272,512]{1,0:T(8,128)(2,1)} %copy-done.6, ...), custom_call_target="tpu_custom_call" | custom-call | flops 9126805504 | bytes 2097152 | tf_op jit(solution)/shard_map/pallas_call | solution.py:136
  101.3 2.0 %dynamic-slice_bitcast_fusion.6 = (bf16[4,32,1024]{2,1,0:T(8,128)(2,1)}, bf16[4,32,1024]{2,1,0:T(8,128)(2,1)S(1)}, bf16[4,32,1024]{2,1,0:T(8,128)(2,1)S(1)}) fusion(bf16[4,4,32,1024]{3,2,1,0:T(8,128)(2,1)} %bitcast.104, s32[]{:T(128)S(6)} %select_n.182, s32[]{:T(128)S(6)} %select_n.186, s32[]{:T(128)S(6)} %select_n.184), kind=kLoop, calls=%fused_computation.39 | loop fusion | bytes 1572876 | tf_op jit(solution)/shard_map/jit(dynamic_index_in_dim)/squeeze | solution.py:168
  103.3 1.3 collective-permute-start.12
  104.6 1.4 collective-permute-start.13
  106.0 1.6 %collective-permute-start.14 = (bf16[4,32,1024]{2,1,0:T(8,128)(2,1)S(1)}, bf16[4,32,1024]{2,1,0:T(8,128)(2,1)S(1)}, u32[]{:S(2)}, u32[]{:S(2)}) collective-permute-start(bf16[4,32,1024]{2,1,0:T(8,128)(2,1)S(1)} %get-tuple-element.17), channel_id=1, source_target_pairs={{0,16},{8,24},{16,0},{24,8},{1,17},{9,25},{17,1},{25,9},{2,18},{10... | collective-permute-start | bytes 786440 | tf_op jit(solution)/shard_map/ppermute | solution.py:32
  107.7 1.3 collective-permute-start.18
  109.0 1.5 %collective-permute-start.19 = (bf16[128,1024]{1,0:T(8,128)(2,1)S(1)}, bf16[128,1024]{1,0:T(8,128)(2,1)S(1)}, u32[]{:S(2)}, u32[]{:S(2)}) collective-permute-start(bf16[128,1024]{1,0:T(8,128)(2,1)S(1)} %get-tuple-element.21), channel_id=1, source_target_pairs={{0,96},{32,0},{64,32},{96,64},{1,97},{33,1},{65,33},{97,65},{2,98}... | collective-permute-start | bytes 786440 | tf_op jit(solution)/shard_map/ppermute | solution.py:32
  110.5 1.8 %collective-permute-done.12 = bf16[4,32,1024]{2,1,0:T(8,128)(2,1)S(1)} collective-permute-done((bf16[4,32,1024]{2,1,0:T(8,128)(2,1)}, bf16[4,32,1024]{2,1,0:T(8,128)(2,1)S(1)}, u32[]{:S(2)}, u32[]{:S(2)}) %collective-permute-start.12) | collective-permute-done | bytes 262176 | tf_op jit(solution)/shard_map/ppermute | solution.py:32
  112.3 2.8 %collective-permute-start.20 = (bf16[128,1024]{1,0:T(8,128)(2,1)S(1)}, bf16[128,1024]{1,0:T(8,128)(2,1)S(1)}, u32[]{:S(2)}, u32[]{:S(2)}) collective-permute-start(bf16[128,1024]{1,0:T(8,128)(2,1)S(1)} %get-tuple-element.20), channel_id=1, source_target_pairs={{0,64},{32,96},{64,0},{96,32},{1,65},{33,97},{65,1},{97,33},{2,66}... | collective-permute-start | bytes 786440 | tf_op jit(solution)/shard_map/ppermute | solution.py:32
  115.1 4.0 %collective-permute-done.14 = bf16[4,32,1024]{2,1,0:T(8,128)(2,1)S(1)} collective-permute-done((bf16[4,32,1024]{2,1,0:T(8,128)(2,1)S(1)}, bf16[4,32,1024]{2,1,0:T(8,128)(2,1)S(1)}, u32[]{:S(2)}, u32[]{:S(2)}) %collective-permute-start.14) | collective-permute-done | bytes 262176 | tf_op jit(solution)/shard_map/ppermute | solution.py:32
  119.1 1.1 fusion.15
  120.2 1.3 collective-permute-start.15
  121.5 1.5 %collective-permute-start.16 = (bf16[32,1024]{1,0:T(8,128)(2,1)S(1)}, bf16[32,1024]{1,0:T(8,128)(2,1)S(1)}, u32[]{:S(2)}, u32[]{:S(2)}) collective-permute-start(bf16[32,1024]{1,0:T(8,128)(2,1)S(1)} %get-tuple-element.24), channel_id=1, source_target_pairs={{0,96},{32,0},{64,32},{96,64},{1,97},{33,1},{65,33},{97,65},{2,98}... | collective-permute-start | bytes 196616 | tf_op jit(solution)/shard_map/ppermute | solution.py:32
  123.0 1.5 %collective-permute-start.17 = (bf16[32,1024]{1,0:T(8,128)(2,1)S(1)}, bf16[32,1024]{1,0:T(8,128)(2,1)S(1)}, u32[]{:S(2)}, u32[]{:S(2)}) collective-permute-start(bf16[32,1024]{1,0:T(8,128)(2,1)S(1)} %get-tuple-element.23), channel_id=1, source_target_pairs={{0,64},{32,96},{64,0},{96,32},{1,65},{33,97},{65,1},{97,33},{2,66}... | collective-permute-start | bytes 196616 | tf_op jit(solution)/shard_map/ppermute | solution.py:32
  125.2 2.3 %collective-permute-start.22 = (bf16[32,1024]{1,0:T(8,128)(2,1)S(1)}, bf16[32,1024]{1,0:T(8,128)(2,1)S(1)}, u32[]{:S(2)}, u32[]{:S(2)}) collective-permute-start(bf16[32,1024]{1,0:T(8,128)(2,1)S(1)} %get-tuple-element.27), channel_id=1, source_target_pairs={{0,24},{8,0},{16,8},{24,16},{1,25},{9,1},{17,9},{25,17},{2,26},{10... | collective-permute-start | bytes 196616 | tf_op jit(solution)/shard_map/ppermute | solution.py:32
  128.0 1.1 collective-permute-done.21
  129.4 3.3 %collective-permute-done.23 = bf16[32,1024]{1,0:T(8,128)(2,1)S(1)} collective-permute-done((bf16[32,1024]{1,0:T(8,128)(2,1)S(1)}, bf16[32,1024]{1,0:T(8,128)(2,1)S(1)}, u32[]{:S(2)}, u32[]{:S(2)}) %collective-permute-start.23) | collective-permute-done | bytes 65568 | tf_op jit(solution)/shard_map/ppermute | solution.py:32
  132.8 12.1 %all_to_all.5 = f32[8,8,1024]{2,1,0:T(8,128)S(1)} all-to-all(f32[8,8,1024]{2,1,0:T(8,128)S(1)} %bitcast.108), channel_id=1, replica_groups=mesh['x'=4,'y'=4,'zl'=2,'core'=2,'zh'=2] {'zl','core','zh'}, dimensions={0} | all-to-all | bytes 524288 | tf_op jit(solution)/shard_map/all_to_all | solution.py:234
  144.9 0.7 copy.15
  (74 shorter events, 6.4 us)
Async XLA Ops:
  0.0 53.0 %copy-start = (bf16[8,128,512]{2,1,0:T(8,128)(2,1)S(1)}, bf16[8,128,512]{2,1,0:T(8,128)(2,1)}, u32[]{:S(2)}) copy-start(bf16[8,128,512]{2,1,0:T(8,128)(2,1)} %param.8) | copy-start | bytes 3145732
  1.4 27.6 %collective-permute-start = (bf16[512,1024]{1,0:T(8,128)(2,1)S(1)}, bf16[512,1024]{1,0:T(8,128)(2,1)}, u32[]{:S(2)}, u32[]{:S(2)}) collective-permute-start(bf16[512,1024]{1,0:T(8,128)(2,1)S(1)} %dynamic-slice_bitcast_fusion), channel_id=1, source_target_pairs={{0,5},{1,4},{4,1},{5,0},{2,7},{3,6},{6,3},{7,2},{8,13},{9,12},{12,... | collective-permute-start | bytes 3145736 | tf_op jit(solution)/shard_map/ppermute | solution.py:241
  17.6 11.4 %copy-start.1 = (bf16[8,272,512]{2,1,0:T(8,128)(2,1)}, bf16[8,272,512]{2,1,0:T(8,128)(2,1)S(1)}, u32[]{:S(2)}) copy-start(bf16[8,272,512]{2,1,0:T(8,128)(2,1)S(1)} %fusion.2) | copy-start | bytes 6684676
  29.0 8.0 %copy-start.12 = (s32[1,8]{1,0:T(1,128)S(1)}, s32[1,8]{1,0:T(1,128)}, u32[]{:S(2)}) copy-start(s32[1,8]{1,0:T(1,128)} %param.10) | copy-start | bytes 100
  29.0 8.1 %copy-start.4 = (bf16[8,512]{1,0:T(8,128)(2,1)S(1)}, bf16[8,512]{1,0:T(8,128)(2,1)}, u32[]{:S(2)}) copy-start(bf16[8,512]{1,0:T(8,128)(2,1)} %param.7) | copy-start | bytes 24580
  35.8 9.5 %collective-permute-start.1 = (bf16[4,272,512]{2,1,0:T(8,128)(2,1)}, bf16[4,272,512]{2,1,0:T(8,128)(2,1)}, u32[]{:S(2)}, u32[]{:S(2)}) collective-permute-start(bf16[4,272,512]{2,1,0:T(8,128)(2,1)} %shard_map.65), channel_id=1, source_target_pairs={{0,2},{2,0},{1,3},{3,1},{4,6},{6,4},{5,7},{7,5},{8,10},{10,8},{9,1... | collective-permute-start | bytes 3342344 | tf_op jit(solution)/shard_map/ppermute | solution.py:36
  48.6 9.7 %collective-permute-start.2 = (bf16[272,512]{1,0:T(8,128)(2,1)}, bf16[272,512]{1,0:T(8,128)(2,1)}, u32[]{:S(2)}, u32[]{:S(2)}) collective-permute-start(bf16[272,512]{1,0:T(8,128)(2,1)} %get-tuple-element.13), channel_id=1, source_target_pairs={{0,4},{4,1},{1,5},{5,0},{2,6},{6,3},{3,7},{7,2},{8,12},{12,9},{9,1... | collective-permute-start | bytes 835592 | tf_op jit(solution)/shard_map/ppermute | solution.py:28
  48.6 14.5 %collective-permute-start.3 = (bf16[272,512]{1,0:T(8,128)(2,1)}, bf16[272,512]{1,0:T(8,128)(2,1)}, u32[]{:S(2)}, u32[]{:S(2)}) collective-permute-start(bf16[272,512]{1,0:T(8,128)(2,1)} %get-tuple-element.15), channel_id=1, source_target_pairs={{0,5},{4,0},{1,4},{5,1},{2,7},{6,2},{3,6},{7,3},{8,13},{12,8},{9,1... | collective-permute-start | bytes 835592 | tf_op jit(solution)/shard_map/ppermute | solution.py:28
  51.3 14.2 %collective-permute-start.4 = (bf16[272,512]{1,0:T(8,128)(2,1)}, bf16[272,512]{1,0:T(8,128)(2,1)}, u32[]{:S(2)}, u32[]{:S(2)}) collective-permute-start(bf16[272,512]{1,0:T(8,128)(2,1)} %get-tuple-element.14), channel_id=1, source_target_pairs={{0,1},{4,5},{1,0},{5,4},{2,3},{6,7},{3,2},{7,6},{8,9},{12,13},{9,8... | collective-permute-start | bytes 835592 | tf_op jit(solution)/shard_map/ppermute | solution.py:28
  66.8 18.2 %copy-start.3 = (bf16[272,512]{1,0:T(8,128)(2,1)}, bf16[272,512]{1,0:T(8,128)(2,1)S(1)}, u32[]{:S(2)}) copy-start(bf16[272,512]{1,0:T(8,128)(2,1)S(1)} %fusion.8.refs_0_) | copy-start | bytes 835588
  66.8 9.0 %collective-permute-start.6 = (bf16[272,512]{1,0:T(8,128)(2,1)S(1)}, bf16[272,512]{1,0:T(8,128)(2,1)S(1)}, u32[]{:S(2)}, u32[]{:S(2)}) collective-permute-start(bf16[272,512]{1,0:T(8,128)(2,1)S(1)} %fusion.8.refs_0_), channel_id=1, source_target_pairs={{0,1},{4,5},{1,0},{5,4},{2,3},{6,7},{3,2},{7,6},{8,9},{12,13},{9,8... | collective-permute-start | bytes 835592 | tf_op jit(solution)/shard_map/ppermute | solution.py:28
  66.9 16.0 %collective-permute-start.7 = (bf16[272,512]{1,0:T(8,128)(2,1)S(1)}, bf16[272,512]{1,0:T(8,128)(2,1)S(1)}, u32[]{:S(2)}, u32[]{:S(2)}) collective-permute-start(bf16[272,512]{1,0:T(8,128)(2,1)S(1)} %fusion.8.refs_0_), channel_id=1, source_target_pairs={{0,4},{4,1},{1,5},{5,0},{2,6},{6,3},{3,7},{7,2},{8,12},{12,9},{9,1... | collective-permute-start | bytes 835592 | tf_op jit(solution)/shard_map/ppermute | solution.py:28
  68.7 14.7 %collective-permute-start.5 = (bf16[272,512]{1,0:T(8,128)(2,1)S(1)}, bf16[272,512]{1,0:T(8,128)(2,1)S(1)}, u32[]{:S(2)}, u32[]{:S(2)}) collective-permute-start(bf16[272,512]{1,0:T(8,128)(2,1)S(1)} %fusion.8.refs_0_), channel_id=1, source_target_pairs={{0,5},{4,0},{1,4},{5,1},{2,7},{6,2},{3,6},{7,3},{8,13},{12,8},{9,1... | collective-permute-start | bytes 835592 | tf_op jit(solution)/shard_map/ppermute | solution.py:28
  69.9 13.7 %collective-permute-start.8 = (bf16[272,512]{1,0:T(8,128)(2,1)S(1)}, bf16[272,512]{1,0:T(8,128)(2,1)S(1)}, u32[]{:S(2)}, u32[]{:S(2)}) collective-permute-start(bf16[272,512]{1,0:T(8,128)(2,1)S(1)} %fusion.8.refs_0_), channel_id=1, source_target_pairs={{0,2},{2,0},{1,3},{3,1},{4,6},{6,4},{5,7},{7,5},{8,10},{10,8},{9,1... | collective-permute-start | bytes 835592 | tf_op jit(solution)/shard_map/ppermute | solution.py:36
  75.8 9.2 %copy-start.5 = (bf16[272,512]{1,0:T(8,128)(2,1)}, bf16[272,512]{1,0:T(8,128)(2,1)S(1)}, u32[]{:S(2)}) copy-start(bf16[272,512]{1,0:T(8,128)(2,1)S(1)} %collective-permute-done.6.refs_2_) | copy-start | bytes 835588
  75.8 7.8 %collective-permute-start.10 = (bf16[272,512]{1,0:T(8,128)(2,1)S(1)}, bf16[272,512]{1,0:T(8,128)(2,1)S(1)}, u32[]{:S(2)}, u32[]{:S(2)}) collective-permute-start(bf16[272,512]{1,0:T(8,128)(2,1)S(1)} %collective-permute-done.6.refs_2_), channel_id=1, source_target_pairs={{0,2},{2,0},{1,3},{3,1},{4,6},{6,4},{5,7},{7,5},{8,10},{10,8},{9,1... | collective-permute-start | bytes 835592 | tf_op jit(solution)/shard_map/ppermute | solution.py:36
  82.9 2.1 %copy-start.6 = (bf16[272,512]{1,0:T(8,128)(2,1)}, bf16[272,512]{1,0:T(8,128)(2,1)S(1)}, u32[]{:S(2)}) copy-start(bf16[272,512]{1,0:T(8,128)(2,1)S(1)} %collective-permute-done.7.refs_3_) | copy-start | bytes 835588
  82.9 1.7 %collective-permute-start.11 = (bf16[272,512]{1,0:T(8,128)(2,1)S(1)}, bf16[272,512]{1,0:T(8,128)(2,1)S(1)}, u32[]{:S(2)}, u32[]{:S(2)}) collective-permute-start(bf16[272,512]{1,0:T(8,128)(2,1)S(1)} %collective-permute-done.7.refs_3_), channel_id=1, source_target_pairs={{0,2},{2,0},{1,3},{3,1},{4,6},{6,4},{5,7},{7,5},{8,10},{10,8},{9,1... | collective-permute-start | bytes 835592 | tf_op jit(solution)/shard_map/ppermute | solution.py:36
  83.4 1.6 %copy-start.7 = (bf16[272,512]{1,0:T(8,128)(2,1)}, bf16[272,512]{1,0:T(8,128)(2,1)S(1)}, u32[]{:S(2)}) copy-start(bf16[272,512]{1,0:T(8,128)(2,1)S(1)} %collective-permute-done.5.refs_1_) | copy-start | bytes 835588
  83.4 1.6 %collective-permute-start.9 = (bf16[272,512]{1,0:T(8,128)(2,1)S(1)}, bf16[272,512]{1,0:T(8,128)(2,1)S(1)}, u32[]{:S(2)}, u32[]{:S(2)}) collective-permute-start(bf16[272,512]{1,0:T(8,128)(2,1)S(1)} %collective-permute-done.5.refs_1_), channel_id=1, source_target_pairs={{0,2},{2,0},{1,3},{3,1},{4,6},{6,4},{5,7},{7,5},{8,10},{10,8},{9,1... | collective-permute-start | bytes 835592 | tf_op jit(solution)/shard_map/ppermute | solution.py:36
  83.5 1.5 %copy-start.8 = (bf16[272,512]{1,0:T(8,128)(2,1)}, bf16[272,512]{1,0:T(8,128)(2,1)S(1)}, u32[]{:S(2)}) copy-start(bf16[272,512]{1,0:T(8,128)(2,1)S(1)} %collective-permute-done.8.refs_4_) | copy-start | bytes 835588
  83.5 1.5 %copy-start.9 = (bf16[272,512]{1,0:T(8,128)(2,1)}, bf16[272,512]{1,0:T(8,128)(2,1)S(1)}, u32[]{:S(2)}) copy-start(bf16[272,512]{1,0:T(8,128)(2,1)S(1)} %collective-permute-done.10.refs_6_) | copy-start | bytes 835588
  84.6 0.7 copy-start.10
  85.0 0.7 copy-start.11
  101.3 6.4 %copy-start.2 = (bf16[512,1024]{1,0:T(8,128)(2,1)S(1)}, bf16[512,1024]{1,0:T(8,128)(2,1)}, u32[]{:S(2)}) copy-start(bf16[512,1024]{1,0:T(8,128)(2,1)} %get-tuple-element.8) | copy-start | bytes 3145732
  103.3 9.0 %collective-permute-start.12 = (bf16[4,32,1024]{2,1,0:T(8,128)(2,1)}, bf16[4,32,1024]{2,1,0:T(8,128)(2,1)S(1)}, u32[]{:S(2)}, u32[]{:S(2)}) collective-permute-start(bf16[4,32,1024]{2,1,0:T(8,128)(2,1)} %get-tuple-element.16), channel_id=1, source_target_pairs={{0,8},{8,16},{16,24},{24,0},{1,9},{9,17},{17,25},{25,1},{2,10},{10... | collective-permute-start | bytes 786440 | tf_op jit(solution)/shard_map/ppermute | solution.py:32
  104.6 10.5 %collective-permute-start.13 = (bf16[4,32,1024]{2,1,0:T(8,128)(2,1)S(1)}, bf16[4,32,1024]{2,1,0:T(8,128)(2,1)S(1)}, u32[]{:S(2)}, u32[]{:S(2)}) collective-permute-start(bf16[4,32,1024]{2,1,0:T(8,128)(2,1)S(1)} %get-tuple-element.18), channel_id=1, source_target_pairs={{0,24},{8,0},{16,8},{24,16},{1,25},{9,1},{17,9},{25,17},{2,26},{10... | collective-permute-start | bytes 786440 | tf_op jit(solution)/shard_map/ppermute | solution.py:32
  106.0 13.0 %collective-permute-start.14 = (bf16[4,32,1024]{2,1,0:T(8,128)(2,1)S(1)}, bf16[4,32,1024]{2,1,0:T(8,128)(2,1)S(1)}, u32[]{:S(2)}, u32[]{:S(2)}) collective-permute-start(bf16[4,32,1024]{2,1,0:T(8,128)(2,1)S(1)} %get-tuple-element.17), channel_id=1, source_target_pairs={{0,16},{8,24},{16,0},{24,8},{1,17},{9,25},{17,1},{25,9},{2,18},{10... | collective-permute-start | bytes 786440 | tf_op jit(solution)/shard_map/ppermute | solution.py:32
  107.7 15.2 %collective-permute-start.18 = (bf16[128,1024]{1,0:T(8,128)(2,1)S(1)}, bf16[128,1024]{1,0:T(8,128)(2,1)S(1)}, u32[]{:S(2)}, u32[]{:S(2)}) collective-permute-start(bf16[128,1024]{1,0:T(8,128)(2,1)S(1)} %get-tuple-element.19), channel_id=1, source_target_pairs={{0,32},{32,64},{64,96},{96,0},{1,33},{33,65},{65,97},{97,1},{2,34}... | collective-permute-start | bytes 786440 | tf_op jit(solution)/shard_map/ppermute | solution.py:32
  109.0 15.5 %collective-permute-start.19 = (bf16[128,1024]{1,0:T(8,128)(2,1)S(1)}, bf16[128,1024]{1,0:T(8,128)(2,1)S(1)}, u32[]{:S(2)}, u32[]{:S(2)}) collective-permute-start(bf16[128,1024]{1,0:T(8,128)(2,1)S(1)} %get-tuple-element.21), channel_id=1, source_target_pairs={{0,96},{32,0},{64,32},{96,64},{1,97},{33,1},{65,33},{97,65},{2,98}... | collective-permute-start | bytes 786440 | tf_op jit(solution)/shard_map/ppermute | solution.py:32
  112.3 12.2 %collective-permute-start.20 = (bf16[128,1024]{1,0:T(8,128)(2,1)S(1)}, bf16[128,1024]{1,0:T(8,128)(2,1)S(1)}, u32[]{:S(2)}, u32[]{:S(2)}) collective-permute-start(bf16[128,1024]{1,0:T(8,128)(2,1)S(1)} %get-tuple-element.20), channel_id=1, source_target_pairs={{0,64},{32,96},{64,0},{96,32},{1,65},{33,97},{65,1},{97,33},{2,66}... | collective-permute-start | bytes 786440 | tf_op jit(solution)/shard_map/ppermute | solution.py:32
  120.2 7.2 %collective-permute-start.15 = (bf16[32,1024]{1,0:T(8,128)(2,1)S(1)}, bf16[32,1024]{1,0:T(8,128)(2,1)S(1)}, u32[]{:S(2)}, u32[]{:S(2)}) collective-permute-start(bf16[32,1024]{1,0:T(8,128)(2,1)S(1)} %get-tuple-element.22), channel_id=1, source_target_pairs={{0,32},{32,64},{64,96},{96,0},{1,33},{33,65},{65,97},{97,1},{2,34}... | collective-permute-start | bytes 196616 | tf_op jit(solution)/shard_map/ppermute | solution.py:32
  121.5 6.0 %collective-permute-start.16 = (bf16[32,1024]{1,0:T(8,128)(2,1)S(1)}, bf16[32,1024]{1,0:T(8,128)(2,1)S(1)}, u32[]{:S(2)}, u32[]{:S(2)}) collective-permute-start(bf16[32,1024]{1,0:T(8,128)(2,1)S(1)} %get-tuple-element.24), channel_id=1, source_target_pairs={{0,96},{32,0},{64,32},{96,64},{1,97},{33,1},{65,33},{97,65},{2,98}... | collective-permute-start | bytes 196616 | tf_op jit(solution)/shard_map/ppermute | solution.py:32
  123.0 5.0 %collective-permute-start.17 = (bf16[32,1024]{1,0:T(8,128)(2,1)S(1)}, bf16[32,1024]{1,0:T(8,128)(2,1)S(1)}, u32[]{:S(2)}, u32[]{:S(2)}) collective-permute-start(bf16[32,1024]{1,0:T(8,128)(2,1)S(1)} %get-tuple-element.23), channel_id=1, source_target_pairs={{0,64},{32,96},{64,0},{96,32},{1,65},{33,97},{65,1},{97,33},{2,66}... | collective-permute-start | bytes 196616 | tf_op jit(solution)/shard_map/ppermute | solution.py:32
  124.7 4.4 %collective-permute-start.21 = (bf16[32,1024]{1,0:T(8,128)(2,1)S(1)}, bf16[32,1024]{1,0:T(8,128)(2,1)S(1)}, u32[]{:S(2)}, u32[]{:S(2)}) collective-permute-start(bf16[32,1024]{1,0:T(8,128)(2,1)S(1)} %get-tuple-element.25), channel_id=1, source_target_pairs={{0,8},{8,16},{16,24},{24,0},{1,9},{9,17},{17,25},{25,1},{2,10},{10... | collective-permute-start | bytes 196616 | tf_op jit(solution)/shard_map/ppermute | solution.py:32
  125.2 4.2 %collective-permute-start.22 = (bf16[32,1024]{1,0:T(8,128)(2,1)S(1)}, bf16[32,1024]{1,0:T(8,128)(2,1)S(1)}, u32[]{:S(2)}, u32[]{:S(2)}) collective-permute-start(bf16[32,1024]{1,0:T(8,128)(2,1)S(1)} %get-tuple-element.27), channel_id=1, source_target_pairs={{0,24},{8,0},{16,8},{24,16},{1,25},{9,1},{17,9},{25,17},{2,26},{10... | collective-permute-start | bytes 196616 | tf_op jit(solution)/shard_map/ppermute | solution.py:32
  127.5 5.2 %collective-permute-start.23 = (bf16[32,1024]{1,0:T(8,128)(2,1)S(1)}, bf16[32,1024]{1,0:T(8,128)(2,1)S(1)}, u32[]{:S(2)}, u32[]{:S(2)}) collective-permute-start(bf16[32,1024]{1,0:T(8,128)(2,1)S(1)} %get-tuple-element.26), channel_id=1, source_target_pairs={{0,16},{8,24},{16,0},{24,8},{1,17},{9,25},{17,1},{25,9},{2,18},{10... | collective-permute-start | bytes 196616 | tf_op jit(solution)/shard_map/ppermute | solution.py:32

commit v2 on v1

v2 whole, which is shorter than its diff:
```python
import jax
import jax.numpy as jnp
from jax import lax
from jax.experimental import pallas as pl
from jax.experimental.pallas import tpu as pltpu
from jax.sharding import Mesh
from jax.sharding import PartitionSpec as P

AXES = ("x", "y", "zl", "core", "zh")
DP = ("x", "y", "zl", "core")
Z = ("zl", "zh")
MICRO = 4
REDUCED = 512
COLS = 1024
HALF = COLS // 2
TANGENTS = 128
CHUNK = 2 * TANGENTS + 16
GROUP = 4 * CHUNK
BLOCK = 256
jacobian_weight = 32.0
f32 = jnp.float32
bf16 = jnp.bfloat16


def z_index(z):
    return (z % 2) * 2 + z // 2


def z_shift(block, d):
    return lax.ppermute(block, Z, [(z_index(z), z_index((z + d) % 4)) for z in range(4)])


def z_facing(block):
    return lax.ppermute(block, Z, [(t, 3 - t) for t in range(4)])


def ring_shift(block, axis, d):
    return lax.ppermute(block, axis, [(i, (i + d) % 4) for i in range(4)])


def core_swap(block):
    return lax.ppermute(block, "core", [(0, 1), (1, 0)])


def slopes(linear):
    squash = jax.nn.sigmoid(linear)
    first = squash * (1.0 + linear * (1.0 - squash))
    second = squash * (1.0 - squash) * (2.0 + linear * (1.0 - 2.0 * squash))
    return linear * squash, first, second


def per_row(top, first):
    return [top[:TANGENTS] * first[0:1], top[TANGENTS : 2 * TANGENTS] * first[1:2]]


def whole_spec(shape):
    return pl.BlockSpec(shape, lambda i, place: (0,) * len(shape))


def forward_kernel(later, final, place, rows, own, *refs):
    refs = list(refs)
    count = 4 if later else 2
    other, refs = refs[:count], refs[count:]
    if later:
        carried, refs = refs[0], refs[1:]
        if final:
            arrived, refs = refs[0], refs[1:]
            refs = refs[3:]
        else:
            refs = refs[4:]
    w_first, w_last = refs[-2:]
    outs = refs[:-2]
    tangents, picked_out, linears = outs[:3]

    @pl.when(pl.program_id(0) == 0)
    def _():
        if later:
            top = jnp.concatenate([other[0][...], other[1][...]], axis=1)
            bottom = jnp.concatenate([other[2][...], other[3][...]], axis=1)
            theirs = jnp.concatenate([top, bottom], axis=0)
        else:
            theirs = jnp.concatenate([other[0][...], other[1][...]], axis=1)
        layer = place[4]
        w_first[...] = jnp.where(layer == 0, own[...], theirs)
        w_last[...] = jnp.where(layer == 0, theirs, own[...])
        if not final:
            outs[3][...] = w_last[...]

    picked = jnp.dot(rows[...], w_first[...], preferred_element_type=f32)
    parts = []
    for c in range(2):
        part = picked[c * CHUNK : (c + 1) * CHUNK]
        linear = part[2 * TANGENTS :]
        hidden, first, _ = slopes(linear)
        parts += per_row(part, first) + [hidden]
        linears[c * 16 : (c + 1) * 16, :] = linear
    tangent = jnp.concatenate(parts, axis=0).astype(bf16)
    tangents[...] = tangent
    picked_out[...] = picked.astype(bf16)
    total = lax.dot_general(
        tangent, w_last[...], (((1,), (1,)), ((), ())), preferred_element_type=f32
    )
    if later:
        total = total + carried[...]
    if not final:
        outs[4][...] = total.astype(outs[4].dtype)
        return
    total = total + arrived[...].astype(f32)
    chunks = outs[3:]

    @pl.when(pl.program_id(0) == 0)
    def _():
        chunks[0][...] = total[:CHUNK]
        chunks[1][...] = total[CHUNK:].astype(bf16)

    @pl.when(pl.program_id(0) == 1)
    def _():
        chunks[2][...] = total[:CHUNK].astype(bf16)
        chunks[3][...] = total[CHUNK:].astype(bf16)


def forward(place, rows, weight, other, carried=None, arrived=None, saved=None, final=False):
    later = carried is not None
    at = 1 if later else 0
    step = 2 * CHUNK
    row_spec = pl.BlockSpec((step, REDUCED), lambda i, place: (i, 0))
    half_spec = pl.BlockSpec((step, HALF), lambda i, place: (i, place[2 + at]))
    in_specs = [row_spec, pl.BlockSpec((REDUCED, HALF), lambda i, place: (0, place[at]))]
    in_specs += [whole_spec(o.shape) for o in other]
    args = [rows, weight, *other]
    out_specs = [half_spec, half_spec]
    out_specs.append(pl.BlockSpec((32, HALF), lambda i, place: (i, place[2 + at])))
    out_shape = [
        jax.ShapeDtypeStruct((GROUP, COLS), bf16),
        jax.ShapeDtypeStruct((GROUP, COLS), bf16),
        jax.ShapeDtypeStruct((64, COLS), f32),
    ]
    if not final:
        out_specs.append(pl.BlockSpec((REDUCED, HALF), lambda i, place: (0, place[2 + at])))
        out_shape.append(jax.ShapeDtypeStruct((REDUCED, COLS), bf16))
        out_specs.append(row_spec)
        out_shape.append(jax.ShapeDtypeStruct((GROUP, REDUCED), bf16 if later else f32))
    else:
        out_specs += [whole_spec((CHUNK, REDUCED))] * 4
        out_shape.append(jax.ShapeDtypeStruct((CHUNK, REDUCED), f32))
        out_shape += [jax.ShapeDtypeStruct((CHUNK, REDUCED), bf16)] * 3
    aliases = {}
    if later:
        in_specs.append(row_spec)
        args.append(carried)
        if final:
            in_specs.append(row_spec)
            args.append(arrived)
        for k, s in enumerate(saved):
            aliases[1 + len(args)] = k
            in_specs.append(pl.BlockSpec(memory_space=pl.ANY))
            args.append(s)
    return pl.pallas_call(
        lambda *refs: forward_kernel(later, final, *refs),
        grid_spec=pltpu.PrefetchScalarGridSpec(
            num_scalar_prefetch=1,
            grid=(2,),
            in_specs=in_specs,
            out_specs=out_specs,
            scratch_shapes=[pltpu.VMEM((REDUCED, HALF), bf16)] * 2,
        ),
        out_shape=out_shape,
        input_output_aliases=aliases,
        compiler_params=pltpu.CompilerParams(dimension_semantics=("arbitrary",)),
        cost_estimate=pl.CostEstimate(
            flops=4 * GROUP * REDUCED * HALF, bytes_accessed=4 * REDUCED * COLS, transcendentals=0
        ),
    )(place, *args)


def transpose_into(target, whole, at_x, at_y, x_major):
    for k in range(2 * GROUP // 128):
        turned = whole[k * 128 : (k + 1) * 128, :].T
        for g in range(16):
            f = lax.rem(g // 4 - at_x + 4, 4)
            e = lax.rem(g % 4 - at_y + 4, 4)
            row = f * 128 + e * 32 if x_major else e * 128 + f * 32
            span = pl.ds(pl.multiple_of(row, 32), 32)
            target[span, k * 128 : (k + 1) * 128] = turned[g * 32 : (g + 1) * 32]


def last_kernel(place, near, far, *refs):
    misfits, outs, misfit_t = refs[:8], refs[8:12], refs[12]

    @pl.when(pl.program_id(0) == 0)
    def _():
        whole = jnp.concatenate([m[...] for m in misfits], axis=0)
        transpose_into(misfit_t, whole, place[5], place[6], True)

    tangents = jnp.concatenate([near[...], far[...]], axis=0)
    total = jnp.dot(misfit_t[...], tangents, preferred_element_type=f32).astype(bf16)
    for d in range(4):
        outs[d][...] = total[d * 128 : (d + 1) * 128]


def first_kernel(place, rows_near, rows_far, near, far, lin_near, lin_far, w_last, *refs):
    misfits, outs, rows_t, cotangents = refs[:8], refs[8:12], refs[12], refs[13]

    @pl.when(pl.program_id(0) == 0)
    def _():
        whole = jnp.concatenate([rows_near[...], rows_far[...]], axis=0)
        transpose_into(rows_t, whole, place[5], place[6], False)

    for c in range(8):
        pair = jnp.dot(misfits[c][...], w_last[...], preferred_element_type=f32)
        back = pair.astype(bf16).astype(f32)
        picked = (near, far)[c // 4][pl.ds((c % 4) * CHUNK, 2 * TANGENTS), :].astype(f32)
        linear = (lin_near, lin_far)[c // 4][pl.ds((c % 4) * 16, 16), :]
        _, first, second = slopes(linear)
        joint = back[: 2 * TANGENTS] * picked
        projected = jnp.concatenate(
            [
                jnp.sum(joint[:TANGENTS], axis=0, keepdims=True),
                jnp.sum(joint[TANGENTS:], axis=0, keepdims=True),
                jnp.zeros((14, BLOCK), f32),
            ],
            axis=0,
        )
        before = back[2 * TANGENTS :] * first + second * projected
        cotangents[pl.ds(c * CHUNK, CHUNK), :] = jnp.concatenate(
            per_row(back, first) + [before], axis=0
        ).astype(bf16)
    total = jnp.dot(rows_t[...], cotangents[...], preferred_element_type=f32).astype(bf16)
    for d in range(4):
        outs[d][...] = total[d * 128 : (d + 1) * 128]


def backward(kernel, place, args, specs, scratch, matmuls):
    return pl.pallas_call(
        kernel,
        grid_spec=pltpu.PrefetchScalarGridSpec(
            num_scalar_prefetch=1,
            grid=(COLS // BLOCK,),
            in_specs=specs,
            out_specs=[pl.BlockSpec((128, BLOCK), lambda j, place: (0, j))] * 4,
            scratch_shapes=scratch,
        ),
        out_shape=[jax.ShapeDtypeStruct((128, COLS), bf16)] * 4,
        compiler_params=pltpu.CompilerParams(dimension_semantics=("arbitrary",)),
        cost_estimate=pl.CostEstimate(
            flops=4 * matmuls * GROUP * REDUCED * COLS,
            bytes_accessed=4 * GROUP * COLS,
            transcendentals=0,
        ),
    )(place, *args)


def ring_sum(chunks, axis):
    got = [ring_shift(chunks[d], axis, d) for d in (2, 1, 3)]
    total = chunks[0].astype(f32)
    for g in got:
        total = total + g.astype(f32)
    return total


def shards(samples, targets, jacobian_targets, directions, plan, weights):
    at_x, at_y = lax.axis_index("x"), lax.axis_index("y")
    zl, core, zh = lax.axis_index("zl"), lax.axis_index("core"), lax.axis_index("zh")
    z = zh * 2 + zl
    parity = at_x % 2
    weight = weights[0]
    mine = (zl * 2 + core) * 2 + zh
    theirs = ((1 - zl) * 2 + core) * 2 + (1 - zh)
    place = jnp.stack(
        [mine * 2 + parity, mine * 2 + 1 - parity, parity, 1 - parity, zh, at_x, at_y]
    ).astype(jnp.int32)

    direct, passed = [], []
    for k in range(2):
        start = theirs * COLS + parity * HALF + k * BLOCK
        direct.append(z_facing(lax.dynamic_slice_in_dim(weight, start, BLOCK, 1)))
    for part, d in ((slice(0, 256), 1), (slice(256, 512), 3)):
        for k in range(2):
            passed.append(ring_shift(direct[k][part], "x", d))

    order = plan[0, :MICRO]
    inputs = jnp.take(samples, order, axis=0).astype(f32)
    chosen = jnp.take(directions, order, axis=0).astype(f32)
    small = lax.all_gather(jnp.concatenate([inputs, chosen], axis=1), ("zl", "core"))
    small = small.reshape(2, 2, 2, 2, REDUCED + TANGENTS).transpose(1, 2, 0, 3, 4)
    small = small.reshape(2, 4, 2, REDUCED + TANGENTS)
    small = jnp.where(core == 0, small, small[::-1])
    small = lax.dynamic_slice_in_dim(jnp.concatenate([small, small], axis=1), z, 4, 1)
    small = small.reshape(8, 2, REDUCED + TANGENTS)
    chosen = small[:, :, REDUCED:].reshape(8, 2 * TANGENTS).astype(jnp.int32)
    onehot = (chosen[:, :, None] == jnp.arange(REDUCED, dtype=jnp.int32)).astype(bf16)
    inputs = jnp.pad(small[:, :, :REDUCED].astype(bf16), ((0, 0), (0, 14), (0, 0)))
    rows = jnp.concatenate([onehot, inputs], axis=1)
    rows_near = rows[:4].reshape(GROUP, REDUCED)
    rows_far = rows[4:].reshape(GROUP, REDUCED)

    own_order = lax.dynamic_slice_in_dim(order, zh * 2, 2)
    target_rows = jnp.take(targets, own_order, axis=0).astype(f32)
    target_jac = jnp.take(jacobian_targets, own_order, axis=0).reshape(2 * TANGENTS, REDUCED)
    wanted = jnp.concatenate(
        [target_jac.astype(f32), jnp.pad(target_rows, ((0, 14), (0, 0)))], axis=0
    )

    *far_saved, far_carried = forward(place, rows_far, weight, direct)
    *near_saved, near_w, near_carried = forward(place, rows_near, weight, direct)
    tan_far, picked_far, lin_far, w_last, sent = forward(
        place, rows_far, weight, passed, far_carried, saved=far_saved
    )
    from_core = core_swap(sent)
    tan_near, picked_near, lin_near, *chunks = forward(
        place, rows_near, weight, passed, near_carried, from_core, near_saved, True
    )
    got = [z_shift(chunks[d], d) for d in (2, 1, 3)]
    total = chunks[0]
    for g in got:
        total = total + g.astype(f32)
    scale = jnp.where(jnp.arange(CHUNK)[:, None] < 2 * TANGENTS, jacobian_weight, 1.0)
    misfit = (scale * (total - wanted)).astype(bf16)
    near = [misfit, None, None, None]
    for d in (2, 1, 3):
        near[d] = z_shift(misfit, 4 - d)
    misfits = near + [core_swap(m) for m in near]

    whole_misfits = [whole_spec((CHUNK, REDUCED))] * 8
    columns = lambda rows: pl.BlockSpec((rows, BLOCK), lambda j, place: (0, j))
    turned = pltpu.VMEM((REDUCED, 2 * GROUP), bf16)
    grad_last = backward(
        last_kernel,
        place,
        [tan_near, tan_far, *misfits],
        [columns(GROUP), columns(GROUP), *whole_misfits],
        [turned],
        1,
    )
    grad_first = backward(
        first_kernel,
        place,
        [rows_near, rows_far, picked_near, picked_far, lin_near, lin_far, w_last, *misfits],
        [whole_spec((GROUP, REDUCED))] * 2
        + [columns(GROUP), columns(GROUP), columns(64), columns(64), columns(REDUCED)]
        + whole_misfits,
        [turned, pltpu.VMEM((2 * GROUP, BLOCK), bf16)],
        2,
    )

    last = ring_sum(grad_last, "x").astype(bf16).reshape(4, 32, COLS)
    first = ring_sum(grad_first, "y").astype(bf16).reshape(4, 32, COLS)
    last = ring_sum(last, "y")
    first = ring_sum(first, "x")

    both = jnp.stack([first.reshape(2, 2, 8, COLS), last.reshape(2, 2, 8, COLS)], axis=2)
    result = lax.all_to_all(
        both.reshape(8, 8, COLS), ("zl", "core", "zh"), split_axis=0, concat_axis=0, tiled=True
    )
    return result.transpose(1, 0, 2).reshape(1, 8, 8 * COLS)


def solution(mesh):
    torus = Mesh(mesh.devices.reshape(4, 4, 2, 2, 2), AXES)
    return jax.shard_map(
        shards,
        mesh=torus,
        in_specs=(
            P(DP, None),
            P(DP, None),
            P(DP, None, None),
            P(DP, None),
            P(DP, None),
            P("zh", None, None),
        ),
        out_specs=P("zh", DP, None),
        check_vma=False,
    )
```

time: 146 us -> 149 us (1.021)
  Pallas kernels: 29.2 us -> 41.2 us
  other arithmetic: 9.41 us -> 5.25 us
  waiting for transfers between devices: 42.4 us -> 39.5 us
  blocking collectives: 18.1 us -> 15.7 us
    pallas_call x3 -> x6, Pallas kernels: 29.2 us -> 41.2 us  [the longest x4 22.7 us: forward(): pl.pallas_call(lambda *refs: forward_kernel(later, final, *refs), grid_sp...]
    ppermute x1 -> x2, waiting for transfers between devices: 9.8 us -> 0.01 us  [z_facing(): return lax.ppermute(block, Z, [(t, 3 - t) for t in range(4)])]
    ppermute x6, waiting for transfers between devices: 20.1 us -> 23.8 us  [z_shift(): lax.ppermute(block, Z, [(z_index(z), z_index((z + d) % 4)) for z in range...]
    ppermute x12 -> x16, waiting for transfers between devices: 11 us -> 14.5 us  [ring_shift(): return lax.ppermute(block, axis, [(i, (i + d) % 4) for i in range(4)])]
    squeeze x5 -> x0, local copies, waits for them, and re-layouts: 3.01 us -> none  [the longest x4 2.09 us: piece(): return lax.dynamic_index_in_dim(chunks, i % 4, 0, keepdims=False)]
    another operation x2 -> x0, other arithmetic: 2.97 us -> none
    all_to_all x1, blocking collectives: 12.1 us -> 9.68 us  [shards(): lax.all_to_all(both.reshape(8, 8, COLS), ('zl', 'core', 'zh'), split_axis...]
    unnamed x28 -> x40, local copies, waits for them, and re-layouts: 1.41 us -> 3.12 us
  transfers between devices with their start and end apart: 24 -> 29, of which waited for: 14 -> 9; matrix products, arithmetic and copies ran while one was open for 8% -> 7% of each run, Pallas kernels for 5% -> 12%
where the time goes in v2:
time: 149 us; the launch traced here: 148 us
  Pallas kernels  41.2 us (28%)
  waiting for transfers between devices  39.5 us (27%)
  starting transfers between devices  36 us (24%)
  blocking collectives  15.7 us (11%)
  local copies, waits for them, and re-layouts  10.3 us (7%)
  other arithmetic  5.25 us (4%)
    ppermute x6, waiting for transfers between devices, z_shift(): lax.ppermute(block, Z, [(z_index(z), z_index((z + d) % 4)) for z in range...  23.8 us
    pallas_call x4, Pallas kernels, forward(): pl.pallas_call(lambda *refs: forward_kernel(later, final, *refs), grid_sp...  22.7 us
    pallas_call x2, Pallas kernels, backward(): pl.pallas_call(kernel, grid_spec=pltpu.PrefetchScalarGridSpec(num_scalar_...  18.5 us
    ppermute x16, starting transfers between devices, ring_shift(): return lax.ppermute(block, axis, [(i, (i + d) % 4) for i in range(4)])  18.3 us
    ppermute x16, waiting for transfers between devices, ring_shift(): return lax.ppermute(block, axis, [(i, (i + d) % 4) for i in range(4)])  14.5 us
    all_to_all x1, blocking collectives, shards(): lax.all_to_all(both.reshape(8, 8, COLS), ('zl', 'core', 'zh'), split_axis...  9.68 us
    ppermute x6, starting transfers between devices, z_shift(): lax.ppermute(block, Z, [(z_index(z), z_index((z + d) % 4)) for z in range...  7.45 us
    all_gather x1, blocking collectives, shards(): lax.all_gather(jnp.concatenate([inputs, chosen], axis=1), ('zl', 'core'))  5.98 us
  transfers between devices with their start and end apart: 29, of which 9 were waited for; matrix products, arithmetic and copies ran while one was open for 7% of the time, Pallas kernels for 12%

profile of v2, /device:TPU:1, one launch (start us, length us, event | category | flops | bytes accessed | tf_op | source)
XLA Modules:
  0.0 148.3 jit_solution(12185874150167062088)
XLA Ops:
  0.0 1.2 dynamic-slice_bitcast_fusion
  1.2 4.7 %collective-permute-start = (bf16[512,256]{1,0:T(8,128)(2,1)S(1)}, bf16[512,256]{1,0:T(8,128)(2,1)S(1)}, u32[]{:S(2)}, u32[]{:S(2)}) collective-permute-start(bf16[512,256]{1,0:T(8,128)(2,1)S(1)} %get-tuple-element.64), channel_id=1, source_target_pairs={{0,5},{1,4},{4,1},{5,0},{2,7},{3,6},{6,3},{7,2},{8,13},{9,12},{12,... | collective-permute-start | bytes 786440 | tf_op jit(solution)/shard_map/ppermute | solution.py:34
  5.9 0.7 fusion.8
  6.6 0.7 compare_and_fusion.1
  7.2 1.3 gather_fusion
  8.5 1.2 gather_fusion.1
  9.9 6.0 %all-gather.1 = f32[4,4,640]{2,1,0:T(4,128)S(1)} all-gather(f32[1,4,640]{2,1,0:T(4,128)S(1)} %maximum_bitcast_fusion), channel_id=2, replica_groups=mesh['x'=4,'y'=4,'zl'=2,'core'=2,'zh'=2] {'zl','core'}, dimensions={0}, use_global_device_ids=true | all-gather | bytes 51200 | tf_op jit(solution)/shard_map/all_gather | solution.py:284
  16.9 1.3 collective-permute-start.1
  18.2 1.3 collective-permute-start.3
  19.5 1.5 collective-permute-start.4
  21.5 1.6 %fusion.10 = (bf16[4,272,512]{2,1,0:T(8,128)(2,1)}, bf16[4,272,512]{2,1,0:T(8,128)(2,1)}) fusion(bf16[8,272,512]{2,1,0:T(8,128)(2,1)S(1)} %fusion.2), kind=kLoop, calls=%fused_computation.47 | loop fusion | bytes 4456448 | tf_op jit(solution)/shard_map/slice | solution.py:295
  23.0 0.6 stack.34.refs_0_.place
  23.7 5.4 %shard_map.65 = (bf16[1088,1024]{1,0:T(8,128)(2,1)}, bf16[1088,1024]{1,0:T(8,128)(2,1)}, f32[64,1024]{1,0:T(8,128)}, bf16[512,1024]{1,0:T(8,128)(2,1)}, f32[1088,512]{1,0:T(8,128)}) custom-call(s32[7]{0:T(128)} %stack.34.refs_0_.place, bf16[1088,512]{1,0:T(8,128)(2,1)} %bitcast.56, bf16[512,8192]{1,0:T(8,128)(2,1)} %bitcast.52, bf16[512,256]{1,0:T(8,128)(2,1)} %copy-done.1, ...), custom_call_target="tpu_custom_call" | custom-call | flops 1140850688 | bytes 2097152 | tf_op jit(solution)/shard_map/pallas_call | solution.py:158
  29.8 5.6 %shard_map.66 = (bf16[1088,1024]{1,0:T(8,128)(2,1)}, bf16[1088,1024]{1,0:T(8,128)(2,1)}, f32[64,1024]{1,0:T(8,128)}, bf16[512,1024]{1,0:T(8,128)(2,1)}, bf16[1088,512]{1,0:T(8,128)(2,1)}) custom-call(s32[7]{0:T(128)} %stack.34.refs_0_.place, bf16[1088,512]{1,0:T(8,128)(2,1)} %bitcast.57, ...), custom_call_target="tpu_custom_call", output_to_operand_aliasing={{0}: (8, {}), {1}: (9, {}), {2}: (10, {}), {3}: (11, {})} | custom-call | flops 1140850688 | bytes 2097152 | tf_op jit(solution)/shard_map/pallas_call | solution.py:158
  35.5 2.1 %collective-permute-start.6 = (bf16[1088,512]{1,0:T(8,128)(2,1)}, bf16[1088,512]{1,0:T(8,128)(2,1)S(1)}, u32[]{:S(2)}, u32[]{:S(2)}) collective-permute-start(bf16[1088,512]{1,0:T(8,128)(2,1)} %get-tuple-element.40), channel_id=1, source_target_pairs={{0,2},{2,0},{1,3},{3,1},{4,6},{6,4},{5,7},{7,5},{8,10},{10,8},{9,1... | collective-permute-start | bytes 3342344 | tf_op jit(solution)/shard_map/ppermute | solution.py:42
  38.4 5.3 %shard_map.64 = (bf16[1088,1024]{1,0:T(8,128)(2,1)}, bf16[1088,1024]{1,0:T(8,128)(2,1)}, f32[64,1024]{1,0:T(8,128)}, bf16[512,1024]{1,0:T(8,128)(2,1)}, f32[1088,512]{1,0:T(8,128)}) custom-call(s32[7]{0:T(128)} %stack.34.refs_0_.place, bf16[1088,512]{1,0:T(8,128)(2,1)} %bitcast.59, bf16[512,8192]{1,0:T(8,128)(2,1)} %bitcast.54, bf16[512,256]{1,0:T(8,128)(2,1)} %copy-done.1, ...), custom_call_target="tpu_custom_call" | custom-call | flops 1140850688 | bytes 2097152 | tf_op jit(solution)/shard_map/pallas_call | solution.py:158
  43.8 1.0 copy-done.3
  44.7 6.4 %shard_map.67 = (bf16[1088,1024]{1,0:T(8,128)(2,1)}, bf16[1088,1024]{1,0:T(8,128)(2,1)}, f32[64,1024]{1,0:T(8,128)}, f32[272,512]{1,0:T(8,128)}, bf16[272,512]{1...) custom-call(s32[7]{0:T(128)} %stack.34.refs_0_.place, ...), custom_call_target="tpu_custom_call", output_to_operand_aliasing={{0}: (9, {}), {1}: (10, {}), {2}: (11, {})} | custom-call | flops 1140850688 | bytes 2097152 | tf_op jit(solution)/shard_map/pallas_call | solution.py:158
  51.2 1.4 collective-permute-start.7
  52.6 1.9 %collective-permute-start.8 = (bf16[272,512]{1,0:T(8,128)(2,1)}, bf16[272,512]{1,0:T(8,128)(2,1)S(1)}, u32[]{:S(2)}, u32[]{:S(2)}) collective-permute-start(bf16[272,512]{1,0:T(8,128)(2,1)} %get-tuple-element.51), channel_id=1, source_target_pairs={{0,4},{4,1},{1,5},{5,0},{2,6},{6,3},{3,7},{7,2},{8,12},{12,9},{9,1... | collective-permute-start | bytes 835592 | tf_op jit(solution)/shard_map/ppermute | solution.py:30
  54.5 0.7 collective-permute-start.9
  55.9 5.3 %collective-permute-done.7 = bf16[272,512]{1,0:T(8,128)(2,1)S(1)} collective-permute-done((bf16[272,512]{1,0:T(8,128)(2,1)}, bf16[272,512]{1,0:T(8,128)(2,1)S(1)}, u32[]{:S(2)}, u32[]{:S(2)}) %collective-permute-start.7) | collective-permute-done | bytes 278560 | tf_op jit(solution)/shard_map/ppermute | solution.py:30
  61.2 6.3 %collective-permute-done.8 = bf16[272,512]{1,0:T(8,128)(2,1)S(1)} collective-permute-done((bf16[272,512]{1,0:T(8,128)(2,1)}, bf16[272,512]{1,0:T(8,128)(2,1)S(1)}, u32[]{:S(2)}, u32[]{:S(2)}) %collective-permute-start.8) | collective-permute-done | bytes 278560 | tf_op jit(solution)/shard_map/ppermute | solution.py:30
  67.6 1.2 multiply_convert_fusion.refs_0_
  68.8 2.7 %collective-permute-start.10 = (bf16[272,512]{1,0:T(8,128)(2,1)S(1)}, bf16[272,512]{1,0:T(8,128)(2,1)S(1)}, u32[]{:S(2)}, u32[]{:S(2)}) collective-permute-start(bf16[272,512]{1,0:T(8,128)(2,1)S(1)} %multiply_convert_fusion.refs_0_), channel_id=1, source_target_pairs={{0,5},{4,0},{1,4},{5,1},{2,7},{6,2},{3,6},{7,3},{8,13},{12,8},{9,1... | collective-permute-start | bytes 835592 | tf_op jit(solution)/shard_map/ppermute | solution.py:30
  71.5 0.7 collective-permute-start.12
  72.2 1.1 collective-permute-start.13
  73.3 9.6 %collective-permute-done.10.refs_1_ = bf16[272,512]{1,0:T(8,128)(2,1)S(1)} collective-permute-done((bf16[272,512]{1,0:T(8,128)(2,1)S(1)}, bf16[272,512]{1,0:T(8,128)(2,1)S(1)}, u32[]{:S(2)}, u32[]{:S(2)}) %collective-permute-start.10) | collective-permute-done | bytes 278560 | tf_op jit(solution)/shard_map/ppermute | solution.py:30
  82.9 1.5 %collective-permute-start.14 = (bf16[272,512]{1,0:T(8,128)(2,1)S(1)}, bf16[272,512]{1,0:T(8,128)(2,1)S(1)}, u32[]{:S(2)}, u32[]{:S(2)}) collective-permute-start(bf16[272,512]{1,0:T(8,128)(2,1)S(1)} %collective-permute-done.10.refs_1_), channel_id=1, source_target_pairs={{0,2},{2,0},{1,3},{3,1},{4,6},{6,4},{5,7},{7,5},{8,10},{10,8},{9,1... | collective-permute-start | bytes 835592 | tf_op jit(solution)/shard_map/ppermute | solution.py:42
  84.5 2.5 %collective-permute-done.12.refs_3_ = bf16[272,512]{1,0:T(8,128)(2,1)S(1)} collective-permute-done((bf16[272,512]{1,0:T(8,128)(2,1)S(1)}, bf16[272,512]{1,0:T(8,128)(2,1)S(1)}, u32[]{:S(2)}, u32[]{:S(2)}) %collective-permute-start.12) | collective-permute-done | bytes 278560 | tf_op jit(solution)/shard_map/ppermute | solution.py:30
  87.0 0.8 collective-permute-start.16
  87.8 1.1 collective-permute-done.16.refs_7_
  89.0 0.7 copy-done.17
  89.7 10.7 %shard_map.68 = (bf16[128,1024]{1,0:T(8,128)(2,1)}, bf16[128,1024]{1,0:T(8,128)(2,1)}, bf16[128,1024]{1,0:T(8,128)(2,1)}, bf16[128,1024]{1,0:T(8,128)(2,1)}) custom-call(s32[7]{0:T(128)} %stack.34.refs_0_.place, bf16[1088,512]{1,0:T(8,128)(2,1)} %bitcast.61, bf16[1088,512]{1,0:T(8,128)(2,1)} %bitcast.58, bf16[1088,1024]{1,0:T(8,128)(2,1)} %get-tuple-element.44.near, ...), custom_call_target="tpu_custom_call" | custom-call | flops 4563402752 | bytes 4456448 | tf_op jit(solution)/shard_map/pallas_call | solution.py:234
  100.4 3.0 %collective-permute-start.17 = (bf16[128,1024]{1,0:T(8,128)(2,1)}, bf16[128,1024]{1,0:T(8,128)(2,1)S(1)}, u32[]{:S(2)}, u32[]{:S(2)}) collective-permute-start(bf16[128,1024]{1,0:T(8,128)(2,1)} %get-tuple-element.54), channel_id=1, source_target_pairs={{0,16},{8,24},{16,0},{24,8},{1,17},{9,25},{17,1},{25,9},{2,18},{10... | collective-permute-start | bytes 786440 | tf_op jit(solution)/shard_map/ppermute | solution.py:38
  103.8 2.3 %collective-permute-start.19 = (bf16[128,1024]{1,0:T(8,128)(2,1)}, bf16[128,1024]{1,0:T(8,128)(2,1)S(1)}, u32[]{:S(2)}, u32[]{:S(2)}) collective-permute-start(bf16[128,1024]{1,0:T(8,128)(2,1)} %get-tuple-element.56), channel_id=1, source_target_pairs={{0,24},{8,0},{16,8},{24,16},{1,25},{9,1},{17,9},{25,17},{2,26},{10... | collective-permute-start | bytes 786440 | tf_op jit(solution)/shard_map/ppermute | solution.py:38
  106.1 7.7 %shard_map.69 = (bf16[128,1024]{1,0:T(8,128)(2,1)}, bf16[128,1024]{1,0:T(8,128)(2,1)}, bf16[128,1024]{1,0:T(8,128)(2,1)}, bf16[128,1024]{1,0:T(8,128)(2,1)}) custom-call(s32[7]{0:T(128)} %stack.34.refs_0_.place, bf16[1088,1024]{1,0:T(8,128)(2,1)} %get-tuple-element.57.near, bf16[1088,1024]{1,0:T(8,128)(2,1)} %get-tuple-element.58.far, ...), custom_call_target="tpu_custom_call" | custom-call | flops 2281701376 | bytes 4456448 | tf_op jit(solution)/shard_map/pallas_call | solution.py:234
  113.8 0.7 collective-permute-start.23
  115.0 2.2 %collective-permute-start.25 = (bf16[128,1024]{1,0:T(8,128)(2,1)}, bf16[128,1024]{1,0:T(8,128)(2,1)S(1)}, u32[]{:S(2)}, u32[]{:S(2)}) collective-permute-start(bf16[128,1024]{1,0:T(8,128)(2,1)} %get-tuple-element.62), channel_id=1, source_target_pairs={{0,96},{32,0},{64,32},{96,64},{1,97},{33,1},{65,33},{97,65},{2,98}... | collective-permute-start | bytes 786440 | tf_op jit(solution)/shard_map/ppermute | solution.py:38
  117.4 1.2 collective-permute-start.20
  118.9 3.4 %collective-permute-done.23 = bf16[128,1024]{1,0:T(8,128)(2,1)S(1)} collective-permute-done((bf16[128,1024]{1,0:T(8,128)(2,1)}, bf16[128,1024]{1,0:T(8,128)(2,1)S(1)}, u32[]{:S(2)}, u32[]{:S(2)}) %collective-permute-start.23) | collective-permute-done | bytes 262176 | tf_op jit(solution)/shard_map/ppermute | solution.py:38
  122.7 7.4 %collective-permute-done.24 = bf16[128,1024]{1,0:T(8,128)(2,1)S(1)} collective-permute-done((bf16[128,1024]{1,0:T(8,128)(2,1)}, bf16[128,1024]{1,0:T(8,128)(2,1)S(1)}, u32[]{:S(2)}, u32[]{:S(2)}) %collective-permute-start.24) | collective-permute-done | bytes 262176 | tf_op jit(solution)/shard_map/ppermute | solution.py:38
  130.2 1.1 add_convert_fusion
  132.0 2.2 %collective-permute-start.28 = (bf16[32,1024]{1,0:T(8,128)(2,1)S(1)}, bf16[32,1024]{1,0:T(8,128)(2,1)S(1)}, u32[]{:S(2)}, u32[]{:S(2)}) collective-permute-start(bf16[32,1024]{1,0:T(8,128)(2,1)S(1)} %get-tuple-element.71), channel_id=1, source_target_pairs={{0,24},{8,0},{16,8},{24,16},{1,25},{9,1},{17,9},{25,17},{2,26},{10... | collective-permute-start | bytes 196616 | tf_op jit(solution)/shard_map/ppermute | solution.py:38
  134.2 1.9 %collective-permute-done.26 = bf16[32,1024]{1,0:T(8,128)(2,1)S(1)} collective-permute-done((bf16[32,1024]{1,0:T(8,128)(2,1)S(1)}, bf16[32,1024]{1,0:T(8,128)(2,1)S(1)}, u32[]{:S(2)}, u32[]{:S(2)}) %collective-permute-start.26) | collective-permute-done | bytes 65568 | tf_op jit(solution)/shard_map/ppermute | solution.py:38
  136.1 1.7 %collective-permute-done.27 = bf16[32,1024]{1,0:T(8,128)(2,1)S(1)} collective-permute-done((bf16[32,1024]{1,0:T(8,128)(2,1)S(1)}, bf16[32,1024]{1,0:T(8,128)(2,1)S(1)}, u32[]{:S(2)}, u32[]{:S(2)}) %collective-permute-start.27) | collective-permute-done | bytes 65568 | tf_op jit(solution)/shard_map/ppermute | solution.py:38
  137.9 9.7 %all_to_all.5 = f32[8,8,1024]{2,1,0:T(8,128)S(1)} all-to-all(f32[8,8,1024]{2,1,0:T(8,128)S(1)} %bitcast.62), channel_id=1, replica_groups=mesh['x'=4,'y'=4,'zl'=2,'core'=2,'zh'=2] {'zl','core','zh'}, dimensions={0} | all-to-all | bytes 524288 | tf_op jit(solution)/shard_map/all_to_all | solution.py:352
  147.6 0.7 copy.31
  (96 shorter events, 6.6 us)
Async XLA Ops:
  0.0 55.3 %copy-start = (bf16[8,128,512]{2,1,0:T(8,128)(2,1)S(1)}, bf16[8,128,512]{2,1,0:T(8,128)(2,1)}, u32[]{:S(2)}) copy-start(bf16[8,128,512]{2,1,0:T(8,128)(2,1)} %param.8) | copy-start | bytes 3145732
  1.2 15.7 %collective-permute-start = (bf16[512,256]{1,0:T(8,128)(2,1)S(1)}, bf16[512,256]{1,0:T(8,128)(2,1)S(1)}, u32[]{:S(2)}, u32[]{:S(2)}) collective-permute-start(bf16[512,256]{1,0:T(8,128)(2,1)S(1)} %get-tuple-element.64), channel_id=1, source_target_pairs={{0,5},{1,4},{4,1},{5,0},{2,7},{3,6},{6,3},{7,2},{8,13},{9,12},{12,... | collective-permute-start | bytes 786440 | tf_op jit(solution)/shard_map/ppermute | solution.py:34
  5.8 12.3 %collective-permute-start.2 = (bf16[512,256]{1,0:T(8,128)(2,1)S(1)}, bf16[512,256]{1,0:T(8,128)(2,1)S(1)}, u32[]{:S(2)}, u32[]{:S(2)}) collective-permute-start(bf16[512,256]{1,0:T(8,128)(2,1)S(1)} %get-tuple-element.63), channel_id=1, source_target_pairs={{0,5},{1,4},{4,1},{5,0},{2,7},{3,6},{6,3},{7,2},{8,13},{9,12},{12,... | collective-permute-start | bytes 786440 | tf_op jit(solution)/shard_map/ppermute | solution.py:34
  16.8 6.2 %copy-start.1 = (bf16[512,256]{1,0:T(8,128)(2,1)}, bf16[512,256]{1,0:T(8,128)(2,1)S(1)}, u32[]{:S(2)}) copy-start(bf16[512,256]{1,0:T(8,128)(2,1)S(1)} %collective-permute-done.refs_3_) | copy-start | bytes 786436
  16.9 12.2 %collective-permute-start.1 = (bf16[256,256]{1,0:T(8,128)(2,1)S(1)}, bf16[256,256]{1,0:T(8,128)(2,1)S(1)}, u32[]{:S(2)}, u32[]{:S(2)}) collective-permute-start(bf16[256,256]{1,0:T(8,128)(2,1)S(1)} %get-tuple-element.76), channel_id=1, source_target_pairs={{0,32},{32,64},{64,96},{96,0},{1,33},{33,65},{65,97},{97,1},{2,34}... | collective-permute-start | bytes 393224 | tf_op jit(solution)/shard_map/ppermute | solution.py:38
  18.1 4.9 %copy-start.2 = (bf16[512,256]{1,0:T(8,128)(2,1)}, bf16[512,256]{1,0:T(8,128)(2,1)S(1)}, u32[]{:S(2)}) copy-start(bf16[512,256]{1,0:T(8,128)(2,1)S(1)} %collective-permute-done.2.refs_4_) | copy-start | bytes 786436
  18.2 10.9 %collective-permute-start.3 = (bf16[256,256]{1,0:T(8,128)(2,1)S(1)}, bf16[256,256]{1,0:T(8,128)(2,1)S(1)}, u32[]{:S(2)}, u32[]{:S(2)}) collective-permute-start(bf16[256,256]{1,0:T(8,128)(2,1)S(1)} %get-tuple-element.74), channel_id=1, source_target_pairs={{0,32},{32,64},{64,96},{96,0},{1,33},{33,65},{65,97},{97,1},{2,34}... | collective-permute-start | bytes 393224 | tf_op jit(solution)/shard_map/ppermute | solution.py:38
  19.5 9.6 %collective-permute-start.4 = (bf16[256,256]{1,0:T(8,128)(2,1)S(1)}, bf16[256,256]{1,0:T(8,128)(2,1)S(1)}, u32[]{:S(2)}, u32[]{:S(2)}) collective-permute-start(bf16[256,256]{1,0:T(8,128)(2,1)S(1)} %get-tuple-element.75), channel_id=1, source_target_pairs={{0,96},{32,0},{64,32},{96,64},{1,97},{33,1},{65,33},{97,65},{2,98}... | collective-permute-start | bytes 393224 | tf_op jit(solution)/shard_map/ppermute | solution.py:38
  20.9 8.2 %collective-permute-start.5 = (bf16[256,256]{1,0:T(8,128)(2,1)S(1)}, bf16[256,256]{1,0:T(8,128)(2,1)S(1)}, u32[]{:S(2)}, u32[]{:S(2)}) collective-permute-start(bf16[256,256]{1,0:T(8,128)(2,1)S(1)} %get-tuple-element.73), channel_id=1, source_target_pairs={{0,96},{32,0},{64,32},{96,64},{1,97},{33,1},{65,33},{97,65},{2,98}... | collective-permute-start | bytes 393224 | tf_op jit(solution)/shard_map/ppermute | solution.py:38
  29.0 0.7 copy-start.4
  29.1 0.7 copy-start.5
  29.1 0.7 copy-start.6
  29.1 0.7 copy-start.7
  29.8 7.7 %copy-start.18 = (s32[1,8]{1,0:T(1,128)S(1)}, s32[1,8]{1,0:T(1,128)}, u32[]{:S(2)}) copy-start(s32[1,8]{1,0:T(1,128)} %param.10) | copy-start | bytes 100
  29.8 7.8 %copy-start.10 = (bf16[8,512]{1,0:T(8,128)(2,1)S(1)}, bf16[8,512]{1,0:T(8,128)(2,1)}, u32[]{:S(2)}) copy-start(bf16[8,512]{1,0:T(8,128)(2,1)} %param.7) | copy-start | bytes 24580
  35.5 8.3 %collective-permute-start.6 = (bf16[1088,512]{1,0:T(8,128)(2,1)}, bf16[1088,512]{1,0:T(8,128)(2,1)S(1)}, u32[]{:S(2)}, u32[]{:S(2)}) collective-permute-start(bf16[1088,512]{1,0:T(8,128)(2,1)} %get-tuple-element.40), channel_id=1, source_target_pairs={{0,2},{2,0},{1,3},{3,1},{4,6},{6,4},{5,7},{7,5},{8,10},{10,8},{9,1... | collective-permute-start | bytes 3342344 | tf_op jit(solution)/shard_map/ppermute | solution.py:42
  43.7 1.0 copy-start.3
  51.2 10.0 %collective-permute-start.7 = (bf16[272,512]{1,0:T(8,128)(2,1)}, bf16[272,512]{1,0:T(8,128)(2,1)S(1)}, u32[]{:S(2)}, u32[]{:S(2)}) collective-permute-start(bf16[272,512]{1,0:T(8,128)(2,1)} %get-tuple-element.50), channel_id=1, source_target_pairs={{0,1},{4,5},{1,0},{5,4},{2,3},{6,7},{3,2},{7,6},{8,9},{12,13},{9,8... | collective-permute-start | bytes 835592 | tf_op jit(solution)/shard_map/ppermute | solution.py:30
  52.6 15.0 %collective-permute-start.8 = (bf16[272,512]{1,0:T(8,128)(2,1)}, bf16[272,512]{1,0:T(8,128)(2,1)S(1)}, u32[]{:S(2)}, u32[]{:S(2)}) collective-permute-start(bf16[272,512]{1,0:T(8,128)(2,1)} %get-tuple-element.51), channel_id=1, source_target_pairs={{0,4},{4,1},{1,5},{5,0},{2,6},{6,3},{3,7},{7,2},{8,12},{12,9},{9,1... | collective-permute-start | bytes 835592 | tf_op jit(solution)/shard_map/ppermute | solution.py:30
  54.5 13.0 %collective-permute-start.9 = (bf16[272,512]{1,0:T(8,128)(2,1)}, bf16[272,512]{1,0:T(8,128)(2,1)S(1)}, u32[]{:S(2)}, u32[]{:S(2)}) collective-permute-start(bf16[272,512]{1,0:T(8,128)(2,1)} %get-tuple-element.52), channel_id=1, source_target_pairs={{0,5},{4,0},{1,4},{5,1},{2,7},{6,2},{3,6},{7,3},{8,13},{12,8},{9,1... | collective-permute-start | bytes 835592 | tf_op jit(solution)/shard_map/ppermute | solution.py:30
  68.8 20.2 %copy-start.8 = (bf16[272,512]{1,0:T(8,128)(2,1)}, bf16[272,512]{1,0:T(8,128)(2,1)S(1)}, u32[]{:S(2)}) copy-start(bf16[272,512]{1,0:T(8,128)(2,1)S(1)} %multiply_convert_fusion.refs_0_) | copy-start | bytes 835588
  68.8 14.1 %collective-permute-start.10 = (bf16[272,512]{1,0:T(8,128)(2,1)S(1)}, bf16[272,512]{1,0:T(8,128)(2,1)S(1)}, u32[]{:S(2)}, u32[]{:S(2)}) collective-permute-start(bf16[272,512]{1,0:T(8,128)(2,1)S(1)} %multiply_convert_fusion.refs_0_), channel_id=1, source_target_pairs={{0,5},{4,0},{1,4},{5,1},{2,7},{6,2},{3,6},{7,3},{8,13},{12,8},{9,1... | collective-permute-start | bytes 835592 | tf_op jit(solution)/shard_map/ppermute | solution.py:30
  71.5 12.8 %collective-permute-start.11 = (bf16[272,512]{1,0:T(8,128)(2,1)S(1)}, bf16[272,512]{1,0:T(8,128)(2,1)S(1)}, u32[]{:S(2)}, u32[]{:S(2)}) collective-permute-start(bf16[272,512]{1,0:T(8,128)(2,1)S(1)} %multiply_convert_fusion.refs_0_), channel_id=1, source_target_pairs={{0,1},{4,5},{1,0},{5,4},{2,3},{6,7},{3,2},{7,6},{8,9},{12,13},{9,8... | collective-permute-start | bytes 835592 | tf_op jit(solution)/shard_map/ppermute | solution.py:30
  71.5 15.5 %collective-permute-start.12 = (bf16[272,512]{1,0:T(8,128)(2,1)S(1)}, bf16[272,512]{1,0:T(8,128)(2,1)S(1)}, u32[]{:S(2)}, u32[]{:S(2)}) collective-permute-start(bf16[272,512]{1,0:T(8,128)(2,1)S(1)} %multiply_convert_fusion.refs_0_), channel_id=1, source_target_pairs={{0,4},{4,1},{1,5},{5,0},{2,6},{6,3},{3,7},{7,2},{8,12},{12,9},{9,1... | collective-permute-start | bytes 835592 | tf_op jit(solution)/shard_map/ppermute | solution.py:30
  72.2 15.6 %collective-permute-start.13 = (bf16[272,512]{1,0:T(8,128)(2,1)S(1)}, bf16[272,512]{1,0:T(8,128)(2,1)S(1)}, u32[]{:S(2)}, u32[]{:S(2)}) collective-permute-start(bf16[272,512]{1,0:T(8,128)(2,1)S(1)} %multiply_convert_fusion.refs_0_), channel_id=1, source_target_pairs={{0,2},{2,0},{1,3},{3,1},{4,6},{6,4},{5,7},{7,5},{8,10},{10,8},{9,1... | collective-permute-start | bytes 835592 | tf_op jit(solution)/shard_map/ppermute | solution.py:42
  82.9 6.1 %copy-start.11 = (bf16[272,512]{1,0:T(8,128)(2,1)}, bf16[272,512]{1,0:T(8,128)(2,1)S(1)}, u32[]{:S(2)}) copy-start(bf16[272,512]{1,0:T(8,128)(2,1)S(1)} %collective-permute-done.10.refs_1_) | copy-start | bytes 835588
  82.9 4.9 %collective-permute-start.14 = (bf16[272,512]{1,0:T(8,128)(2,1)S(1)}, bf16[272,512]{1,0:T(8,128)(2,1)S(1)}, u32[]{:S(2)}, u32[]{:S(2)}) collective-permute-start(bf16[272,512]{1,0:T(8,128)(2,1)S(1)} %collective-permute-done.10.refs_1_), channel_id=1, source_target_pairs={{0,2},{2,0},{1,3},{3,1},{4,6},{6,4},{5,7},{7,5},{8,10},{10,8},{9,1... | collective-permute-start | bytes 835592 | tf_op jit(solution)/shard_map/ppermute | solution.py:42
  84.4 4.6 %copy-start.12 = (bf16[272,512]{1,0:T(8,128)(2,1)}, bf16[272,512]{1,0:T(8,128)(2,1)S(1)}, u32[]{:S(2)}) copy-start(bf16[272,512]{1,0:T(8,128)(2,1)S(1)} %collective-permute-done.11.refs_2_) | copy-start | bytes 835588
  84.4 3.4 %collective-permute-start.15 = (bf16[272,512]{1,0:T(8,128)(2,1)S(1)}, bf16[272,512]{1,0:T(8,128)(2,1)S(1)}, u32[]{:S(2)}, u32[]{:S(2)}) collective-permute-start(bf16[272,512]{1,0:T(8,128)(2,1)S(1)} %collective-permute-done.11.refs_2_), channel_id=1, source_target_pairs={{0,2},{2,0},{1,3},{3,1},{4,6},{6,4},{5,7},{7,5},{8,10},{10,8},{9,1... | collective-permute-start | bytes 835592 | tf_op jit(solution)/shard_map/ppermute | solution.py:42
  87.0 2.0 %copy-start.13 = (bf16[272,512]{1,0:T(8,128)(2,1)}, bf16[272,512]{1,0:T(8,128)(2,1)S(1)}, u32[]{:S(2)}) copy-start(bf16[272,512]{1,0:T(8,128)(2,1)S(1)} %collective-permute-done.12.refs_3_) | copy-start | bytes 835588
  87.0 2.0 %collective-permute-start.16 = (bf16[272,512]{1,0:T(8,128)(2,1)S(1)}, bf16[272,512]{1,0:T(8,128)(2,1)S(1)}, u32[]{:S(2)}, u32[]{:S(2)}) collective-permute-start(bf16[272,512]{1,0:T(8,128)(2,1)S(1)} %collective-permute-done.12.refs_3_), channel_id=1, source_target_pairs={{0,2},{2,0},{1,3},{3,1},{4,6},{6,4},{5,7},{7,5},{8,10},{10,8},{9,1... | collective-permute-start | bytes 835592 | tf_op jit(solution)/shard_map/ppermute | solution.py:42
  87.8 1.2 copy-start.14
  87.8 1.2 copy-start.15
  87.8 1.2 copy-start.16
  89.0 0.7 copy-start.17
  100.4 14.5 %collective-permute-start.17 = (bf16[128,1024]{1,0:T(8,128)(2,1)}, bf16[128,1024]{1,0:T(8,128)(2,1)S(1)}, u32[]{:S(2)}, u32[]{:S(2)}) collective-permute-start(bf16[128,1024]{1,0:T(8,128)(2,1)} %get-tuple-element.54), channel_id=1, source_target_pairs={{0,16},{8,24},{16,0},{24,8},{1,17},{9,25},{17,1},{25,9},{2,18},{10... | collective-permute-start | bytes 786440 | tf_op jit(solution)/shard_map/ppermute | solution.py:38
  103.4 13.8 %collective-permute-start.18 = (bf16[128,1024]{1,0:T(8,128)(2,1)}, bf16[128,1024]{1,0:T(8,128)(2,1)S(1)}, u32[]{:S(2)}, u32[]{:S(2)}) collective-permute-start(bf16[128,1024]{1,0:T(8,128)(2,1)} %get-tuple-element.55), channel_id=1, source_target_pairs={{0,8},{8,16},{16,24},{24,0},{1,9},{9,17},{17,25},{25,1},{2,10},{10... | collective-permute-start | bytes 786440 | tf_op jit(solution)/shard_map/ppermute | solution.py:38
  103.8 13.4 %collective-permute-start.19 = (bf16[128,1024]{1,0:T(8,128)(2,1)}, bf16[128,1024]{1,0:T(8,128)(2,1)S(1)}, u32[]{:S(2)}, u32[]{:S(2)}) collective-permute-start(bf16[128,1024]{1,0:T(8,128)(2,1)} %get-tuple-element.56), channel_id=1, source_target_pairs={{0,24},{8,0},{16,8},{24,16},{1,25},{9,1},{17,9},{25,17},{2,26},{10... | collective-permute-start | bytes 786440 | tf_op jit(solution)/shard_map/ppermute | solution.py:38
  106.1 11.1 %copy-start.9 = (bf16[128,1024]{1,0:T(8,128)(2,1)S(1)}, bf16[128,1024]{1,0:T(8,128)(2,1)}, u32[]{:S(2)}) copy-start(bf16[128,1024]{1,0:T(8,128)(2,1)} %get-tuple-element.53) | copy-start | bytes 786436
  113.8 8.5 %collective-permute-start.23 = (bf16[128,1024]{1,0:T(8,128)(2,1)}, bf16[128,1024]{1,0:T(8,128)(2,1)S(1)}, u32[]{:S(2)}, u32[]{:S(2)}) collective-permute-start(bf16[128,1024]{1,0:T(8,128)(2,1)} %get-tuple-element.60), channel_id=1, source_target_pairs={{0,64},{32,96},{64,0},{96,32},{1,65},{33,97},{65,1},{97,33},{2,66}... | collective-permute-start | bytes 786440 | tf_op jit(solution)/shard_map/ppermute | solution.py:38
  114.5 15.6 %collective-permute-start.24 = (bf16[128,1024]{1,0:T(8,128)(2,1)}, bf16[128,1024]{1,0:T(8,128)(2,1)S(1)}, u32[]{:S(2)}, u32[]{:S(2)}) collective-permute-start(bf16[128,1024]{1,0:T(8,128)(2,1)} %get-tuple-element.61), channel_id=1, source_target_pairs={{0,32},{32,64},{64,96},{96,0},{1,33},{33,65},{65,97},{97,1},{2,34}... | collective-permute-start | bytes 786440 | tf_op jit(solution)/shard_map/ppermute | solution.py:38
  115.0 15.2 %collective-permute-start.25 = (bf16[128,1024]{1,0:T(8,128)(2,1)}, bf16[128,1024]{1,0:T(8,128)(2,1)S(1)}, u32[]{:S(2)}, u32[]{:S(2)}) collective-permute-start(bf16[128,1024]{1,0:T(8,128)(2,1)} %get-tuple-element.62), channel_id=1, source_target_pairs={{0,96},{32,0},{64,32},{96,64},{1,97},{33,1},{65,33},{97,65},{2,98}... | collective-permute-start | bytes 786440 | tf_op jit(solution)/shard_map/ppermute | solution.py:38
  117.4 14.6 %collective-permute-start.20 = (bf16[32,1024]{1,0:T(8,128)(2,1)S(1)}, bf16[32,1024]{1,0:T(8,128)(2,1)S(1)}, u32[]{:S(2)}, u32[]{:S(2)}) collective-permute-start(bf16[32,1024]{1,0:T(8,128)(2,1)S(1)} %get-tuple-element.67), channel_id=1, source_target_pairs={{0,64},{32,96},{64,0},{96,32},{1,65},{33,97},{65,1},{97,33},{2,66}... | collective-permute-start | bytes 196616 | tf_op jit(solution)/shard_map/ppermute | solution.py:38
  118.6 15.5 %collective-permute-start.21 = (bf16[32,1024]{1,0:T(8,128)(2,1)S(1)}, bf16[32,1024]{1,0:T(8,128)(2,1)S(1)}, u32[]{:S(2)}, u32[]{:S(2)}) collective-permute-start(bf16[32,1024]{1,0:T(8,128)(2,1)S(1)} %get-tuple-element.69), channel_id=1, source_target_pairs={{0,32},{32,64},{64,96},{96,0},{1,33},{33,65},{65,97},{97,1},{2,34}... | collective-permute-start | bytes 196616 | tf_op jit(solution)/shard_map/ppermute | solution.py:38
  122.3 11.9 %collective-permute-start.22 = (bf16[32,1024]{1,0:T(8,128)(2,1)S(1)}, bf16[32,1024]{1,0:T(8,128)(2,1)S(1)}, u32[]{:S(2)}, u32[]{:S(2)}) collective-permute-start(bf16[32,1024]{1,0:T(8,128)(2,1)S(1)} %get-tuple-element.68), channel_id=1, source_target_pairs={{0,96},{32,0},{64,32},{96,64},{1,97},{33,1},{65,33},{97,65},{2,98}... | collective-permute-start | bytes 196616 | tf_op jit(solution)/shard_map/ppermute | solution.py:38
  131.3 4.8 %collective-permute-start.26 = (bf16[32,1024]{1,0:T(8,128)(2,1)S(1)}, bf16[32,1024]{1,0:T(8,128)(2,1)S(1)}, u32[]{:S(2)}, u32[]{:S(2)}) collective-permute-start(bf16[32,1024]{1,0:T(8,128)(2,1)S(1)} %get-tuple-element.70), channel_id=1, source_target_pairs={{0,16},{8,24},{16,0},{24,8},{1,17},{9,25},{17,1},{25,9},{2,18},{10... | collective-permute-start | bytes 196616 | tf_op jit(solution)/shard_map/ppermute | solution.py:38
  131.4 6.5 %collective-permute-start.27 = (bf16[32,1024]{1,0:T(8,128)(2,1)S(1)}, bf16[32,1024]{1,0:T(8,128)(2,1)S(1)}, u32[]{:S(2)}, u32[]{:S(2)}) collective-permute-start(bf16[32,1024]{1,0:T(8,128)(2,1)S(1)} %get-tuple-element.72), channel_id=1, source_target_pairs={{0,8},{8,16},{16,24},{24,0},{1,9},{9,17},{17,25},{25,1},{2,10},{10... | collective-permute-start | bytes 196616 | tf_op jit(solution)/shard_map/ppermute | solution.py:38
  132.0 5.9 %collective-permute-start.28 = (bf16[32,1024]{1,0:T(8,128)(2,1)S(1)}, bf16[32,1024]{1,0:T(8,128)(2,1)S(1)}, u32[]{:S(2)}, u32[]{:S(2)}) collective-permute-start(bf16[32,1024]{1,0:T(8,128)(2,1)S(1)} %get-tuple-element.71), channel_id=1, source_target_pairs={{0,24},{8,0},{16,8},{24,16},{1,25},{9,1},{17,9},{25,17},{2,26},{10... | collective-permute-start | bytes 196616 | tf_op jit(solution)/shard_map/ppermute | solution.py:38

commit v3 on v1

v3 whole, which is shorter than its diff:
```python
import jax
import jax.numpy as jnp
from jax import lax
from jax.experimental import pallas as pl
from jax.experimental.pallas import tpu as pltpu
from jax.sharding import Mesh
from jax.sharding import PartitionSpec as P

AXES = ("x", "y", "zl", "core", "zh")
DP = ("x", "y", "zl", "core")
Z = ("zl", "zh")
MICRO = 4
REDUCED = 512
COLS = 1024
BLOCK = 256
TANGENTS = 128
CHUNK = 2 * TANGENTS + 16
GROUP = 4 * CHUNK
STEP = 2 * CHUNK
jacobian_weight = 32.0
f32 = jnp.float32
bf16 = jnp.bfloat16


def z_index(z):
    return (z % 2) * 2 + z // 2


def z_shift(block, d):
    return lax.ppermute(block, Z, [(z_index(z), z_index((z + d) % 4)) for z in range(4)])


def z_facing(block):
    return lax.ppermute(block, Z, [(t, 3 - t) for t in range(4)])


def ring_shift(block, axis, d):
    return lax.ppermute(block, axis, [(i, (i + d) % 4) for i in range(4)])


def core_swap(block):
    return lax.ppermute(block, "core", [(0, 1), (1, 0)])


def slopes(linear):
    squash = jax.nn.sigmoid(linear)
    first = squash * (1.0 + linear * (1.0 - squash))
    second = squash * (1.0 - squash) * (2.0 + linear * (1.0 - 2.0 * squash))
    return linear * squash, first, second


def per_row(top, first):
    return [top[:TANGENTS] * first[0:1], top[TANGENTS : 2 * TANGENTS] * first[1:2]]


def whole_spec(shape):
    return pl.BlockSpec(shape, lambda i, place: (0,) * len(shape))


def own_specs():
    return [pl.BlockSpec((REDUCED, BLOCK), lambda i, place, k=k: (0, place[k])) for k in range(4)]


def forward_kernel(final, place, rows, *refs):
    own, other, refs = refs[:4], refs[4:8], refs[8:]
    if final:
        arrived, refs = refs[0], refs[1:]
    w_first, w_last = refs[-2:]
    outs = refs[:-2]

    @pl.when(pl.program_id(0) == 0)
    def _():
        here = place[4] == 0
        for k in range(4):
            span = slice(k * BLOCK, (k + 1) * BLOCK)
            w_first[:, span] = jnp.where(here, own[k][...], other[k][...])
            w_last[:, span] = jnp.where(here, other[k][...], own[k][...])

    picked = jnp.dot(rows[...], w_first[...], preferred_element_type=f32)
    parts = []
    for c in range(2):
        part = picked[c * CHUNK : (c + 1) * CHUNK]
        hidden, first, _ = slopes(part[2 * TANGENTS :])
        parts += per_row(part, first) + [hidden]
    tangent = jnp.concatenate(parts, axis=0).astype(bf16)
    total = lax.dot_general(
        tangent, w_last[...], (((1,), (1,)), ((), ())), preferred_element_type=f32
    )
    if not final:
        outs[0][...] = total.astype(bf16)
        return
    total = total + arrived[...].astype(f32)

    @pl.when(pl.program_id(0) == 0)
    def _():
        outs[0][...] = total[:CHUNK]
        outs[1][...] = total[CHUNK:].astype(bf16)

    @pl.when(pl.program_id(0) == 1)
    def _():
        outs[2][...] = total[:CHUNK].astype(bf16)
        outs[3][...] = total[CHUNK:].astype(bf16)


def forward(place, rows, weight, other, arrived=None):
    final = arrived is not None
    base = 0 if final else 2
    in_specs = [pl.BlockSpec((STEP, REDUCED), lambda i, place: (i + base, 0)), *own_specs()]
    in_specs += [whole_spec((REDUCED, BLOCK))] * 4
    args = [rows, weight, weight, weight, weight, *other]
    out_specs = pl.BlockSpec((STEP, REDUCED), lambda i, place: (i, 0))
    out_shape = jax.ShapeDtypeStruct((GROUP, REDUCED), bf16)
    if final:
        in_specs.append(out_specs)
        args.append(arrived)
        out_specs = [whole_spec((CHUNK, REDUCED))] * 4
        out_shape = [jax.ShapeDtypeStruct((CHUNK, REDUCED), f32)]
        out_shape += [jax.ShapeDtypeStruct((CHUNK, REDUCED), bf16)] * 3
    return pl.pallas_call(
        lambda *refs: forward_kernel(final, *refs),
        grid_spec=pltpu.PrefetchScalarGridSpec(
            num_scalar_prefetch=1,
            grid=(2,),
            in_specs=in_specs,
            out_specs=out_specs,
            scratch_shapes=[pltpu.VMEM((REDUCED, COLS), bf16)] * 2,
        ),
        out_shape=out_shape,
        compiler_params=pltpu.CompilerParams(dimension_semantics=("arbitrary",)),
        cost_estimate=pl.CostEstimate(
            flops=4 * GROUP * REDUCED * COLS, bytes_accessed=4 * REDUCED * COLS, transcendentals=0
        ),
    )(place, *args)


def backward_kernel(place, rows, own, *refs):
    other, misfits, out = refs[:4], refs[4:12], refs[12]
    tangents, cotangents = refs[13:]
    step = pl.program_id(0)
    theirs = other[3][...]
    for k in range(3):
        theirs = jnp.where(step == k, other[k][...], theirs)
    here = place[4] == 0
    w_first = jnp.where(here, own[...], theirs)
    w_last = jnp.where(here, theirs, own[...])
    for c in range(8):
        span = pl.ds(c * CHUNK, CHUNK)
        picked = jnp.dot(rows[span, :], w_first, preferred_element_type=f32)
        hidden, first, second = slopes(picked[2 * TANGENTS :])
        tangents[span, :] = jnp.concatenate(per_row(picked, first) + [hidden], axis=0).astype(bf16)
        back = jnp.dot(misfits[c][...], w_last, preferred_element_type=f32)
        back = back.astype(bf16).astype(f32)
        joint = back[: 2 * TANGENTS] * picked[: 2 * TANGENTS]
        projected = jnp.concatenate(
            [
                jnp.sum(joint[:TANGENTS], axis=0, keepdims=True),
                jnp.sum(joint[TANGENTS:], axis=0, keepdims=True),
                jnp.zeros((14, BLOCK), f32),
            ],
            axis=0,
        )
        before = back[2 * TANGENTS :] * first + second * projected
        cotangents[span, :] = jnp.concatenate(per_row(back, first) + [before], axis=0).astype(bf16)
    over_rows = (((0,), (0,)), ((), ()))
    whole = jnp.concatenate([m[...] for m in misfits], axis=0)
    last = lax.dot_general(whole, tangents[...], over_rows, preferred_element_type=f32)
    first = lax.dot_general(rows[...], cotangents[...], over_rows, preferred_element_type=f32)
    out[:, 0] = first.astype(bf16).reshape(64, 8, BLOCK)
    out[:, 1] = last.astype(bf16).reshape(64, 8, BLOCK)


def backward(place, rows, misfits, weight, other):
    return pl.pallas_call(
        backward_kernel,
        grid_spec=pltpu.PrefetchScalarGridSpec(
            num_scalar_prefetch=1,
            grid=(4,),
            in_specs=[
                whole_spec((2 * GROUP, REDUCED)),
                pl.BlockSpec((REDUCED, BLOCK), lambda j, place: (0, place[j])),
                *[whole_spec((REDUCED, BLOCK))] * 4,
                *[whole_spec((CHUNK, REDUCED))] * 8,
            ],
            out_specs=pl.BlockSpec((64, 2, 8, BLOCK), lambda j, place: (0, 0, 0, place[5 + j])),
            scratch_shapes=[pltpu.VMEM((2 * GROUP, BLOCK), bf16)] * 2,
        ),
        out_shape=jax.ShapeDtypeStruct((64, 2, 8, COLS), bf16),
        compiler_params=pltpu.CompilerParams(dimension_semantics=("arbitrary",)),
        cost_estimate=pl.CostEstimate(
            flops=16 * GROUP * REDUCED * COLS, bytes_accessed=4 * REDUCED * COLS, transcendentals=0
        ),
    )(place, rows, weight, *other, *misfits)


def total_kernel(pieces, out):
    for u in range(2):
        total = pieces[0, u].astype(f32)
        for k in range(1, 16):
            total = total + pieces[k, u].astype(f32)
        out[0, :, u * COLS : (u + 1) * COLS] = total


def total_of(pieces):
    return pl.pallas_call(
        total_kernel,
        grid=(4,),
        in_specs=[pl.BlockSpec((16, 2, 8, COLS), lambda i: (0, i, 0, 0))],
        out_specs=pl.BlockSpec((1, 8, 2 * COLS), lambda i: (0, 0, i)),
        out_shape=jax.ShapeDtypeStruct((1, 8, 8 * COLS), f32),
        compiler_params=pltpu.CompilerParams(dimension_semantics=("arbitrary",)),
    )(pieces)


def shards(samples, targets, jacobian_targets, directions, plan, weights):
    at_x, at_y = lax.axis_index("x"), lax.axis_index("y")
    zl, core, zh = lax.axis_index("zl"), lax.axis_index("core"), lax.axis_index("zh")
    z = zh * 2 + zl
    kind = (at_x + 2 * at_y) % 4
    weight = weights[0]
    mine = (zl * 2 + core) * 2 + zh
    theirs = ((1 - zl) * 2 + core) * 2 + (1 - zh)
    turn = [(kind + k) % 4 for k in range(4)]
    place = jnp.stack([mine * 4 + t for t in turn] + [zh] + turn).astype(jnp.int32)

    quarter = lax.dynamic_slice_in_dim(weight, theirs * COLS + kind * BLOCK, BLOCK, 1)
    direct = z_facing(quarter)

    order = plan[0, :MICRO]
    inputs = jnp.take(samples, order, axis=0).astype(f32)
    chosen = jnp.take(directions, order, axis=0).astype(f32)
    packed = jnp.concatenate([inputs, chosen], axis=1)
    direct, packed = lax.optimization_barrier((direct, packed))
    other = [
        direct,
        ring_shift(direct, "x", 3),
        ring_shift(direct, "y", 3),
        ring_shift(direct, "x", 1),
    ]
    small = lax.all_gather(packed, ("zl", "core"))
    small = small.reshape(2, 2, 2, 2, REDUCED + TANGENTS).transpose(1, 2, 0, 3, 4)
    small = small.reshape(2, 4, 2, REDUCED + TANGENTS)
    small = jnp.where(core == 0, small, small[::-1])
    small = lax.dynamic_slice_in_dim(jnp.concatenate([small, small], axis=1), z, 4, 1)
    small = small.reshape(8, 2, REDUCED + TANGENTS)
    chosen = small[:, :, REDUCED:].reshape(8, 2 * TANGENTS).astype(jnp.int32)
    onehot = (chosen[:, :, None] == jnp.arange(REDUCED, dtype=jnp.int32)).astype(bf16)
    inputs = jnp.pad(small[:, :, :REDUCED].astype(bf16), ((0, 0), (0, 14), (0, 0)))
    rows = jnp.concatenate([onehot, inputs], axis=1).reshape(2 * GROUP, REDUCED)

    own_order = lax.dynamic_slice_in_dim(order, zh * 2, 2)
    target_rows = jnp.take(targets, own_order, axis=0).astype(f32)
    target_jac = jnp.take(jacobian_targets, own_order, axis=0).reshape(2 * TANGENTS, REDUCED)
    wanted = jnp.concatenate(
        [target_jac.astype(f32), jnp.pad(target_rows, ((0, 14), (0, 0)))], axis=0
    )

    from_core = core_swap(forward(place, rows, weight, other))
    chunks = forward(place, rows, weight, other, from_core)
    got = [z_shift(chunks[d], d) for d in (2, 1, 3)]
    total = chunks[0]
    for g in got:
        total = total + g.astype(f32)
    scale = jnp.where(jnp.arange(CHUNK)[:, None] < 2 * TANGENTS, jacobian_weight, 1.0)
    misfit = (scale * (total - wanted)).astype(bf16)
    near = [misfit, None, None, None]
    for d in (2, 1, 3):
        near[d] = z_shift(misfit, 4 - d)
    misfits = near + [core_swap(m) for m in near]
    sent = backward(place, rows, misfits, weight, other)
    pieces = lax.all_to_all(
        sent.reshape(128, 8, COLS), AXES, split_axis=0, concat_axis=0, tiled=True
    )
    return total_of(pieces.reshape(16, 8, 8, COLS))


def solution(mesh):
    torus = Mesh(mesh.devices.reshape(4, 4, 2, 2, 2), AXES)
    return jax.shard_map(
        shards,
        mesh=torus,
        in_specs=(
            P(DP, None),
            P(DP, None),
            P(DP, None, None),
            P(DP, None),
            P(DP, None),
            P("zh", None, None),
        ),
        out_specs=P("zh", DP, None),
        check_vma=False,
    )
```

time: 146 us -> 136 us (0.932)
  blocking collectives: 18.1 us -> 41.6 us
  waiting for transfers between devices: 42.4 us -> 24.4 us
  starting transfers between devices: 35 us -> 23.7 us
  other arithmetic: 9.41 us -> 5.24 us
  local copies, waits for them, and re-layouts: 11.2 us -> 8.37 us
  Pallas kernels: 29.2 us -> 31.6 us
    all_to_all x1, blocking collectives: 12.1 us -> 34.5 us  [shards(): lax.all_to_all(sent.reshape(128, 8, COLS), AXES, split_axis=0, concat_axi...]
    ppermute x12 -> x3, starting transfers between devices: 16.9 us -> 5.41 us  [ring_shift(): return lax.ppermute(block, axis, [(i, (i + d) % 4) for i in range(4)])]
    ppermute x12 -> x3, waiting for transfers between devices: 11 us -> 0.01 us  [ring_shift(): return lax.ppermute(block, axis, [(i, (i + d) % 4) for i in range(4)])]
    ppermute x1, waiting for transfers between devices: 9.8 us -> 1.35 us  [z_facing(): return lax.ppermute(block, Z, [(t, 3 - t) for t in range(4)])]
    pallas_call x2 -> x3, Pallas kernels: 13.6 us -> 16.7 us  [the longest x2 13.2 us: forward(): pl.pallas_call(lambda *refs: forward_kernel(final, *refs), grid_spec=pltp...]
    squeeze x5 -> x0, local copies, waits for them, and re-layouts: 3.01 us -> none  [the longest x4 2.09 us: piece(): return lax.dynamic_index_in_dim(chunks, i % 4, 0, keepdims=False)]
    another operation x3 -> x0, other arithmetic: 2.99 us -> none
    ppermute x6, starting transfers between devices: 6.9 us -> 8.94 us  [z_shift(): lax.ppermute(block, Z, [(z_index(z), z_index((z + d) % 4)) for z in range...]
  transfers between devices with their start and end apart: 24 -> 15, of which waited for: 14 -> 8; matrix products, arithmetic and copies ran while one was open for 8% -> 6% of each run, Pallas kernels for 5% -> 0%
where the time goes in v3:
time: 136 us; the launch traced here: 135 us
  blocking collectives  41.6 us (31%)
  Pallas kernels  31.6 us (23%)
  waiting for transfers between devices  24.4 us (18%)
  starting transfers between devices  23.7 us (17%)
  local copies, waits for them, and re-layouts  8.37 us (6%)
  other arithmetic  5.24 us (4%)
    all_to_all x1, blocking collectives, shards(): lax.all_to_all(sent.reshape(128, 8, COLS), AXES, split_axis=0, concat_axi...  34.5 us
    ppermute x6, waiting for transfers between devices, z_shift(): lax.ppermute(block, Z, [(z_index(z), z_index((z + d) % 4)) for z in range...  19.7 us
    pallas_call x1, Pallas kernels, backward(): pl.pallas_call(backward_kernel, grid_spec=pltpu.PrefetchScalarGridSpec(nu...  14.9 us
    pallas_call x2, Pallas kernels, forward(): pl.pallas_call(lambda *refs: forward_kernel(final, *refs), grid_spec=pltp...  13.2 us
    ppermute x6, starting transfers between devices, z_shift(): lax.ppermute(block, Z, [(z_index(z), z_index((z + d) % 4)) for z in range...  8.94 us
    all_gather x1, blocking collectives, shards(): small = lax.all_gather(packed, ('zl', 'core'))  7.12 us
    ppermute x3, starting transfers between devices, ring_shift(): return lax.ppermute(block, axis, [(i, (i + d) % 4) for i in range(4)])  5.41 us
    ppermute x5, starting transfers between devices, core_swap(): return lax.ppermute(block, 'core', [(0, 1), (1, 0)])  4.71 us
  transfers between devices with their start and end apart: 15, of which 8 were waited for; matrix products, arithmetic and copies ran while one was open for 6% of the time, Pallas kernels for 0%

profile of v3, /device:TPU:1, one launch (start us, length us, event | category | flops | bytes accessed | tf_op | source)
XLA Modules:
  0.0 135.2 jit_solution(3193330327704078519)
XLA Ops:
  0.0 1.1 dynamic-slice_bitcast_fusion
  1.1 4.7 %collective-permute-start = (bf16[512,256]{1,0:T(8,128)(2,1)S(1)}, bf16[512,256]{1,0:T(8,128)(2,1)S(1)}, u32[]{:S(2)}, u32[]{:S(2)}) collective-permute-start(bf16[512,256]{1,0:T(8,128)(2,1)S(1)} %dynamic-slice_bitcast_fusion), channel_id=1, source_target_pairs={{0,5},{1,4},{4,1},{5,0},{2,7},{3,6},{6,3},{7,2},{8,13},{9,12},{12,... | collective-permute-start | bytes 786440 | tf_op jit(solution)/shard_map/ppermute | solution.py:34
  5.7 0.7 compare_and_fusion.1
  6.4 0.7 fusion.8
  7.0 1.2 gather_fusion.1
  8.3 1.3 gather_fusion
  9.6 0.7 stack.39.refs_0_.place
  10.4 1.4 %collective-permute-done.refs_6_.refs_0_ = bf16[512,256]{1,0:T(8,128)(2,1)S(1)} collective-permute-done((bf16[512,256]{1,0:T(8,128)(2,1)S(1)}, bf16[512,256]{1,0:T(8,128)(2,1)S(1)}, u32[]{:S(2)}, u32[]{:S(2)}) %collective-permute-start) | collective-permute-done | bytes 262176 | tf_op jit(solution)/shard_map/ppermute | solution.py:34
  11.7 1.2 collective-permute-start.3
  12.9 2.7 %collective-permute-start.2 = (bf16[512,256]{1,0:T(8,128)(2,1)S(1)}, bf16[512,256]{1,0:T(8,128)(2,1)S(1)}, u32[]{:S(2)}, u32[]{:S(2)}) collective-permute-start(bf16[512,256]{1,0:T(8,128)(2,1)S(1)} %collective-permute-done.refs_6_.refs_0_), channel_id=1, source_target_pairs={{0,24},{8,0},{16,8},{24,16},{1,25},{9,1},{17,9},{25,17},{2,26},{10... | collective-permute-start | bytes 786440 | tf_op jit(solution)/shard_map/ppermute | solution.py:38
  15.7 1.5 %collective-permute-start.1 = (bf16[512,256]{1,0:T(8,128)(2,1)S(1)}, bf16[512,256]{1,0:T(8,128)(2,1)S(1)}, u32[]{:S(2)}, u32[]{:S(2)}) collective-permute-start(bf16[512,256]{1,0:T(8,128)(2,1)S(1)} %collective-permute-done.refs_6_.refs_0_), channel_id=1, source_target_pairs={{0,96},{32,0},{64,32},{96,64},{1,97},{33,1},{65,33},{97,65},{2,98}... | collective-permute-start | bytes 786440 | tf_op jit(solution)/shard_map/ppermute | solution.py:38
  17.1 7.1 %all-gather.1 = f32[4,4,640]{2,1,0:T(4,128)S(1)} all-gather(f32[1,4,640]{2,1,0:T(4,128)S(1)} %bitcast.59), channel_id=2, replica_groups=mesh['x'=4,'y'=4,'zl'=2,'core'=2,'zh'=2] {'zl','core'}, dimensions={0}, use_global_device_ids=true | all-gather | bytes 51200 | tf_op jit(solution)/shard_map/all_gather | solution.py:239
  24.4 0.5 fusion.1
  25.0 1.6 %fusion.2 = bf16[8,272,512]{2,1,0:T(8,128)(2,1)} fusion(bf16[8,2,512]{2,1,0:T(2,128)(2,1)S(1)} %slice.29, bf16[8,256,512]{2,1,0:T(8,128)(2,1)S(1)} %fusion.1), kind=kLoop, calls=%fused_computation.8 | loop fusion | flops 6684672 | bytes 4341760 | tf_op jit(solution)/shard_map/concatenate | solution.py:248
  26.6 0.6 copy-done.3
  27.2 0.1 copy-done.4
  27.4 0.1 copy-done.5
  27.5 6.4 %shard_map.64 = bf16[1088,512]{1,0:T(8,128)(2,1)} custom-call(s32[9]{0:T(128)} %stack.39.refs_0_.place, bf16[2176,512]{1,0:T(8,128)(2,1)} %bitcast.51, bf16[512,8192]{1,0:T(8,128)(2,1)} %bitcast.42, bf16[512,8192]{1,0:T(8,128)(2,1)} %bitcast.43, bf16[512,8192]{1,0:T(8,128)(2,1)} %bitcast.44, bf16[512,8192]{1,0:T(8,128)(2,1)} %bitcast.45, ...), custom_call_target="tpu_custom_call" | custom-call | flops 2281701376 | bytes 2097152 | tf_op jit(solution)/shard_map/pallas_call | solution.py:119
  33.8 0.2 collective-permute-start.4
  34.1 0.6 gather_fusion.3
  34.7 0.1 compare_and_fusion
  34.9 1.9 %collective-permute-done.4.refs_10_ = bf16[1088,512]{1,0:T(8,128)(2,1)S(1)} collective-permute-done((bf16[1088,512]{1,0:T(8,128)(2,1)}, bf16[1088,512]{1,0:T(8,128)(2,1)S(1)}, u32[]{:S(2)}, u32[]{:S(2)}) %collective-permute-start.4) | collective-permute-done | bytes 1114144 | tf_op jit(solution)/shard_map/ppermute | solution.py:42
  36.8 1.0 copy-done.1
  37.8 6.8 %shard_map.65 = (f32[272,512]{1,0:T(8,128)}, bf16[272,512]{1,0:T(8,128)(2,1)}, bf16[272,512]{1,0:T(8,128)(2,1)}, bf16[272,512]{1,0:T(8,128)(2,1)}) custom-call(s32[9]{0:T(128)} %stack.39.refs_0_.place, bf16[2176,512]{1,0:T(8,128)(2,1)} %bitcast.52, bf16[512,8192]{1,0:T(8,128)(2,1)} %bitcast.46, bf16[512,8192]{1,0:T(8,128)(2,1)} %bitcast.47, ...), custom_call_target="tpu_custom_call" | custom-call | flops 2281701376 | bytes 2097152 | tf_op jit(solution)/shard_map/pallas_call | solution.py:119
  44.6 2.2 %collective-permute-start.5 = (bf16[272,512]{1,0:T(8,128)(2,1)}, bf16[272,512]{1,0:T(8,128)(2,1)S(1)}, u32[]{:S(2)}, u32[]{:S(2)}) collective-permute-start(bf16[272,512]{1,0:T(8,128)(2,1)} %get-tuple-element.14), channel_id=1, source_target_pairs={{0,1},{4,5},{1,0},{5,4},{2,3},{6,7},{3,2},{7,6},{8,9},{12,13},{9,8... | collective-permute-start | bytes 835592 | tf_op jit(solution)/shard_map/ppermute | solution.py:30
  46.8 1.1 collective-permute-start.6
  47.9 1.6 %collective-permute-start.7 = (bf16[272,512]{1,0:T(8,128)(2,1)}, bf16[272,512]{1,0:T(8,128)(2,1)S(1)}, u32[]{:S(2)}, u32[]{:S(2)}) collective-permute-start(bf16[272,512]{1,0:T(8,128)(2,1)} %get-tuple-element.16), channel_id=1, source_target_pairs={{0,5},{4,0},{1,4},{5,1},{2,7},{6,2},{3,6},{7,3},{8,13},{12,8},{9,1... | collective-permute-start | bytes 835592 | tf_op jit(solution)/shard_map/ppermute | solution.py:30
  49.5 0.6 gather_fusion.2
  50.1 0.1 bitcast_select_fusion
  50.2 4.3 %collective-permute-done.5 = bf16[272,512]{1,0:T(8,128)(2,1)S(1)} collective-permute-done((bf16[272,512]{1,0:T(8,128)(2,1)}, bf16[272,512]{1,0:T(8,128)(2,1)S(1)}, u32[]{:S(2)}, u32[]{:S(2)}) %collective-permute-start.5) | collective-permute-done | bytes 278560 | tf_op jit(solution)/shard_map/ppermute | solution.py:30
  54.4 6.5 %collective-permute-done.6 = bf16[272,512]{1,0:T(8,128)(2,1)S(1)} collective-permute-done((bf16[272,512]{1,0:T(8,128)(2,1)}, bf16[272,512]{1,0:T(8,128)(2,1)S(1)}, u32[]{:S(2)}, u32[]{:S(2)}) %collective-permute-start.6) | collective-permute-done | bytes 278560 | tf_op jit(solution)/shard_map/ppermute | solution.py:30
  60.9 1.2 multiply_convert_fusion.refs_4_
  62.2 0.3 collective-permute-start.10
  62.5 3.6 %collective-permute-start.9 = (bf16[272,512]{1,0:T(8,128)(2,1)S(1)}, bf16[272,512]{1,0:T(8,128)(2,1)S(1)}, u32[]{:S(2)}, u32[]{:S(2)}) collective-permute-start(bf16[272,512]{1,0:T(8,128)(2,1)S(1)} %multiply_convert_fusion.refs_4_), channel_id=1, source_target_pairs={{0,1},{4,5},{1,0},{5,4},{2,3},{6,7},{3,2},{7,6},{8,9},{12,13},{9,8... | collective-permute-start | bytes 835592 | tf_op jit(solution)/shard_map/ppermute | solution.py:30
  66.1 0.2 collective-permute-start.8
  66.2 1.4 %collective-permute-start.11 = (bf16[272,512]{1,0:T(8,128)(2,1)S(1)}, bf16[272,512]{1,0:T(8,128)(2,1)S(1)}, u32[]{:S(2)}, u32[]{:S(2)}) collective-permute-start(bf16[272,512]{1,0:T(8,128)(2,1)S(1)} %multiply_convert_fusion.refs_4_), channel_id=1, source_target_pairs={{0,2},{2,0},{1,3},{3,1},{4,6},{6,4},{5,7},{7,5},{8,10},{10,8},{9,1... | collective-permute-start | bytes 835592 | tf_op jit(solution)/shard_map/ppermute | solution.py:42
  67.7 3.2 %collective-permute-done.10.refs_7_ = bf16[272,512]{1,0:T(8,128)(2,1)S(1)} collective-permute-done((bf16[272,512]{1,0:T(8,128)(2,1)S(1)}, bf16[272,512]{1,0:T(8,128)(2,1)S(1)}, u32[]{:S(2)}, u32[]{:S(2)}) %collective-permute-start.10) | collective-permute-done | bytes 278560 | tf_op jit(solution)/shard_map/ppermute | solution.py:30
  70.9 1.7 %collective-permute-start.14 = (bf16[272,512]{1,0:T(8,128)(2,1)S(1)}, bf16[272,512]{1,0:T(8,128)(2,1)S(1)}, u32[]{:S(2)}, u32[]{:S(2)}) collective-permute-start(bf16[272,512]{1,0:T(8,128)(2,1)S(1)} %collective-permute-done.10.refs_7_), channel_id=1, source_target_pairs={{0,2},{2,0},{1,3},{3,1},{4,6},{6,4},{5,7},{7,5},{8,10},{10,8},{9,1... | collective-permute-start | bytes 835592 | tf_op jit(solution)/shard_map/ppermute | solution.py:42
  72.5 5.8 %collective-permute-done.9.refs_6_ = bf16[272,512]{1,0:T(8,128)(2,1)S(1)} collective-permute-done((bf16[272,512]{1,0:T(8,128)(2,1)S(1)}, bf16[272,512]{1,0:T(8,128)(2,1)S(1)}, u32[]{:S(2)}, u32[]{:S(2)}) %collective-permute-start.9) | collective-permute-done | bytes 278560 | tf_op jit(solution)/shard_map/ppermute | solution.py:30
  78.3 1.3 collective-permute-start.13
  79.6 0.1 collective-permute-start.12
  79.8 1.1 collective-permute-done.13.refs_10_
  80.8 0.4 collective-permute-done.12.refs_9_
  81.3 0.3 copy-done.13
  81.5 0.7 copy-done.14
  82.2 14.9 %shard_map.66 = bf16[64,2,8,1024]{3,2,1,0:T(8,128)(2,1)} custom-call(s32[9]{0:T(128)} %stack.39.refs_0_.place, bf16[2176,512]{1,0:T(8,128)(2,1)} %bitcast.53, bf16[512,8192]{1,0:T(8,128)(2,1)} %bitcast.50, bf16[512,256]{1,0:T(8,128)(2,1)} %copy-done.2, bf16[512,256]{1,0:T(8,128)(2,1)} %copy-done.5, bf16[512,256]{1,0:T(8,128)(2,1)} %copy-done.4, ...), custom_call_target="tpu_custom_call" | custom-call | flops 9126805504 | bytes 2097152 | tf_op jit(solution)/shard_map/pallas_call | solution.py:173
  97.1 34.5 %all_to_all.5 = bf16[128,8,1024]{2,1,0:T(8,128)(2,1)} all-to-all(bf16[128,8,1024]{2,1,0:T(8,128)(2,1)} %bitcast.55), channel_id=1, replica_groups=mesh['x'=4,'y'=4,'zl'=2,'core'=2,'zh'=2] {'x','y','zl','core','zh'}, dimensions={0} | all-to-all | bytes 4194304 | tf_op jit(solution)/shard_map/all_to_all | solution.py:270
  131.6 3.5 %shard_map.67 = f32[1,8,8192]{2,1,0:T(8,128)} custom-call(bf16[16,8,8,1024]{3,2,1,0:T(8,128)(2,1)} %bitcast.54), custom_call_target="tpu_custom_call" | custom-call | tf_op jit(solution)/shard_map/pallas_call | solution.py:204
  (49 shorter events, 0.6 us)
Async XLA Ops:
  0.0 49.5 %copy-start = (bf16[8,128,512]{2,1,0:T(8,128)(2,1)S(1)}, bf16[8,128,512]{2,1,0:T(8,128)(2,1)}, u32[]{:S(2)}) copy-start(bf16[8,128,512]{2,1,0:T(8,128)(2,1)} %param.8) | copy-start | bytes 3145732
  1.1 10.7 %collective-permute-start = (bf16[512,256]{1,0:T(8,128)(2,1)S(1)}, bf16[512,256]{1,0:T(8,128)(2,1)S(1)}, u32[]{:S(2)}, u32[]{:S(2)}) collective-permute-start(bf16[512,256]{1,0:T(8,128)(2,1)S(1)} %dynamic-slice_bitcast_fusion), channel_id=1, source_target_pairs={{0,5},{1,4},{4,1},{5,0},{2,7},{3,6},{6,3},{7,2},{8,13},{9,12},{12,... | collective-permute-start | bytes 786440 | tf_op jit(solution)/shard_map/ppermute | solution.py:34
  11.7 14.8 %copy-start.2 = (bf16[512,256]{1,0:T(8,128)(2,1)}, bf16[512,256]{1,0:T(8,128)(2,1)S(1)}, u32[]{:S(2)}) copy-start(bf16[512,256]{1,0:T(8,128)(2,1)S(1)} %collective-permute-done.refs_6_.refs_0_) | copy-start | bytes 786436
  11.7 14.8 %collective-permute-start.3 = (bf16[512,256]{1,0:T(8,128)(2,1)S(1)}, bf16[512,256]{1,0:T(8,128)(2,1)S(1)}, u32[]{:S(2)}, u32[]{:S(2)}) collective-permute-start(bf16[512,256]{1,0:T(8,128)(2,1)S(1)} %collective-permute-done.refs_6_.refs_0_), channel_id=1, source_target_pairs={{0,32},{32,64},{64,96},{96,0},{1,33},{33,65},{65,97},{97,1},{2,34}... | collective-permute-start | bytes 786440 | tf_op jit(solution)/shard_map/ppermute | solution.py:38
  12.9 13.6 %collective-permute-start.2 = (bf16[512,256]{1,0:T(8,128)(2,1)S(1)}, bf16[512,256]{1,0:T(8,128)(2,1)S(1)}, u32[]{:S(2)}, u32[]{:S(2)}) collective-permute-start(bf16[512,256]{1,0:T(8,128)(2,1)S(1)} %collective-permute-done.refs_6_.refs_0_), channel_id=1, source_target_pairs={{0,24},{8,0},{16,8},{24,16},{1,25},{9,1},{17,9},{25,17},{2,26},{10... | collective-permute-start | bytes 786440 | tf_op jit(solution)/shard_map/ppermute | solution.py:38
  15.7 10.9 %collective-permute-start.1 = (bf16[512,256]{1,0:T(8,128)(2,1)S(1)}, bf16[512,256]{1,0:T(8,128)(2,1)S(1)}, u32[]{:S(2)}, u32[]{:S(2)}) collective-permute-start(bf16[512,256]{1,0:T(8,128)(2,1)S(1)} %collective-permute-done.refs_6_.refs_0_), channel_id=1, source_target_pairs={{0,96},{32,0},{64,32},{96,64},{1,97},{33,1},{65,33},{97,65},{2,98}... | collective-permute-start | bytes 786440 | tf_op jit(solution)/shard_map/ppermute | solution.py:38
  26.6 0.7 copy-start.3
  26.6 0.8 copy-start.4
  26.6 0.9 copy-start.5
  27.4 6.6 %copy-start.15 = (s32[1,8]{1,0:T(1,128)S(1)}, s32[1,8]{1,0:T(1,128)}, u32[]{:S(2)}) copy-start(s32[1,8]{1,0:T(1,128)} %param.10) | copy-start | bytes 100
  27.5 6.7 %copy-start.7 = (bf16[8,512]{1,0:T(8,128)(2,1)S(1)}, bf16[8,512]{1,0:T(8,128)(2,1)}, u32[]{:S(2)}) copy-start(bf16[8,512]{1,0:T(8,128)(2,1)} %param.7) | copy-start | bytes 24580
  33.8 3.0 %collective-permute-start.4 = (bf16[1088,512]{1,0:T(8,128)(2,1)}, bf16[1088,512]{1,0:T(8,128)(2,1)S(1)}, u32[]{:S(2)}, u32[]{:S(2)}) collective-permute-start(bf16[1088,512]{1,0:T(8,128)(2,1)} %shard_map.64), channel_id=1, source_target_pairs={{0,2},{2,0},{1,3},{3,1},{4,6},{6,4},{5,7},{7,5},{8,10},{10,8},{9,1... | collective-permute-start | bytes 3342344 | tf_op jit(solution)/shard_map/ppermute | solution.py:42
  36.8 1.0 copy-start.1
  44.6 9.8 %collective-permute-start.5 = (bf16[272,512]{1,0:T(8,128)(2,1)}, bf16[272,512]{1,0:T(8,128)(2,1)S(1)}, u32[]{:S(2)}, u32[]{:S(2)}) collective-permute-start(bf16[272,512]{1,0:T(8,128)(2,1)} %get-tuple-element.14), channel_id=1, source_target_pairs={{0,1},{4,5},{1,0},{5,4},{2,3},{6,7},{3,2},{7,6},{8,9},{12,13},{9,8... | collective-permute-start | bytes 835592 | tf_op jit(solution)/shard_map/ppermute | solution.py:30
  46.8 14.1 %collective-permute-start.6 = (bf16[272,512]{1,0:T(8,128)(2,1)}, bf16[272,512]{1,0:T(8,128)(2,1)S(1)}, u32[]{:S(2)}, u32[]{:S(2)}) collective-permute-start(bf16[272,512]{1,0:T(8,128)(2,1)} %get-tuple-element.15), channel_id=1, source_target_pairs={{0,4},{4,1},{1,5},{5,0},{2,6},{6,3},{3,7},{7,2},{8,12},{12,9},{9,1... | collective-permute-start | bytes 835592 | tf_op jit(solution)/shard_map/ppermute | solution.py:30
  47.9 13.0 %collective-permute-start.7 = (bf16[272,512]{1,0:T(8,128)(2,1)}, bf16[272,512]{1,0:T(8,128)(2,1)S(1)}, u32[]{:S(2)}, u32[]{:S(2)}) collective-permute-start(bf16[272,512]{1,0:T(8,128)(2,1)} %get-tuple-element.16), channel_id=1, source_target_pairs={{0,5},{4,0},{1,4},{5,1},{2,7},{6,2},{3,6},{7,3},{8,13},{12,8},{9,1... | collective-permute-start | bytes 835592 | tf_op jit(solution)/shard_map/ppermute | solution.py:30
  62.1 19.1 %copy-start.6 = (bf16[272,512]{1,0:T(8,128)(2,1)}, bf16[272,512]{1,0:T(8,128)(2,1)S(1)}, u32[]{:S(2)}) copy-start(bf16[272,512]{1,0:T(8,128)(2,1)S(1)} %multiply_convert_fusion.refs_4_) | copy-start | bytes 835588
  62.2 8.7 %collective-permute-start.10 = (bf16[272,512]{1,0:T(8,128)(2,1)S(1)}, bf16[272,512]{1,0:T(8,128)(2,1)S(1)}, u32[]{:S(2)}, u32[]{:S(2)}) collective-permute-start(bf16[272,512]{1,0:T(8,128)(2,1)S(1)} %multiply_convert_fusion.refs_4_), channel_id=1, source_target_pairs={{0,4},{4,1},{1,5},{5,0},{2,6},{6,3},{3,7},{7,2},{8,12},{12,9},{9,1... | collective-permute-start | bytes 835592 | tf_op jit(solution)/shard_map/ppermute | solution.py:30
  62.5 15.8 %collective-permute-start.9 = (bf16[272,512]{1,0:T(8,128)(2,1)S(1)}, bf16[272,512]{1,0:T(8,128)(2,1)S(1)}, u32[]{:S(2)}, u32[]{:S(2)}) collective-permute-start(bf16[272,512]{1,0:T(8,128)(2,1)S(1)} %multiply_convert_fusion.refs_4_), channel_id=1, source_target_pairs={{0,1},{4,5},{1,0},{5,4},{2,3},{6,7},{3,2},{7,6},{8,9},{12,13},{9,8... | collective-permute-start | bytes 835592 | tf_op jit(solution)/shard_map/ppermute | solution.py:30
  66.1 13.6 %collective-permute-start.8 = (bf16[272,512]{1,0:T(8,128)(2,1)S(1)}, bf16[272,512]{1,0:T(8,128)(2,1)S(1)}, u32[]{:S(2)}, u32[]{:S(2)}) collective-permute-start(bf16[272,512]{1,0:T(8,128)(2,1)S(1)} %multiply_convert_fusion.refs_4_), channel_id=1, source_target_pairs={{0,5},{4,0},{1,4},{5,1},{2,7},{6,2},{3,6},{7,3},{8,13},{12,8},{9,1... | collective-permute-start | bytes 835592 | tf_op jit(solution)/shard_map/ppermute | solution.py:30
  66.2 13.5 %collective-permute-start.11 = (bf16[272,512]{1,0:T(8,128)(2,1)S(1)}, bf16[272,512]{1,0:T(8,128)(2,1)S(1)}, u32[]{:S(2)}, u32[]{:S(2)}) collective-permute-start(bf16[272,512]{1,0:T(8,128)(2,1)S(1)} %multiply_convert_fusion.refs_4_), channel_id=1, source_target_pairs={{0,2},{2,0},{1,3},{3,1},{4,6},{6,4},{5,7},{7,5},{8,10},{10,8},{9,1... | collective-permute-start | bytes 835592 | tf_op jit(solution)/shard_map/ppermute | solution.py:42
  70.9 10.4 %copy-start.8 = (bf16[272,512]{1,0:T(8,128)(2,1)}, bf16[272,512]{1,0:T(8,128)(2,1)S(1)}, u32[]{:S(2)}) copy-start(bf16[272,512]{1,0:T(8,128)(2,1)S(1)} %collective-permute-done.10.refs_7_) | copy-start | bytes 835588
  70.9 8.9 %collective-permute-start.14 = (bf16[272,512]{1,0:T(8,128)(2,1)S(1)}, bf16[272,512]{1,0:T(8,128)(2,1)S(1)}, u32[]{:S(2)}, u32[]{:S(2)}) collective-permute-start(bf16[272,512]{1,0:T(8,128)(2,1)S(1)} %collective-permute-done.10.refs_7_), channel_id=1, source_target_pairs={{0,2},{2,0},{1,3},{3,1},{4,6},{6,4},{5,7},{7,5},{8,10},{10,8},{9,1... | collective-permute-start | bytes 835592 | tf_op jit(solution)/shard_map/ppermute | solution.py:42
  78.3 2.9 %copy-start.9 = (bf16[272,512]{1,0:T(8,128)(2,1)}, bf16[272,512]{1,0:T(8,128)(2,1)S(1)}, u32[]{:S(2)}) copy-start(bf16[272,512]{1,0:T(8,128)(2,1)S(1)} %collective-permute-done.9.refs_6_) | copy-start | bytes 835588
  78.3 2.5 %collective-permute-start.13 = (bf16[272,512]{1,0:T(8,128)(2,1)S(1)}, bf16[272,512]{1,0:T(8,128)(2,1)S(1)}, u32[]{:S(2)}, u32[]{:S(2)}) collective-permute-start(bf16[272,512]{1,0:T(8,128)(2,1)S(1)} %collective-permute-done.9.refs_6_), channel_id=1, source_target_pairs={{0,2},{2,0},{1,3},{3,1},{4,6},{6,4},{5,7},{7,5},{8,10},{10,8},{9,1... | collective-permute-start | bytes 835592 | tf_op jit(solution)/shard_map/ppermute | solution.py:42
  79.6 1.6 %copy-start.10 = (bf16[272,512]{1,0:T(8,128)(2,1)}, bf16[272,512]{1,0:T(8,128)(2,1)S(1)}, u32[]{:S(2)}) copy-start(bf16[272,512]{1,0:T(8,128)(2,1)S(1)} %collective-permute-done.8.refs_5_) | copy-start | bytes 835588
  79.6 1.6 %collective-permute-start.12 = (bf16[272,512]{1,0:T(8,128)(2,1)S(1)}, bf16[272,512]{1,0:T(8,128)(2,1)S(1)}, u32[]{:S(2)}, u32[]{:S(2)}) collective-permute-start(bf16[272,512]{1,0:T(8,128)(2,1)S(1)} %collective-permute-done.8.refs_5_), channel_id=1, source_target_pairs={{0,2},{2,0},{1,3},{3,1},{4,6},{6,4},{5,7},{7,5},{8,10},{10,8},{9,1... | collective-permute-start | bytes 835592 | tf_op jit(solution)/shard_map/ppermute | solution.py:42
  79.7 1.5 %copy-start.11 = (bf16[272,512]{1,0:T(8,128)(2,1)}, bf16[272,512]{1,0:T(8,128)(2,1)S(1)}, u32[]{:S(2)}) copy-start(bf16[272,512]{1,0:T(8,128)(2,1)S(1)} %collective-permute-done.11.refs_8_) | copy-start | bytes 835588
  79.8 1.5 %copy-start.12 = (bf16[272,512]{1,0:T(8,128)(2,1)}, bf16[272,512]{1,0:T(8,128)(2,1)S(1)}, u32[]{:S(2)}) copy-start(bf16[272,512]{1,0:T(8,128)(2,1)S(1)} %collective-permute-done.14.refs_11_) | copy-start | bytes 835588
  80.8 0.7 copy-start.13
  81.5 0.7 copy-start.14

commit v4 on v3

--- a/solution.py
+++ b/solution.py
@@ -17,6 +17,7 @@
 CHUNK = 2 * TANGENTS + 16
 GROUP = 4 * CHUNK
 STEP = 2 * CHUNK
+PARTS = (TANGENTS, TANGENTS + 16)
 jacobian_weight = 32.0
 f32 = jnp.float32
 bf16 = jnp.bfloat16
@@ -90,16 +91,16 @@
         outs[0][...] = total.astype(bf16)
         return
     total = total + arrived[...].astype(f32)
-
-    @pl.when(pl.program_id(0) == 0)
-    def _():
-        outs[0][...] = total[:CHUNK]
-        outs[1][...] = total[CHUNK:].astype(bf16)
-
-    @pl.when(pl.program_id(0) == 1)
-    def _():
-        outs[2][...] = total[:CHUNK].astype(bf16)
-        outs[3][...] = total[CHUNK:].astype(bf16)
+    for step in range(2):
+
+        @pl.when(pl.program_id(0) == step)
+        def _():
+            for c in range(2):
+                at = c * CHUNK
+                for part in PARTS:
+                    out = outs[2 * (2 * step + c) + (part > TANGENTS)]
+                    out[...] = total[at : at + part].astype(out.dtype)
+                    at += part
 
 
 def forward(place, rows, weight, other, arrived=None):
@@ -113,9 +114,9 @@
     if final:
         in_specs.append(out_specs)
         args.append(arrived)
-        out_specs = [whole_spec((CHUNK, REDUCED))] * 4
-        out_shape = [jax.ShapeDtypeStruct((CHUNK, REDUCED), f32)]
-        out_shape += [jax.ShapeDtypeStruct((CHUNK, REDUCED), bf16)] * 3
+        out_specs = [whole_spec((part, REDUCED)) for part in PARTS] * 4
+        out_shape = [jax.ShapeDtypeStruct((part, REDUCED), f32) for part in PARTS]
+        out_shape += [jax.ShapeDtypeStruct((part, REDUCED), bf16) for part in PARTS] * 3
     return pl.pallas_call(
         lambda *refs: forward_kernel(final, *refs),
         grid_spec=pltpu.PrefetchScalarGridSpec(
@@ -134,8 +135,9 @@
 
 
 def backward_kernel(place, rows, own, *refs):
-    other, misfits, out = refs[:4], refs[4:12], refs[12]
-    tangents, cotangents = refs[13:]
+    other, misfits, out = refs[:4], refs[4:20], refs[20]
+    tangents, cotangents = refs[21:]
+    whole = jnp.concatenate([m[...] for m in misfits], axis=0)
     step = pl.program_id(0)
     theirs = other[3][...]
     for k in range(3):
@@ -148,7 +150,8 @@
         picked = jnp.dot(rows[span, :], w_first, preferred_element_type=f32)
         hidden, first, second = slopes(picked[2 * TANGENTS :])
         tangents[span, :] = jnp.concatenate(per_row(picked, first) + [hidden], axis=0).astype(bf16)
-        back = jnp.dot(misfits[c][...], w_last, preferred_element_type=f32)
+        misfit = jnp.concatenate([misfits[2 * c][...], misfits[2 * c + 1][...]], axis=0)
+        back = jnp.dot(misfit, w_last, preferred_element_type=f32)
         back = back.astype(bf16).astype(f32)
         joint = back[: 2 * TANGENTS] * picked[: 2 * TANGENTS]
         projected = jnp.concatenate(
@@ -162,7 +165,6 @@
         before = back[2 * TANGENTS :] * first + second * projected
         cotangents[span, :] = jnp.concatenate(per_row(back, first) + [before], axis=0).astype(bf16)
     over_rows = (((0,), (0,)), ((), ()))
-    whole = jnp.concatenate([m[...] for m in misfits], axis=0)
     last = lax.dot_general(whole, tangents[...], over_rows, preferred_element_type=f32)
     first = lax.dot_general(rows[...], cotangents[...], over_rows, preferred_element_type=f32)
     out[:, 0] = first.astype(bf16).reshape(64, 8, BLOCK)
@@ -179,7 +181,7 @@
                 whole_spec((2 * GROUP, REDUCED)),
                 pl.BlockSpec((REDUCED, BLOCK), lambda j, place: (0, place[j])),
                 *[whole_spec((REDUCED, BLOCK))] * 4,
-                *[whole_spec((CHUNK, REDUCED))] * 8,
+                *[whole_spec((part, REDUCED)) for part in PARTS] * 8,
             ],
             out_specs=pl.BlockSpec((64, 2, 8, BLOCK), lambda j, place: (0, 0, 0, place[5 + j])),
             scratch_shapes=[pltpu.VMEM((2 * GROUP, BLOCK), bf16)] * 2,
@@ -229,17 +231,19 @@
     inputs = jnp.take(samples, order, axis=0).astype(f32)
     chosen = jnp.take(directions, order, axis=0).astype(f32)
     packed = jnp.concatenate([inputs, chosen], axis=1)
-    direct, packed = lax.optimization_barrier((direct, packed))
+    swapped = core_swap(packed)
+    direct, packed, swapped = lax.optimization_barrier((direct, packed, swapped))
     other = [
         direct,
         ring_shift(direct, "x", 3),
         ring_shift(direct, "y", 3),
         ring_shift(direct, "x", 1),
     ]
-    small = lax.all_gather(packed, ("zl", "core"))
-    small = small.reshape(2, 2, 2, 2, REDUCED + TANGENTS).transpose(1, 2, 0, 3, 4)
-    small = small.reshape(2, 4, 2, REDUCED + TANGENTS)
-    small = jnp.where(core == 0, small, small[::-1])
+    pair = jnp.concatenate([packed, swapped], axis=0)
+    beside = lax.ppermute(pair, "zl", [(0, 1), (1, 0)])
+    low = jnp.where(zl == 0, pair, beside).reshape(2, 2, 2, REDUCED + TANGENTS)
+    high = jnp.where(zl == 0, beside, pair).reshape(2, 2, 2, REDUCED + TANGENTS)
+    small = jnp.stack([low, high], axis=2).reshape(2, 4, 2, REDUCED + TANGENTS)
     small = lax.dynamic_slice_in_dim(jnp.concatenate([small, small], axis=1), z, 4, 1)
     small = small.reshape(8, 2, REDUCED + TANGENTS)
     chosen = small[:, :, REDUCED:].reshape(8, 2 * TANGENTS).astype(jnp.int32)
@@ -250,21 +254,28 @@
     own_order = lax.dynamic_slice_in_dim(order, zh * 2, 2)
     target_rows = jnp.take(targets, own_order, axis=0).astype(f32)
     target_jac = jnp.take(jacobian_targets, own_order, axis=0).reshape(2 * TANGENTS, REDUCED)
-    wanted = jnp.concatenate(
-        [target_jac.astype(f32), jnp.pad(target_rows, ((0, 14), (0, 0)))], axis=0
-    )
+    wanted = [
+        target_jac[:TANGENTS].astype(f32),
+        jnp.concatenate(
+            [target_jac[TANGENTS:].astype(f32), jnp.pad(target_rows, ((0, 14), (0, 0)))], axis=0
+        ),
+    ]
 
     from_core = core_swap(forward(place, rows, weight, other))
-    chunks = forward(place, rows, weight, other, from_core)
-    got = [z_shift(chunks[d], d) for d in (2, 1, 3)]
-    total = chunks[0]
-    for g in got:
-        total = total + g.astype(f32)
-    scale = jnp.where(jnp.arange(CHUNK)[:, None] < 2 * TANGENTS, jacobian_weight, 1.0)
-    misfit = (scale * (total - wanted)).astype(bf16)
-    near = [misfit, None, None, None]
-    for d in (2, 1, 3):
-        near[d] = z_shift(misfit, 4 - d)
+    from_core, wanted = lax.optimization_barrier((from_core, wanted))
+    parts = forward(place, rows, weight, other, from_core)
+    got = [[z_shift(parts[2 * d + p], d) for d in (2, 1, 3)] for p in range(2)]
+    near = [[], []]
+    for p in range(2):
+        total = parts[p]
+        for g in got[p]:
+            total = total + g.astype(f32)
+        scale = jnp.where(jnp.arange(PARTS[p])[:, None] < TANGENTS, jacobian_weight, 1.0)
+        misfit = (scale * (total - wanted[p])).astype(bf16)
+        near[p] = [misfit, None, None, None]
+        for d in (2, 1, 3):
+            near[p][d] = z_shift(misfit, 4 - d)
+    near = [near[p][d] for d in range(4) for p in range(2)]
     misfits = near + [core_swap(m) for m in near]
     sent = backward(place, rows, misfits, weight, other)
     pieces = lax.all_to_all(

time: 136 us -> 134 us (0.985)
  starting transfers between devices: 23.7 us -> 39.2 us
  waiting for transfers between devices: 24.4 us -> 12.2 us
  blocking collectives: 41.6 us -> 35.9 us
    ppermute x6 -> x12, waiting for transfers between devices: 19.7 us -> 6.78 us  [z_shift(): lax.ppermute(block, Z, [(z_index(z), z_index((z + d) % 4)) for z in range...]
    ppermute x6 -> x12, starting transfers between devices: 8.94 us -> 17.3 us  [z_shift(): lax.ppermute(block, Z, [(z_index(z), z_index((z + d) % 4)) for z in range...]
    all_gather x1 -> x0, blocking collectives: 7.12 us -> none  [shards(): small = lax.all_gather(packed, ('zl', 'core'))]
    ppermute x5 -> x10, starting transfers between devices: 4.71 us -> 11.7 us  [core_swap(): return lax.ppermute(block, 'core', [(0, 1), (1, 0)])]
    ppermute x3, waiting for transfers between devices: 0.01 us -> 2.27 us  [ring_shift(): return lax.ppermute(block, axis, [(i, (i + d) % 4) for i in range(4)])]
    all_to_all x1, blocking collectives: 34.5 us -> 35.9 us  [shards(): lax.all_to_all(sent.reshape(128, 8, COLS), AXES, split_axis=0, concat_axi...]
    ppermute x5 -> x10, waiting for transfers between devices: 3.38 us -> 2.95 us  [core_swap(): return lax.ppermute(block, 'core', [(0, 1), (1, 0)])]
    unnamed x33 -> x49, local copies, waits for them, and re-layouts: 2.9 us -> 3.03 us
  transfers between devices with their start and end apart: 15 -> 27, of which waited for: 8 -> 13; matrix products, arithmetic and copies ran while one was open for 6% -> 8% of each run, Pallas kernels for 0% -> 0%
where the time goes in v4:
time: 134 us
  starting transfers between devices  39.2 us (29%)
  blocking collectives  35.9 us (27%)
  Pallas kernels  31.6 us (24%)
  waiting for transfers between devices  12.2 us (9%)
  local copies, waits for them, and re-layouts  8.38 us (6%)
  other arithmetic  6.18 us (5%)
    all_to_all x1, blocking collectives, shards(): lax.all_to_all(sent.reshape(128, 8, COLS), AXES, split_axis=0, concat_axi...  35.9 us
    ppermute x12, starting transfers between devices, z_shift(): lax.ppermute(block, Z, [(z_index(z), z_index((z + d) % 4)) for z in range...  17.3 us
    pallas_call x1, Pallas kernels, backward(): pl.pallas_call(backward_kernel, grid_spec=pltpu.PrefetchScalarGridSpec(nu...  14.9 us
    pallas_call x2, Pallas kernels, forward(): pl.pallas_call(lambda *refs: forward_kernel(final, *refs), grid_spec=pltp...  13.2 us
    ppermute x10, starting transfers between devices, core_swap(): return lax.ppermute(block, 'core', [(0, 1), (1, 0)])  11.7 us
    ppermute x12, waiting for transfers between devices, z_shift(): lax.ppermute(block, Z, [(z_index(z), z_index((z + d) % 4)) for z in range...  6.78 us
    ppermute x3, starting transfers between devices, ring_shift(): return lax.ppermute(block, axis, [(i, (i + d) % 4) for i in range(4)])  5.41 us
    ppermute x1, starting transfers between devices, z_facing(): return lax.ppermute(block, Z, [(t, 3 - t) for t in range(4)])  4.65 us
  transfers between devices with their start and end apart: 27, of which 13 were waited for; matrix products, arithmetic and copies ran while one was open for 8% of the time, Pallas kernels for 0%

profile of v4, /device:TPU:1, one launch (start us, length us, event | category | flops | bytes accessed | tf_op | source)
XLA Modules:
  0.0 133.7 jit_solution(15080801681452124868)
XLA Ops:
  0.0 1.1 dynamic-slice_bitcast_fusion
  1.1 4.7 %collective-permute-start = (bf16[512,256]{1,0:T(8,128)(2,1)S(1)}, bf16[512,256]{1,0:T(8,128)(2,1)S(1)}, u32[]{:S(2)}, u32[]{:S(2)}) collective-permute-start(bf16[512,256]{1,0:T(8,128)(2,1)S(1)} %dynamic-slice_bitcast_fusion), channel_id=1, source_target_pairs={{0,5},{1,4},{4,1},{5,0},{2,7},{3,6},{6,3},{7,2},{8,13},{9,12},{12,... | collective-permute-start | bytes 786440 | tf_op jit(solution)/shard_map/ppermute | solution.py:35
  5.7 0.7 compare_and_fusion.1
  6.4 0.7 fusion.9
  7.0 1.2 gather_fusion.1
  8.3 1.3 gather_fusion
  9.7 1.0 collective-permute-start.1
  10.7 0.8 collective-permute-done.1
  11.9 0.6 stack.42.refs_0_.place
  12.5 1.2 collective-permute-start.5
  13.7 2.7 %collective-permute-start.4 = (bf16[512,256]{1,0:T(8,128)(2,1)S(1)}, bf16[512,256]{1,0:T(8,128)(2,1)S(1)}, u32[]{:S(2)}, u32[]{:S(2)}) collective-permute-start(bf16[512,256]{1,0:T(8,128)(2,1)S(1)} %collective-permute-done.refs_6_.refs_0_), channel_id=1, source_target_pairs={{0,24},{8,0},{16,8},{24,16},{1,25},{9,1},{17,9},{25,17},{2,26},{10... | collective-permute-start | bytes 786440 | tf_op jit(solution)/shard_map/ppermute | solution.py:39
  16.5 1.5 %collective-permute-start.3 = (bf16[512,256]{1,0:T(8,128)(2,1)S(1)}, bf16[512,256]{1,0:T(8,128)(2,1)S(1)}, u32[]{:S(2)}, u32[]{:S(2)}) collective-permute-start(bf16[512,256]{1,0:T(8,128)(2,1)S(1)} %collective-permute-done.refs_6_.refs_0_), channel_id=1, source_target_pairs={{0,96},{32,0},{64,32},{96,64},{1,97},{33,1},{65,33},{97,65},{2,98}... | collective-permute-start | bytes 786440 | tf_op jit(solution)/shard_map/ppermute | solution.py:39
  18.1 0.5 fusion.1
  18.6 1.6 %fusion.2 = bf16[8,272,512]{2,1,0:T(8,128)(2,1)} fusion(bf16[8,2,512]{2,1,0:T(2,128)(2,1)S(1)} %slice.45, bf16[8,256,512]{2,1,0:T(8,128)(2,1)S(1)} %fusion.1), kind=kLoop, calls=%fused_computation.8 | loop fusion | flops 6684672 | bytes 4341760 | tf_op jit(solution)/shard_map/concatenate | solution.py:252
  20.6 1.9 %collective-permute-done.3.refs_7_.refs_1_ = bf16[512,256]{1,0:T(8,128)(2,1)S(1)} collective-permute-done((bf16[512,256]{1,0:T(8,128)(2,1)S(1)}, bf16[512,256]{1,0:T(8,128)(2,1)S(1)}, u32[]{:S(2)}, u32[]{:S(2)}) %collective-permute-start.3) | collective-permute-done | bytes 262176 | tf_op jit(solution)/shard_map/ppermute | solution.py:39
  22.5 0.7 copy-done.5
  23.2 6.4 %shard_map.64 = bf16[1088,512]{1,0:T(8,128)(2,1)} custom-call(s32[9]{0:T(128)} %stack.42.refs_0_.place, bf16[2176,512]{1,0:T(8,128)(2,1)} %bitcast.53, bf16[512,8192]{1,0:T(8,128)(2,1)} %bitcast.44, bf16[512,8192]{1,0:T(8,128)(2,1)} %bitcast.45, bf16[512,8192]{1,0:T(8,128)(2,1)} %bitcast.46, bf16[512,8192]{1,0:T(8,128)(2,1)} %bitcast.47, ...), custom_call_target="tpu_custom_call" | custom-call | flops 2281701376 | bytes 2097152 | tf_op jit(solution)/shard_map/pallas_call | solution.py:120
  29.6 2.7 %collective-permute-start.6 = (bf16[1088,512]{1,0:T(8,128)(2,1)}, bf16[1088,512]{1,0:T(8,128)(2,1)S(1)}, u32[]{:S(2)}, u32[]{:S(2)}) collective-permute-start(bf16[1088,512]{1,0:T(8,128)(2,1)} %shard_map.64), channel_id=1, source_target_pairs={{0,2},{2,0},{1,3},{3,1},{4,6},{6,4},{5,7},{7,5},{8,10},{10,8},{9,1... | collective-permute-start | bytes 3342344 | tf_op jit(solution)/shard_map/ppermute | solution.py:43
  32.4 0.6 gather_fusion.3
  32.9 0.6 gather_fusion.2
  33.8 1.0 collective-permute-done.6.refs_10_
  34.9 1.0 copy-done.1
  35.9 6.8 %shard_map.65 = (f32[128,512]{1,0:T(8,128)}, f32[144,512]{1,0:T(8,128)}, bf16[128,512]{1,0:T(8,128)(2,1)}, bf16[144,512]{1,0:T(8,128)(2,1)}, bf16[128,512]{1,0:T...) custom-call(s32[9]{0:T(128)} %stack.42.refs_0_.place, ...), custom_call_target="tpu_custom_call" | custom-call | flops 2281701376 | bytes 2097152 | tf_op jit(solution)/shard_map/pallas_call | solution.py:120
  42.7 3.6 %collective-permute-start.7 = (bf16[128,512]{1,0:T(8,128)(2,1)}, bf16[128,512]{1,0:T(8,128)(2,1)S(1)}, u32[]{:S(2)}, u32[]{:S(2)}) collective-permute-start(bf16[128,512]{1,0:T(8,128)(2,1)} %get-tuple-element.24), channel_id=1, source_target_pairs={{0,1},{4,5},{1,0},{5,4},{2,3},{6,7},{3,2},{7,6},{8,9},{12,13},{9,8... | collective-permute-start | bytes 393224 | tf_op jit(solution)/shard_map/ppermute | solution.py:31
  46.2 2.7 %collective-permute-start.9 = (bf16[128,512]{1,0:T(8,128)(2,1)}, bf16[128,512]{1,0:T(8,128)(2,1)S(1)}, u32[]{:S(2)}, u32[]{:S(2)}) collective-permute-start(bf16[128,512]{1,0:T(8,128)(2,1)} %get-tuple-element.26), channel_id=1, source_target_pairs={{0,5},{4,0},{1,4},{5,1},{2,7},{6,2},{3,6},{7,3},{8,13},{12,8},{9,1... | collective-permute-start | bytes 393224 | tf_op jit(solution)/shard_map/ppermute | solution.py:31
  48.9 0.7 collective-permute-start.11
  49.6 0.4 collective-permute-done.7
  49.9 1.7 %collective-permute-start.12 = (bf16[144,512]{1,0:T(8,128)(2,1)}, bf16[144,512]{1,0:T(8,128)(2,1)S(1)}, u32[]{:S(2)}, u32[]{:S(2)}) collective-permute-start(bf16[144,512]{1,0:T(8,128)(2,1)} %get-tuple-element.31), channel_id=1, source_target_pairs={{0,5},{4,0},{1,4},{5,1},{2,7},{6,2},{3,6},{7,3},{8,13},{12,8},{9,1... | collective-permute-start | bytes 442376 | tf_op jit(solution)/shard_map/ppermute | solution.py:31
  51.7 1.1 collective-permute-done.8
  52.7 1.0 multiply_convert_fusion.1.refs_4_
  53.8 4.2 %collective-permute-start.19 = (bf16[128,512]{1,0:T(8,128)(2,1)S(1)}, bf16[128,512]{1,0:T(8,128)(2,1)S(1)}, u32[]{:S(2)}, u32[]{:S(2)}) collective-permute-start(bf16[128,512]{1,0:T(8,128)(2,1)S(1)} %multiply_convert_fusion.1.refs_4_), channel_id=1, source_target_pairs={{0,2},{2,0},{1,3},{3,1},{4,6},{6,4},{5,7},{7,5},{8,10},{10,8},{9,1... | collective-permute-start | bytes 393224 | tf_op jit(solution)/shard_map/ppermute | solution.py:43
  58.0 4.6 %collective-permute-start.15 = (bf16[128,512]{1,0:T(8,128)(2,1)S(1)}, bf16[128,512]{1,0:T(8,128)(2,1)S(1)}, u32[]{:S(2)}, u32[]{:S(2)}) collective-permute-start(bf16[128,512]{1,0:T(8,128)(2,1)S(1)} %multiply_convert_fusion.1.refs_4_), channel_id=1, source_target_pairs={{0,1},{4,5},{1,0},{5,4},{2,3},{6,7},{3,2},{7,6},{8,9},{12,13},{9,8... | collective-permute-start | bytes 393224 | tf_op jit(solution)/shard_map/ppermute | solution.py:31
  62.6 1.1 multiply_convert_fusion.refs_5_
  63.7 1.5 %collective-permute-start.18 = (bf16[144,512]{1,0:T(8,128)(2,1)S(1)}, bf16[144,512]{1,0:T(8,128)(2,1)S(1)}, u32[]{:S(2)}, u32[]{:S(2)}) collective-permute-start(bf16[144,512]{1,0:T(8,128)(2,1)S(1)} %multiply_convert_fusion.refs_5_), channel_id=1, source_target_pairs={{0,4},{4,1},{1,5},{5,0},{2,6},{6,3},{3,7},{7,2},{8,12},{12,9},{9,1... | collective-permute-start | bytes 442376 | tf_op jit(solution)/shard_map/ppermute | solution.py:31
  65.3 2.4 %collective-permute-start.14 = (bf16[144,512]{1,0:T(8,128)(2,1)S(1)}, bf16[144,512]{1,0:T(8,128)(2,1)S(1)}, u32[]{:S(2)}, u32[]{:S(2)}) collective-permute-start(bf16[144,512]{1,0:T(8,128)(2,1)S(1)} %multiply_convert_fusion.refs_5_), channel_id=1, source_target_pairs={{0,5},{4,0},{1,4},{5,1},{2,7},{6,2},{3,6},{7,3},{8,13},{12,8},{9,1... | collective-permute-start | bytes 442376 | tf_op jit(solution)/shard_map/ppermute | solution.py:31
  67.7 1.2 collective-permute-done.15.refs_8_
  68.9 1.5 %collective-permute-start.20 = (bf16[144,512]{1,0:T(8,128)(2,1)S(1)}, bf16[144,512]{1,0:T(8,128)(2,1)S(1)}, u32[]{:S(2)}, u32[]{:S(2)}) collective-permute-start(bf16[144,512]{1,0:T(8,128)(2,1)S(1)} %multiply_convert_fusion.refs_5_), channel_id=1, source_target_pairs={{0,2},{2,0},{1,3},{3,1},{4,6},{6,4},{5,7},{7,5},{8,10},{10,8},{9,1... | collective-permute-start | bytes 442376 | tf_op jit(solution)/shard_map/ppermute | solution.py:43
  70.5 2.5 %collective-permute-done.18.refs_11_ = bf16[144,512]{1,0:T(8,128)(2,1)S(1)} collective-permute-done((bf16[144,512]{1,0:T(8,128)(2,1)S(1)}, bf16[144,512]{1,0:T(8,128)(2,1)S(1)}, u32[]{:S(2)}, u32[]{:S(2)}) %collective-permute-start.18) | collective-permute-done | bytes 147488 | tf_op jit(solution)/shard_map/ppermute | solution.py:31
  73.0 0.6 collective-permute-start.26
  73.6 1.7 %collective-permute-done.16.refs_9_ = bf16[144,512]{1,0:T(8,128)(2,1)S(1)} collective-permute-done((bf16[144,512]{1,0:T(8,128)(2,1)S(1)}, bf16[144,512]{1,0:T(8,128)(2,1)S(1)}, u32[]{:S(2)}, u32[]{:S(2)}) %collective-permute-start.16) | collective-permute-done | bytes 147488 | tf_op jit(solution)/shard_map/ppermute | solution.py:31
  75.2 0.9 collective-permute-start.24
  76.2 0.3 collective-permute-start.22
  76.7 0.3 collective-permute-start.21
  77.0 0.8 collective-permute-done.23.refs_16_
  78.8 0.7 copy-done.15
  79.5 14.9 %shard_map.66 = bf16[64,2,8,1024]{3,2,1,0:T(8,128)(2,1)} custom-call(s32[9]{0:T(128)} %stack.42.refs_0_.place, bf16[2176,512]{1,0:T(8,128)(2,1)} %bitcast.55, bf16[512,8192]{1,0:T(8,128)(2,1)} %bitcast.52, bf16[512,256]{1,0:T(8,128)(2,1)} %copy-done.2, bf16[512,256]{1,0:T(8,128)(2,1)} %copy-done.5, bf16[512,256]{1,0:T(8,128)(2,1)} %copy-done.4, ...), custom_call_target="tpu_custom_call" | custom-call | flops 9126805504 | bytes 2097152 | tf_op jit(solution)/shard_map/pallas_call | solution.py:175
  94.3 35.9 %all_to_all.5 = bf16[128,8,1024]{2,1,0:T(8,128)(2,1)} all-to-all(bf16[128,8,1024]{2,1,0:T(8,128)(2,1)} %bitcast.57), channel_id=1, replica_groups=mesh['x'=4,'y'=4,'zl'=2,'core'=2,'zh'=2] {'x','y','zl','core','zh'}, dimensions={0} | all-to-all | bytes 4194304 | tf_op jit(solution)/shard_map/all_to_all | solution.py:281
  130.2 3.5 %shard_map.67 = f32[1,8,8192]{2,1,0:T(8,128)} custom-call(bf16[16,8,8,1024]{3,2,1,0:T(8,128)(2,1)} %bitcast.56), custom_call_target="tpu_custom_call" | custom-call | tf_op jit(solution)/shard_map/pallas_call | solution.py:206
  (93 shorter events, 2.7 us)
Async XLA Ops:
  0.0 32.9 %copy-start = (bf16[8,128,512]{2,1,0:T(8,128)(2,1)S(1)}, bf16[8,128,512]{2,1,0:T(8,128)(2,1)}, u32[]{:S(2)}) copy-start(bf16[8,128,512]{2,1,0:T(8,128)(2,1)} %param.8) | copy-start | bytes 3145732
  1.1 10.7 %collective-permute-start = (bf16[512,256]{1,0:T(8,128)(2,1)S(1)}, bf16[512,256]{1,0:T(8,128)(2,1)S(1)}, u32[]{:S(2)}, u32[]{:S(2)}) collective-permute-start(bf16[512,256]{1,0:T(8,128)(2,1)S(1)} %dynamic-slice_bitcast_fusion), channel_id=1, source_target_pairs={{0,5},{1,4},{4,1},{5,0},{2,7},{3,6},{6,3},{7,2},{8,13},{9,12},{12,... | collective-permute-start | bytes 786440 | tf_op jit(solution)/shard_map/ppermute | solution.py:35
  9.7 1.8 %collective-permute-start.1 = (f32[4,640]{1,0:T(4,128)S(1)}, f32[4,640]{1,0:T(4,128)S(1)}, u32[]{:S(2)}, u32[]{:S(2)}) collective-permute-start(f32[4,640]{1,0:T(4,128)S(1)} %pad_maximum_fusion.2), channel_id=1, source_target_pairs={{0,2},{2,0},{1,3},{3,1},{4,6},{6,4},{5,7},{7,5},{8,10},{10,8},{9,1... | collective-permute-start | bytes 30728 | tf_op jit(solution)/shard_map/ppermute | solution.py:43
  11.7 8.5 %copy-start.2 = (bf16[512,256]{1,0:T(8,128)(2,1)}, bf16[512,256]{1,0:T(8,128)(2,1)S(1)}, u32[]{:S(2)}) copy-start(bf16[512,256]{1,0:T(8,128)(2,1)S(1)} %collective-permute-done.refs_6_.refs_0_) | copy-start | bytes 786436
  11.7 6.2 %collective-permute-start.2 = (f32[8,640]{1,0:T(8,128)S(1)}, f32[8,640]{1,0:T(8,128)S(1)}, u32[]{:S(2)}, u32[]{:S(2)}) collective-permute-start(f32[8,640]{1,0:T(8,128)S(1)} %pad_maximum_fusion.1), channel_id=1, source_target_pairs={{0,4},{4,0},{1,5},{5,1},{2,6},{6,2},{3,7},{7,3},{8,12},{12,8},{9,1... | collective-permute-start | bytes 61448 | tf_op jit(solution)/shard_map/ppermute | solution.py:243
  12.5 7.8 %collective-permute-start.5 = (bf16[512,256]{1,0:T(8,128)(2,1)S(1)}, bf16[512,256]{1,0:T(8,128)(2,1)S(1)}, u32[]{:S(2)}, u32[]{:S(2)}) collective-permute-start(bf16[512,256]{1,0:T(8,128)(2,1)S(1)} %collective-permute-done.refs_6_.refs_0_), channel_id=1, source_target_pairs={{0,32},{32,64},{64,96},{96,0},{1,33},{33,65},{65,97},{97,1},{2,34}... | collective-permute-start | bytes 786440 | tf_op jit(solution)/shard_map/ppermute | solution.py:39
  13.7 6.9 %collective-permute-start.4 = (bf16[512,256]{1,0:T(8,128)(2,1)S(1)}, bf16[512,256]{1,0:T(8,128)(2,1)S(1)}, u32[]{:S(2)}, u32[]{:S(2)}) collective-permute-start(bf16[512,256]{1,0:T(8,128)(2,1)S(1)} %collective-permute-done.refs_6_.refs_0_), channel_id=1, source_target_pairs={{0,24},{8,0},{16,8},{24,16},{1,25},{9,1},{17,9},{25,17},{2,26},{10... | collective-permute-start | bytes 786440 | tf_op jit(solution)/shard_map/ppermute | solution.py:39
  16.5 6.1 %collective-permute-start.3 = (bf16[512,256]{1,0:T(8,128)(2,1)S(1)}, bf16[512,256]{1,0:T(8,128)(2,1)S(1)}, u32[]{:S(2)}, u32[]{:S(2)}) collective-permute-start(bf16[512,256]{1,0:T(8,128)(2,1)S(1)} %collective-permute-done.refs_6_.refs_0_), channel_id=1, source_target_pairs={{0,96},{32,0},{64,32},{96,64},{1,97},{33,1},{65,33},{97,65},{2,98}... | collective-permute-start | bytes 786440 | tf_op jit(solution)/shard_map/ppermute | solution.py:39
  20.3 2.2 %copy-start.3 = (bf16[512,256]{1,0:T(8,128)(2,1)}, bf16[512,256]{1,0:T(8,128)(2,1)S(1)}, u32[]{:S(2)}) copy-start(bf16[512,256]{1,0:T(8,128)(2,1)S(1)} %collective-permute-done.5.refs_9_.refs_3_) | copy-start | bytes 786436
  20.6 1.9 %copy-start.4 = (bf16[512,256]{1,0:T(8,128)(2,1)}, bf16[512,256]{1,0:T(8,128)(2,1)S(1)}, u32[]{:S(2)}) copy-start(bf16[512,256]{1,0:T(8,128)(2,1)S(1)} %collective-permute-done.4.refs_8_.refs_2_) | copy-start | bytes 786436
  22.5 0.7 copy-start.5
  23.2 9.0 %copy-start.23 = (s32[1,8]{1,0:T(1,128)S(1)}, s32[1,8]{1,0:T(1,128)}, u32[]{:S(2)}) copy-start(s32[1,8]{1,0:T(1,128)} %param.10) | copy-start | bytes 100
  23.2 9.1 %copy-start.8 = (bf16[8,512]{1,0:T(8,128)(2,1)S(1)}, bf16[8,512]{1,0:T(8,128)(2,1)}, u32[]{:S(2)}) copy-start(bf16[8,512]{1,0:T(8,128)(2,1)} %param.7) | copy-start | bytes 24580
  29.6 5.3 %collective-permute-start.6 = (bf16[1088,512]{1,0:T(8,128)(2,1)}, bf16[1088,512]{1,0:T(8,128)(2,1)S(1)}, u32[]{:S(2)}, u32[]{:S(2)}) collective-permute-start(bf16[1088,512]{1,0:T(8,128)(2,1)} %shard_map.64), channel_id=1, source_target_pairs={{0,2},{2,0},{1,3},{3,1},{4,6},{6,4},{5,7},{7,5},{8,10},{10,8},{9,1... | collective-permute-start | bytes 3342344 | tf_op jit(solution)/shard_map/ppermute | solution.py:43
  34.9 1.0 copy-start.1
  42.7 7.3 %collective-permute-start.7 = (bf16[128,512]{1,0:T(8,128)(2,1)}, bf16[128,512]{1,0:T(8,128)(2,1)S(1)}, u32[]{:S(2)}, u32[]{:S(2)}) collective-permute-start(bf16[128,512]{1,0:T(8,128)(2,1)} %get-tuple-element.24), channel_id=1, source_target_pairs={{0,1},{4,5},{1,0},{5,4},{2,3},{6,7},{3,2},{7,6},{8,9},{12,13},{9,8... | collective-permute-start | bytes 393224 | tf_op jit(solution)/shard_map/ppermute | solution.py:31
  46.2 6.5 %collective-permute-start.8 = (bf16[128,512]{1,0:T(8,128)(2,1)}, bf16[128,512]{1,0:T(8,128)(2,1)S(1)}, u32[]{:S(2)}, u32[]{:S(2)}) collective-permute-start(bf16[128,512]{1,0:T(8,128)(2,1)} %get-tuple-element.25), channel_id=1, source_target_pairs={{0,4},{4,1},{1,5},{5,0},{2,6},{6,3},{3,7},{7,2},{8,12},{12,9},{9,1... | collective-permute-start | bytes 393224 | tf_op jit(solution)/shard_map/ppermute | solution.py:31
  46.2 6.5 %collective-permute-start.9 = (bf16[128,512]{1,0:T(8,128)(2,1)}, bf16[128,512]{1,0:T(8,128)(2,1)S(1)}, u32[]{:S(2)}, u32[]{:S(2)}) collective-permute-start(bf16[128,512]{1,0:T(8,128)(2,1)} %get-tuple-element.26), channel_id=1, source_target_pairs={{0,5},{4,0},{1,4},{5,1},{2,7},{6,2},{3,6},{7,3},{8,13},{12,8},{9,1... | collective-permute-start | bytes 393224 | tf_op jit(solution)/shard_map/ppermute | solution.py:31
  48.9 9.1 %collective-permute-start.10 = (bf16[144,512]{1,0:T(8,128)(2,1)}, bf16[144,512]{1,0:T(8,128)(2,1)S(1)}, u32[]{:S(2)}, u32[]{:S(2)}) collective-permute-start(bf16[144,512]{1,0:T(8,128)(2,1)} %get-tuple-element.29), channel_id=1, source_target_pairs={{0,1},{4,5},{1,0},{5,4},{2,3},{6,7},{3,2},{7,6},{8,9},{12,13},{9,8... | collective-permute-start | bytes 442376 | tf_op jit(solution)/shard_map/ppermute | solution.py:31
  48.9 13.7 %collective-permute-start.11 = (bf16[144,512]{1,0:T(8,128)(2,1)}, bf16[144,512]{1,0:T(8,128)(2,1)S(1)}, u32[]{:S(2)}, u32[]{:S(2)}) collective-permute-start(bf16[144,512]{1,0:T(8,128)(2,1)} %get-tuple-element.30), channel_id=1, source_target_pairs={{0,4},{4,1},{1,5},{5,0},{2,6},{6,3},{3,7},{7,2},{8,12},{12,9},{9,1... | collective-permute-start | bytes 442376 | tf_op jit(solution)/shard_map/ppermute | solution.py:31
  49.9 12.7 %collective-permute-start.12 = (bf16[144,512]{1,0:T(8,128)(2,1)}, bf16[144,512]{1,0:T(8,128)(2,1)S(1)}, u32[]{:S(2)}, u32[]{:S(2)}) collective-permute-start(bf16[144,512]{1,0:T(8,128)(2,1)} %get-tuple-element.31), channel_id=1, source_target_pairs={{0,5},{4,0},{1,4},{5,1},{2,7},{6,2},{3,6},{7,3},{8,13},{12,8},{9,1... | collective-permute-start | bytes 442376 | tf_op jit(solution)/shard_map/ppermute | solution.py:31
  53.8 24.3 %copy-start.7 = (bf16[128,512]{1,0:T(8,128)(2,1)}, bf16[128,512]{1,0:T(8,128)(2,1)S(1)}, u32[]{:S(2)}) copy-start(bf16[128,512]{1,0:T(8,128)(2,1)S(1)} %multiply_convert_fusion.1.refs_4_) | copy-start | bytes 393220
  53.8 11.4 %collective-permute-start.19 = (bf16[128,512]{1,0:T(8,128)(2,1)S(1)}, bf16[128,512]{1,0:T(8,128)(2,1)S(1)}, u32[]{:S(2)}, u32[]{:S(2)}) collective-permute-start(bf16[128,512]{1,0:T(8,128)(2,1)S(1)} %multiply_convert_fusion.1.refs_4_), channel_id=1, source_target_pairs={{0,2},{2,0},{1,3},{3,1},{4,6},{6,4},{5,7},{7,5},{8,10},{10,8},{9,1... | collective-permute-start | bytes 393224 | tf_op jit(solution)/shard_map/ppermute | solution.py:43
  58.0 7.3 %collective-permute-start.17 = (bf16[128,512]{1,0:T(8,128)(2,1)S(1)}, bf16[128,512]{1,0:T(8,128)(2,1)S(1)}, u32[]{:S(2)}, u32[]{:S(2)}) collective-permute-start(bf16[128,512]{1,0:T(8,128)(2,1)S(1)} %multiply_convert_fusion.1.refs_4_), channel_id=1, source_target_pairs={{0,4},{4,1},{1,5},{5,0},{2,6},{6,3},{3,7},{7,2},{8,12},{12,9},{9,1... | collective-permute-start | bytes 393224 | tf_op jit(solution)/shard_map/ppermute | solution.py:31
  58.0 10.9 %collective-permute-start.15 = (bf16[128,512]{1,0:T(8,128)(2,1)S(1)}, bf16[128,512]{1,0:T(8,128)(2,1)S(1)}, u32[]{:S(2)}, u32[]{:S(2)}) collective-permute-start(bf16[128,512]{1,0:T(8,128)(2,1)S(1)} %multiply_convert_fusion.1.refs_4_), channel_id=1, source_target_pairs={{0,1},{4,5},{1,0},{5,4},{2,3},{6,7},{3,2},{7,6},{8,9},{12,13},{9,8... | collective-permute-start | bytes 393224 | tf_op jit(solution)/shard_map/ppermute | solution.py:31
  62.6 7.8 %collective-permute-start.13 = (bf16[128,512]{1,0:T(8,128)(2,1)S(1)}, bf16[128,512]{1,0:T(8,128)(2,1)S(1)}, u32[]{:S(2)}, u32[]{:S(2)}) collective-permute-start(bf16[128,512]{1,0:T(8,128)(2,1)S(1)} %multiply_convert_fusion.1.refs_4_), channel_id=1, source_target_pairs={{0,5},{4,0},{1,4},{5,1},{2,7},{6,2},{3,6},{7,3},{8,13},{12,8},{9,1... | collective-permute-start | bytes 393224 | tf_op jit(solution)/shard_map/ppermute | solution.py:31
  63.7 14.4 %copy-start.6 = (bf16[144,512]{1,0:T(8,128)(2,1)}, bf16[144,512]{1,0:T(8,128)(2,1)S(1)}, u32[]{:S(2)}) copy-start(bf16[144,512]{1,0:T(8,128)(2,1)S(1)} %multiply_convert_fusion.refs_5_) | copy-start | bytes 442372
  63.7 9.3 %collective-permute-start.18 = (bf16[144,512]{1,0:T(8,128)(2,1)S(1)}, bf16[144,512]{1,0:T(8,128)(2,1)S(1)}, u32[]{:S(2)}, u32[]{:S(2)}) collective-permute-start(bf16[144,512]{1,0:T(8,128)(2,1)S(1)} %multiply_convert_fusion.refs_5_), channel_id=1, source_target_pairs={{0,4},{4,1},{1,5},{5,0},{2,6},{6,3},{3,7},{7,2},{8,12},{12,9},{9,1... | collective-permute-start | bytes 442376 | tf_op jit(solution)/shard_map/ppermute | solution.py:31
  65.2 12.9 %copy-start.16 = (bf16[128,512]{1,0:T(8,128)(2,1)}, bf16[128,512]{1,0:T(8,128)(2,1)S(1)}, u32[]{:S(2)}) copy-start(bf16[128,512]{1,0:T(8,128)(2,1)S(1)} %collective-permute-done.19.refs_12_) | copy-start | bytes 393220
  65.2 10.0 %collective-permute-start.16 = (bf16[144,512]{1,0:T(8,128)(2,1)S(1)}, bf16[144,512]{1,0:T(8,128)(2,1)S(1)}, u32[]{:S(2)}, u32[]{:S(2)}) collective-permute-start(bf16[144,512]{1,0:T(8,128)(2,1)S(1)} %multiply_convert_fusion.refs_5_), channel_id=1, source_target_pairs={{0,1},{4,5},{1,0},{5,4},{2,3},{6,7},{3,2},{7,6},{8,9},{12,13},{9,8... | collective-permute-start | bytes 442376 | tf_op jit(solution)/shard_map/ppermute | solution.py:31
  65.3 12.8 %copy-start.17 = (bf16[128,512]{1,0:T(8,128)(2,1)}, bf16[128,512]{1,0:T(8,128)(2,1)S(1)}, u32[]{:S(2)}) copy-start(bf16[128,512]{1,0:T(8,128)(2,1)S(1)} %collective-permute-done.17.refs_10_) | copy-start | bytes 393220
  65.3 10.9 %collective-permute-start.14 = (bf16[144,512]{1,0:T(8,128)(2,1)S(1)}, bf16[144,512]{1,0:T(8,128)(2,1)S(1)}, u32[]{:S(2)}, u32[]{:S(2)}) collective-permute-start(bf16[144,512]{1,0:T(8,128)(2,1)S(1)} %multiply_convert_fusion.refs_5_), channel_id=1, source_target_pairs={{0,5},{4,0},{1,4},{5,1},{2,7},{6,2},{3,6},{7,3},{8,13},{12,8},{9,1... | collective-permute-start | bytes 442376 | tf_op jit(solution)/shard_map/ppermute | solution.py:31
  68.9 9.2 %copy-start.18 = (bf16[128,512]{1,0:T(8,128)(2,1)}, bf16[128,512]{1,0:T(8,128)(2,1)S(1)}, u32[]{:S(2)}) copy-start(bf16[128,512]{1,0:T(8,128)(2,1)S(1)} %collective-permute-done.15.refs_8_) | copy-start | bytes 393220
  68.9 7.5 %collective-permute-start.20 = (bf16[144,512]{1,0:T(8,128)(2,1)S(1)}, bf16[144,512]{1,0:T(8,128)(2,1)S(1)}, u32[]{:S(2)}, u32[]{:S(2)}) collective-permute-start(bf16[144,512]{1,0:T(8,128)(2,1)S(1)} %multiply_convert_fusion.refs_5_), channel_id=1, source_target_pairs={{0,2},{2,0},{1,3},{3,1},{4,6},{6,4},{5,7},{7,5},{8,10},{10,8},{9,1... | collective-permute-start | bytes 442376 | tf_op jit(solution)/shard_map/ppermute | solution.py:43
  70.4 7.7 %copy-start.19 = (bf16[128,512]{1,0:T(8,128)(2,1)}, bf16[128,512]{1,0:T(8,128)(2,1)S(1)}, u32[]{:S(2)}) copy-start(bf16[128,512]{1,0:T(8,128)(2,1)S(1)} %collective-permute-done.13.refs_6_) | copy-start | bytes 393220
  70.4 6.3 %collective-permute-start.25 = (bf16[128,512]{1,0:T(8,128)(2,1)S(1)}, bf16[128,512]{1,0:T(8,128)(2,1)S(1)}, u32[]{:S(2)}, u32[]{:S(2)}) collective-permute-start(bf16[128,512]{1,0:T(8,128)(2,1)S(1)} %collective-permute-done.17.refs_10_), channel_id=1, source_target_pairs={{0,2},{2,0},{1,3},{3,1},{4,6},{6,4},{5,7},{7,5},{8,10},{10,8},{9,1... | collective-permute-start | bytes 393224 | tf_op jit(solution)/shard_map/ppermute | solution.py:43
  73.0 5.2 %copy-start.9 = (bf16[144,512]{1,0:T(8,128)(2,1)}, bf16[144,512]{1,0:T(8,128)(2,1)S(1)}, u32[]{:S(2)}) copy-start(bf16[144,512]{1,0:T(8,128)(2,1)S(1)} %collective-permute-done.18.refs_11_) | copy-start | bytes 442372
  73.0 5.1 %collective-permute-start.26 = (bf16[144,512]{1,0:T(8,128)(2,1)S(1)}, bf16[144,512]{1,0:T(8,128)(2,1)S(1)}, u32[]{:S(2)}, u32[]{:S(2)}) collective-permute-start(bf16[144,512]{1,0:T(8,128)(2,1)S(1)} %collective-permute-done.18.refs_11_), channel_id=1, source_target_pairs={{0,2},{2,0},{1,3},{3,1},{4,6},{6,4},{5,7},{7,5},{8,10},{10,8},{9,1... | collective-permute-start | bytes 442376 | tf_op jit(solution)/shard_map/ppermute | solution.py:43
  75.2 2.9 %copy-start.10 = (bf16[144,512]{1,0:T(8,128)(2,1)}, bf16[144,512]{1,0:T(8,128)(2,1)S(1)}, u32[]{:S(2)}) copy-start(bf16[144,512]{1,0:T(8,128)(2,1)S(1)} %collective-permute-done.16.refs_9_) | copy-start | bytes 442372
  75.2 2.8 %collective-permute-start.24 = (bf16[144,512]{1,0:T(8,128)(2,1)S(1)}, bf16[144,512]{1,0:T(8,128)(2,1)S(1)}, u32[]{:S(2)}, u32[]{:S(2)}) collective-permute-start(bf16[144,512]{1,0:T(8,128)(2,1)S(1)} %collective-permute-done.16.refs_9_), channel_id=1, source_target_pairs={{0,2},{2,0},{1,3},{3,1},{4,6},{6,4},{5,7},{7,5},{8,10},{10,8},{9,1... | collective-permute-start | bytes 442376 | tf_op jit(solution)/shard_map/ppermute | solution.py:43
  76.2 2.0 %copy-start.11 = (bf16[144,512]{1,0:T(8,128)(2,1)}, bf16[144,512]{1,0:T(8,128)(2,1)S(1)}, u32[]{:S(2)}) copy-start(bf16[144,512]{1,0:T(8,128)(2,1)S(1)} %collective-permute-done.14.refs_7_) | copy-start | bytes 442372
  76.2 1.9 %collective-permute-start.22 = (bf16[144,512]{1,0:T(8,128)(2,1)S(1)}, bf16[144,512]{1,0:T(8,128)(2,1)S(1)}, u32[]{:S(2)}, u32[]{:S(2)}) collective-permute-start(bf16[144,512]{1,0:T(8,128)(2,1)S(1)} %collective-permute-done.14.refs_7_), channel_id=1, source_target_pairs={{0,2},{2,0},{1,3},{3,1},{4,6},{6,4},{5,7},{7,5},{8,10},{10,8},{9,1... | collective-permute-start | bytes 442376 | tf_op jit(solution)/shard_map/ppermute | solution.py:43
  76.5 1.7 %copy-start.12 = (bf16[144,512]{1,0:T(8,128)(2,1)}, bf16[144,512]{1,0:T(8,128)(2,1)S(1)}, u32[]{:S(2)}) copy-start(bf16[144,512]{1,0:T(8,128)(2,1)S(1)} %collective-permute-done.20.refs_13_) | copy-start | bytes 442372
  76.5 1.3 %collective-permute-start.23 = (bf16[128,512]{1,0:T(8,128)(2,1)S(1)}, bf16[128,512]{1,0:T(8,128)(2,1)S(1)}, u32[]{:S(2)}, u32[]{:S(2)}) collective-permute-start(bf16[128,512]{1,0:T(8,128)(2,1)S(1)} %collective-permute-done.15.refs_8_), channel_id=1, source_target_pairs={{0,2},{2,0},{1,3},{3,1},{4,6},{6,4},{5,7},{7,5},{8,10},{10,8},{9,1... | collective-permute-start | bytes 393224 | tf_op jit(solution)/shard_map/ppermute | solution.py:43
  76.7 1.5 %copy-start.20 = (bf16[128,512]{1,0:T(8,128)(2,1)}, bf16[128,512]{1,0:T(8,128)(2,1)S(1)}, u32[]{:S(2)}) copy-start(bf16[128,512]{1,0:T(8,128)(2,1)S(1)} %collective-permute-done.25.refs_18_) | copy-start | bytes 393220
  76.7 1.3 %collective-permute-start.21 = (bf16[128,512]{1,0:T(8,128)(2,1)S(1)}, bf16[128,512]{1,0:T(8,128)(2,1)S(1)}, u32[]{:S(2)}, u32[]{:S(2)}) collective-permute-start(bf16[128,512]{1,0:T(8,128)(2,1)S(1)} %collective-permute-done.13.refs_6_), channel_id=1, source_target_pairs={{0,2},{2,0},{1,3},{3,1},{4,6},{6,4},{5,7},{7,5},{8,10},{10,8},{9,1... | collective-permute-start | bytes 393224 | tf_op jit(solution)/shard_map/ppermute | solution.py:43
  78.1 0.7 copy-start.13
  78.1 0.7 copy-start.14
  (3 other events, 2.0 us)

commit v5 on v3

--- a/solution.py
+++ b/solution.py
@@ -17,6 +17,7 @@
 CHUNK = 2 * TANGENTS + 16
 GROUP = 4 * CHUNK
 STEP = 2 * CHUNK
+LIMIT = 24 * 2**20
 jacobian_weight = 32.0
 f32 = jnp.float32
 bf16 = jnp.bfloat16
@@ -90,24 +91,21 @@
         outs[0][...] = total.astype(bf16)
         return
     total = total + arrived[...].astype(f32)
-
-    @pl.when(pl.program_id(0) == 0)
-    def _():
-        outs[0][...] = total[:CHUNK]
-        outs[1][...] = total[CHUNK:].astype(bf16)
-
-    @pl.when(pl.program_id(0) == 1)
-    def _():
-        outs[2][...] = total[:CHUNK].astype(bf16)
-        outs[3][...] = total[CHUNK:].astype(bf16)
-
-
-def forward(place, rows, weight, other, arrived=None):
+    for step in range(2):
+
+        @pl.when(pl.program_id(0) == step)
+        def _():
+            for c in range(2):
+                out = outs[2 * step + c]
+                out[...] = total[c * CHUNK : (c + 1) * CHUNK].astype(out.dtype)
+
+
+def forward(place, rows, own, other, arrived=None):
     final = arrived is not None
     base = 0 if final else 2
     in_specs = [pl.BlockSpec((STEP, REDUCED), lambda i, place: (i + base, 0)), *own_specs()]
     in_specs += [whole_spec((REDUCED, BLOCK))] * 4
-    args = [rows, weight, weight, weight, weight, *other]
+    args = [rows, own, own, own, own, *other]
     out_specs = pl.BlockSpec((STEP, REDUCED), lambda i, place: (i, 0))
     out_shape = jax.ShapeDtypeStruct((GROUP, REDUCED), bf16)
     if final:
@@ -126,31 +124,78 @@
             scratch_shapes=[pltpu.VMEM((REDUCED, COLS), bf16)] * 2,
         ),
         out_shape=out_shape,
-        compiler_params=pltpu.CompilerParams(dimension_semantics=("arbitrary",)),
+        compiler_params=pltpu.CompilerParams(
+            dimension_semantics=("arbitrary",), vmem_limit_bytes=LIMIT
+        ),
         cost_estimate=pl.CostEstimate(
             flops=4 * GROUP * REDUCED * COLS, bytes_accessed=4 * REDUCED * COLS, transcendentals=0
         ),
     )(place, *args)
 
 
-def backward_kernel(place, rows, own, *refs):
-    other, misfits, out = refs[:4], refs[4:12], refs[12]
-    tangents, cotangents = refs[13:]
-    step = pl.program_id(0)
-    theirs = other[3][...]
+def piece_of(step, pieces):
+    chosen = pieces[3][...]
     for k in range(3):
-        theirs = jnp.where(step == k, other[k][...], theirs)
-    here = place[4] == 0
-    w_first = jnp.where(here, own[...], theirs)
-    w_last = jnp.where(here, theirs, own[...])
+        chosen = jnp.where(step == k, pieces[k][...], chosen)
+    return chosen
+
+
+def prepare_kernel(place, rows, own, *refs):
+    other, (picked_out, tangents, linears) = refs[:4], refs[4:]
+    theirs = piece_of(pl.program_id(0), other)
+    w_first = jnp.where(place[4] == 0, own[...], theirs)
+    for c in range(0, 8, 2):
+        span = pl.ds(c * CHUNK, STEP)
+        picked = jnp.dot(rows[span, :], w_first, preferred_element_type=f32)
+        picked_out[span, :] = picked.astype(bf16)
+        parts = []
+        for e in range(2):
+            part = picked[e * CHUNK : (e + 1) * CHUNK]
+            linear = part[2 * TANGENTS :]
+            hidden, first, _ = slopes(linear)
+            parts += per_row(part, first) + [hidden]
+            linears[pl.ds((c + e) * 16, 16), :] = linear
+        tangents[span, :] = jnp.concatenate(parts, axis=0).astype(bf16)
+
+
+def prepare(place, rows, own, other):
+    columns = lambda height: pl.BlockSpec((height, BLOCK), lambda j, place: (0, j))
+    return pl.pallas_call(
+        prepare_kernel,
+        grid_spec=pltpu.PrefetchScalarGridSpec(
+            num_scalar_prefetch=1,
+            grid=(4,),
+            in_specs=[
+                whole_spec((2 * GROUP, REDUCED)),
+                pl.BlockSpec((REDUCED, BLOCK), lambda j, place: (0, place[j])),
+                *[whole_spec((REDUCED, BLOCK))] * 4,
+            ],
+            out_specs=[columns(2 * GROUP), columns(2 * GROUP), columns(128)],
+        ),
+        out_shape=[
+            jax.ShapeDtypeStruct((2 * GROUP, COLS), bf16),
+            jax.ShapeDtypeStruct((2 * GROUP, COLS), bf16),
+            jax.ShapeDtypeStruct((128, COLS), f32),
+        ],
+        compiler_params=pltpu.CompilerParams(
+            dimension_semantics=("arbitrary",), vmem_limit_bytes=LIMIT
+        ),
+        cost_estimate=pl.CostEstimate(
+            flops=4 * GROUP * REDUCED * COLS, bytes_accessed=4 * REDUCED * COLS, transcendentals=0
+        ),
+    )(place, rows, own, *other)
+
+
+def backward_kernel(place, rows, picked, tangents, linears, own, *refs):
+    other, misfits, out, cotangents = refs[:4], refs[4:12], refs[12], refs[13]
+    theirs = piece_of(pl.program_id(0), other)
+    w_last = jnp.where(place[4] == 0, theirs, own[...])
     for c in range(8):
         span = pl.ds(c * CHUNK, CHUNK)
-        picked = jnp.dot(rows[span, :], w_first, preferred_element_type=f32)
-        hidden, first, second = slopes(picked[2 * TANGENTS :])
-        tangents[span, :] = jnp.concatenate(per_row(picked, first) + [hidden], axis=0).astype(bf16)
         back = jnp.dot(misfits[c][...], w_last, preferred_element_type=f32)
         back = back.astype(bf16).astype(f32)
-        joint = back[: 2 * TANGENTS] * picked[: 2 * TANGENTS]
+        _, first, second = slopes(linears[pl.ds(c * 16, 16), :])
+        joint = back[: 2 * TANGENTS] * picked[pl.ds(c * CHUNK, 2 * TANGENTS), :].astype(f32)
         projected = jnp.concatenate(
             [
                 jnp.sum(joint[:TANGENTS], axis=0, keepdims=True),
@@ -169,7 +214,8 @@
     out[:, 1] = last.astype(bf16).reshape(64, 8, BLOCK)
 
 
-def backward(place, rows, misfits, weight, other):
+def backward(place, rows, prepared, own, other, misfits):
+    columns = lambda height: pl.BlockSpec((height, BLOCK), lambda j, place: (0, j))
     return pl.pallas_call(
         backward_kernel,
         grid_spec=pltpu.PrefetchScalarGridSpec(
@@ -177,19 +223,24 @@
             grid=(4,),
             in_specs=[
                 whole_spec((2 * GROUP, REDUCED)),
+                columns(2 * GROUP),
+                columns(2 * GROUP),
+                columns(128),
                 pl.BlockSpec((REDUCED, BLOCK), lambda j, place: (0, place[j])),
                 *[whole_spec((REDUCED, BLOCK))] * 4,
                 *[whole_spec((CHUNK, REDUCED))] * 8,
             ],
-            out_specs=pl.BlockSpec((64, 2, 8, BLOCK), lambda j, place: (0, 0, 0, place[5 + j])),
-            scratch_shapes=[pltpu.VMEM((2 * GROUP, BLOCK), bf16)] * 2,
+            out_specs=pl.BlockSpec((64, 2, 8, BLOCK), lambda j, place: (0, 0, 0, place[j])),
+            scratch_shapes=[pltpu.VMEM((2 * GROUP, BLOCK), bf16)],
         ),
         out_shape=jax.ShapeDtypeStruct((64, 2, 8, COLS), bf16),
-        compiler_params=pltpu.CompilerParams(dimension_semantics=("arbitrary",)),
+        compiler_params=pltpu.CompilerParams(
+            dimension_semantics=("arbitrary",), vmem_limit_bytes=LIMIT
+        ),
         cost_estimate=pl.CostEstimate(
-            flops=16 * GROUP * REDUCED * COLS, bytes_accessed=4 * REDUCED * COLS, transcendentals=0
-        ),
-    )(place, rows, weight, *other, *misfits)
+            flops=12 * GROUP * REDUCED * COLS, bytes_accessed=4 * REDUCED * COLS, transcendentals=0
+        ),
+    )(place, rows, *prepared, own, *other, *misfits)
 
 
 def total_kernel(pieces, out):
@@ -207,8 +258,15 @@
         in_specs=[pl.BlockSpec((16, 2, 8, COLS), lambda i: (0, i, 0, 0))],
         out_specs=pl.BlockSpec((1, 8, 2 * COLS), lambda i: (0, 0, i)),
         out_shape=jax.ShapeDtypeStruct((1, 8, 8 * COLS), f32),
-        compiler_params=pltpu.CompilerParams(dimension_semantics=("arbitrary",)),
+        compiler_params=pltpu.CompilerParams(
+            dimension_semantics=("arbitrary",), vmem_limit_bytes=LIMIT
+        ),
     )(pieces)
+
+
+def rows_at(array, order, places):
+    picked = [lax.dynamic_slice_in_dim(array, order[k], 1, 0) for k in places]
+    return jnp.concatenate(picked, axis=0)
 
 
 def shards(samples, targets, jacobian_targets, directions, plan, weights):
@@ -220,26 +278,29 @@
     mine = (zl * 2 + core) * 2 + zh
     theirs = ((1 - zl) * 2 + core) * 2 + (1 - zh)
     turn = [(kind + k) % 4 for k in range(4)]
-    place = jnp.stack([mine * 4 + t for t in turn] + [zh] + turn).astype(jnp.int32)
+    place = jnp.stack(turn + [zh]).astype(jnp.int32)
 
     quarter = lax.dynamic_slice_in_dim(weight, theirs * COLS + kind * BLOCK, BLOCK, 1)
     direct = z_facing(quarter)
+    own = lax.dynamic_slice_in_dim(weight, mine * COLS, COLS, 1)
 
     order = plan[0, :MICRO]
-    inputs = jnp.take(samples, order, axis=0).astype(f32)
-    chosen = jnp.take(directions, order, axis=0).astype(f32)
+    inputs = rows_at(samples, order, range(MICRO)).astype(f32)
+    chosen = rows_at(directions, order, range(MICRO)).astype(f32)
     packed = jnp.concatenate([inputs, chosen], axis=1)
-    direct, packed = lax.optimization_barrier((direct, packed))
+    swapped = core_swap(packed)
+    direct, packed, swapped = lax.optimization_barrier((direct, packed, swapped))
     other = [
         direct,
         ring_shift(direct, "x", 3),
         ring_shift(direct, "y", 3),
         ring_shift(direct, "x", 1),
     ]
-    small = lax.all_gather(packed, ("zl", "core"))
-    small = small.reshape(2, 2, 2, 2, REDUCED + TANGENTS).transpose(1, 2, 0, 3, 4)
-    small = small.reshape(2, 4, 2, REDUCED + TANGENTS)
-    small = jnp.where(core == 0, small, small[::-1])
+    pair = jnp.concatenate([packed, swapped], axis=0)
+    beside = lax.ppermute(pair, "zl", [(0, 1), (1, 0)])
+    low = jnp.where(zl == 0, pair, beside).reshape(2, 2, 2, REDUCED + TANGENTS)
+    high = jnp.where(zl == 0, beside, pair).reshape(2, 2, 2, REDUCED + TANGENTS)
+    small = jnp.stack([low, high], axis=2).reshape(2, 4, 2, REDUCED + TANGENTS)
     small = lax.dynamic_slice_in_dim(jnp.concatenate([small, small], axis=1), z, 4, 1)
     small = small.reshape(8, 2, REDUCED + TANGENTS)
     chosen = small[:, :, REDUCED:].reshape(8, 2 * TANGENTS).astype(jnp.int32)
@@ -248,15 +309,19 @@
     rows = jnp.concatenate([onehot, inputs], axis=1).reshape(2 * GROUP, REDUCED)
 
     own_order = lax.dynamic_slice_in_dim(order, zh * 2, 2)
-    target_rows = jnp.take(targets, own_order, axis=0).astype(f32)
-    target_jac = jnp.take(jacobian_targets, own_order, axis=0).reshape(2 * TANGENTS, REDUCED)
+    target_rows = rows_at(targets, own_order, range(2)).astype(f32)
+    target_jac = rows_at(jacobian_targets, own_order, range(2)).reshape(2 * TANGENTS, REDUCED)
     wanted = jnp.concatenate(
         [target_jac.astype(f32), jnp.pad(target_rows, ((0, 14), (0, 0)))], axis=0
     )
 
-    from_core = core_swap(forward(place, rows, weight, other))
-    chunks = forward(place, rows, weight, other, from_core)
+    from_core = core_swap(forward(place, rows, own, other))
+    from_core, wanted = lax.optimization_barrier((from_core, wanted))
+    chunks = forward(place, rows, own, other, from_core)
+    chunks, ready = lax.optimization_barrier((chunks, rows))
     got = [z_shift(chunks[d], d) for d in (2, 1, 3)]
+    prepared = prepare(place, ready, own, other)
+    got, prepared = lax.optimization_barrier((got, prepared))
     total = chunks[0]
     for g in got:
         total = total + g.astype(f32)
@@ -266,7 +331,7 @@
     for d in (2, 1, 3):
         near[d] = z_shift(misfit, 4 - d)
     misfits = near + [core_swap(m) for m in near]
-    sent = backward(place, rows, misfits, weight, other)
+    sent = backward(place, rows, prepared, own, other, misfits)
     pieces = lax.all_to_all(
         sent.reshape(128, 8, COLS), AXES, split_axis=0, concat_axis=0, tiled=True
     )

time: 136 us -> 133 us (0.978)
  between operations: 0.19 us -> 11.6 us
  waiting for transfers between devices: 24.4 us -> 16.6 us
  starting transfers between devices: 23.7 us -> 29.6 us
  blocking collectives: 41.6 us -> 36.2 us
  other arithmetic: 5.24 us -> 1.12 us
    ppermute x6, waiting for transfers between devices: 19.7 us -> 9.69 us  [z_shift(): lax.ppermute(block, Z, [(z_index(z), z_index((z + d) % 4)) for z in range...]
    all_gather x1 -> x0, blocking collectives: 7.12 us -> none  [shards(): small = lax.all_gather(packed, ('zl', 'core'))]
    ppermute x5 -> x6, starting transfers between devices: 4.71 us -> 11.5 us  [core_swap(): return lax.ppermute(block, 'core', [(0, 1), (1, 0)])]
    pallas_call x0 -> x1, Pallas kernels: none -> 6.78 us  [prepare(): pl.pallas_call(prepare_kernel, grid_spec=pltpu.PrefetchScalarGridSpec(num...]
    ppermute x3, waiting for transfers between devices: 0.01 us -> 4.67 us  [ring_shift(): return lax.ppermute(block, axis, [(i, (i + d) % 4) for i in range(4)])]
    dynamic_slice x0 -> x6, local copies, waits for them, and re-layouts: none -> 4.09 us  [the longest x4 2.71 us: rows_at(): picked = [lax.dynamic_slice_in_dim(array, order[k], 1, 0) for k in places]]
    pallas_call x1, Pallas kernels: 14.9 us -> 11.2 us  [backward(): pl.pallas_call(backward_kernel, grid_spec=pltpu.PrefetchScalarGridSpec(nu...]
    gather x4 -> x0, local copies, waits for them, and re-layouts: 3.64 us -> none  [the longest x1 1.27 us: shards(): inputs = jnp.take(samples, order, axis=0).astype(f32)]
  transfers between devices with their start and end apart: 15 -> 17, of which waited for: 8 -> 9; matrix products, arithmetic and copies ran while one was open for 6% -> 5% of each run, Pallas kernels for 0% -> 5%
where the time goes in v5:
time: 133 us
  blocking collectives  36.2 us (27%)
  Pallas kernels  30.4 us (23%)
  starting transfers between devices  29.6 us (22%)
  waiting for transfers between devices  16.6 us (12%)
  between operations  11.6 us (9%)
  local copies, waits for them, and re-layouts  7.25 us (5%)
    all_to_all x1, blocking collectives, shards(): lax.all_to_all(sent.reshape(128, 8, COLS), AXES, split_axis=0, concat_axi...  36.2 us
    ppermute x6, starting transfers between devices, core_swap(): return lax.ppermute(block, 'core', [(0, 1), (1, 0)])  11.5 us
    pallas_call x1, Pallas kernels, backward(): pl.pallas_call(backward_kernel, grid_spec=pltpu.PrefetchScalarGridSpec(nu...  11.2 us
    pallas_call x2, Pallas kernels, forward(): pl.pallas_call(lambda *refs: forward_kernel(final, *refs), grid_spec=pltp...  10.8 us
    ppermute x6, waiting for transfers between devices, z_shift(): lax.ppermute(block, Z, [(z_index(z), z_index((z + d) % 4)) for z in range...  9.69 us
    ppermute x6, starting transfers between devices, z_shift(): lax.ppermute(block, Z, [(z_index(z), z_index((z + d) % 4)) for z in range...  7.89 us
    pallas_call x1, Pallas kernels, prepare(): pl.pallas_call(prepare_kernel, grid_spec=pltpu.PrefetchScalarGridSpec(num...  6.78 us
    ppermute x3, starting transfers between devices, ring_shift(): return lax.ppermute(block, axis, [(i, (i + d) % 4) for i in range(4)])  5.41 us
  transfers between devices with their start and end apart: 17, of which 9 were waited for; matrix products, arithmetic and copies ran while one was open for 5% of the time, Pallas kernels for 5%

profile of v5, /device:TPU:1, one launch (start us, length us, event | category | flops | bytes accessed | tf_op | source)
XLA Modules:
  0.0 132.7 jit_solution(9843860012981915020)
XLA Ops:
  0.0 1.0 dynamic-slice_bitcast_fusion.1
  1.0 4.7 %collective-permute-start = (bf16[512,256]{1,0:T(8,128)(2,1)S(1)}, bf16[512,256]{1,0:T(8,128)(2,1)S(1)}, u32[]{:S(2)}, u32[]{:S(2)}) collective-permute-start(bf16[512,256]{1,0:T(8,128)(2,1)S(1)} %dynamic-slice_bitcast_fusion.1), channel_id=1, source_target_pairs={{0,5},{1,4},{4,1},{5,0},{2,7},{3,6},{6,3},{7,2},{8,13},{9,12},{12,... | collective-permute-start | bytes 786440 | tf_op jit(solution)/shard_map/ppermute | solution.py:35
  5.6 1.5 %fusion.10 = (s32[1,1]{1,0:T(1,128)}, s32[1,1]{1,0:T(1,128)}, s32[1,1]{1,0:T(1,128)}, s32[1,1]{1,0:T(1,128)}) fusion(s32[1,8]{1,0:T(1,128)} %param.10), kind=kLoop, calls=%fused_computation.44 | loop fusion | bytes 32 | tf_op jit(solution)/shard_map/slice | solution.py:268
  14.8 0.9 constant_dynamic-slice_fusion.8
  15.7 0.9 constant_dynamic-slice_fusion.12
  16.6 1.0 collective-permute-start.1
  17.6 0.8 collective-permute-done.1
  18.5 0.0 collective-permute-done.refs_6_.refs_0_
  18.5 0.1 collective-permute-start.2
  18.6 1.3 dynamic-slice_bitcast_fusion.refs_2_.refs_3_.refs_4_.refs_5_.own
  19.9 0.1 stack.26.refs_0_.place
  20.0 1.2 collective-permute-start.5
  21.2 2.7 %collective-permute-start.4 = (bf16[512,256]{1,0:T(8,128)(2,1)S(1)}, bf16[512,256]{1,0:T(8,128)(2,1)}, u32[]{:S(2)}, u32[]{:S(2)}) collective-permute-start(bf16[512,256]{1,0:T(8,128)(2,1)S(1)} %collective-permute-done.refs_6_.refs_0_), channel_id=1, source_target_pairs={{0,24},{8,0},{16,8},{24,16},{1,25},{9,1},{17,9},{25,17},{2,26},{10... | collective-permute-start | bytes 786440 | tf_op jit(solution)/shard_map/ppermute | solution.py:39
  24.0 1.5 %collective-permute-start.3 = (bf16[512,256]{1,0:T(8,128)(2,1)S(1)}, bf16[512,256]{1,0:T(8,128)(2,1)}, u32[]{:S(2)}, u32[]{:S(2)}) collective-permute-start(bf16[512,256]{1,0:T(8,128)(2,1)S(1)} %collective-permute-done.refs_6_.refs_0_), channel_id=1, source_target_pairs={{0,96},{32,0},{64,32},{96,64},{1,97},{33,1},{65,33},{97,65},{2,98}... | collective-permute-start | bytes 786440 | tf_op jit(solution)/shard_map/ppermute | solution.py:39
  25.4 0.0 collective-permute-done.2
  25.6 0.5 fusion.1
  26.2 0.2 fusion.2
  26.4 2.5 %collective-permute-done.5.refs_9_.refs_3_ = bf16[512,256]{1,0:T(8,128)(2,1)} collective-permute-done((bf16[512,256]{1,0:T(8,128)(2,1)S(1)}, bf16[512,256]{1,0:T(8,128)(2,1)}, u32[]{:S(2)}, u32[]{:S(2)}) %collective-permute-start.5) | collective-permute-done | bytes 262176 | tf_op jit(solution)/shard_map/ppermute | solution.py:39
  28.9 0.1 collective-permute-done.4.refs_8_.refs_2_
  29.0 2.0 %collective-permute-done.3.refs_7_.refs_1_ = bf16[512,256]{1,0:T(8,128)(2,1)} collective-permute-done((bf16[512,256]{1,0:T(8,128)(2,1)S(1)}, bf16[512,256]{1,0:T(8,128)(2,1)}, u32[]{:S(2)}, u32[]{:S(2)}) %collective-permute-start.3) | collective-permute-done | bytes 262176 | tf_op jit(solution)/shard_map/ppermute | solution.py:39
  31.0 5.7 %shard_map.64 = bf16[1088,512]{1,0:T(8,128)(2,1)} custom-call(s32[5]{0:T(128)S(1)} %stack.26.refs_0_.place, bf16[2176,512]{1,0:T(8,128)(2,1)S(1)} %bitcast.29, bf16[512,1024]{1,0:T(8,128)(2,1)S(1)} %dynamic-slice_bitcast_fusion.refs_2_.refs_3_.refs_4_.refs_5_.own, bf16[512,1024]{1,0:T(8,128)(2,1)S(1)} %dynamic-slice_bitcast_fusion.refs_2_.refs_3_.refs_4_.refs_5_.own, ...), custom_call_target="tpu_custom_call" | custom-call | flops 2281701376 | bytes 2097152 | tf_op jit(solution)/shard_map/pallas_call | solution.py:117
  36.8 1.8 %collective-permute-start.6 = (bf16[1088,512]{1,0:T(8,128)(2,1)}, bf16[1088,512]{1,0:T(8,128)(2,1)}, u32[]{:S(2)}, u32[]{:S(2)}) collective-permute-start(bf16[1088,512]{1,0:T(8,128)(2,1)} %shard_map.64), channel_id=1, source_target_pairs={{0,2},{2,0},{1,3},{3,1},{4,6},{6,4},{5,7},{7,5},{8,10},{10,8},{9,1... | collective-permute-start | bytes 3342344 | tf_op jit(solution)/shard_map/ppermute | solution.py:43
  38.5 0.1 constant_dynamic-slice_fusion.4
  38.6 0.6 fusion.9
  42.9 1.0 constant_dynamic-slice_fusion.3
  43.9 0.1 maximum_convert_fusion
  44.0 0.0 collective-permute-done.6.refs_10_
  44.0 5.1 %shard_map.65 = (f32[272,512]{1,0:T(8,128)S(1)}, bf16[272,512]{1,0:T(8,128)(2,1)S(1)}, bf16[272,512]{1,0:T(8,128)(2,1)S(1)}, bf16[272,512]{1,0:T(8,128)(2,1)S(1)}) custom-call(s32[5]{0:T(128)S(1)} %stack.26.refs_0_.place, bf16[2176,512]{1,0:T(8,128)(2,1)S(1)} %bitcast.30, bf16[512,1024]{1,0:T(8,128)(2,1)S(1)} %dynamic-slice_bitcast_fusion.refs_2_.refs_3_.refs_4_.refs_5_.own, ...), custom_call_target="tpu_custom_call" | custom-call | flops 2281701376 | bytes 2097152 | tf_op jit(solution)/shard_map/pallas_call | solution.py:117
  49.0 1.0 collective-permute-start.7
  50.0 0.6 collective-permute-start.8
  50.7 2.3 %collective-permute-start.9 = (bf16[272,512]{1,0:T(8,128)(2,1)S(1)}, bf16[272,512]{1,0:T(8,128)(2,1)S(1)}, u32[]{:S(2)}, u32[]{:S(2)}) collective-permute-start(bf16[272,512]{1,0:T(8,128)(2,1)S(1)} %get-tuple-element.38), channel_id=1, source_target_pairs={{0,5},{4,0},{1,4},{5,1},{2,7},{6,2},{3,6},{7,3},{8,13},{12,8},{9,1... | collective-permute-start | bytes 835592 | tf_op jit(solution)/shard_map/ppermute | solution.py:31
  53.0 6.8 %shard_map.66 = (bf16[2176,1024]{1,0:T(8,128)(2,1)S(1)}, bf16[2176,1024]{1,0:T(8,128)(2,1)S(1)}, f32[128,1024]{1,0:T(8,128)S(1)}) custom-call(s32[5]{0:T(128)S(1)} %stack.26.refs_0_.place, bf16[2176,512]{1,0:T(8,128)(2,1)S(1)} %bitcast.31, bf16[512,1024]{1,0:T(8,128)(2,1)S(1)} %dynamic-slice_bitcast_fusion.refs_2_.refs_3_.refs_4_.refs_5_.own, ...), custom_call_target="tpu_custom_call" | custom-call | flops 2281701376 | bytes 2097152 | tf_op jit(solution)/shard_map/pallas_call | solution.py:163
  59.8 5.5 %collective-permute-done.8 = bf16[272,512]{1,0:T(8,128)(2,1)S(1)} collective-permute-done((bf16[272,512]{1,0:T(8,128)(2,1)S(1)}, bf16[272,512]{1,0:T(8,128)(2,1)S(1)}, u32[]{:S(2)}, u32[]{:S(2)}) %collective-permute-start.8) | collective-permute-done | bytes 278560 | tf_op jit(solution)/shard_map/ppermute | solution.py:31
  65.2 0.2 multiply_convert_fusion.refs_4_
  65.4 1.5 %collective-permute-start.12 = (bf16[272,512]{1,0:T(8,128)(2,1)S(1)}, bf16[272,512]{1,0:T(8,128)(2,1)S(1)}, u32[]{:S(2)}, u32[]{:S(2)}) collective-permute-start(bf16[272,512]{1,0:T(8,128)(2,1)S(1)} %multiply_convert_fusion.refs_4_), channel_id=1, source_target_pairs={{0,4},{4,1},{1,5},{5,0},{2,6},{6,3},{3,7},{7,2},{8,12},{12,9},{9,1... | collective-permute-start | bytes 835592 | tf_op jit(solution)/shard_map/ppermute | solution.py:31
  66.9 0.6 collective-permute-start.11
  67.5 1.9 %collective-permute-start.10 = (bf16[272,512]{1,0:T(8,128)(2,1)S(1)}, bf16[272,512]{1,0:T(8,128)(2,1)S(1)}, u32[]{:S(2)}, u32[]{:S(2)}) collective-permute-start(bf16[272,512]{1,0:T(8,128)(2,1)S(1)} %multiply_convert_fusion.refs_4_), channel_id=1, source_target_pairs={{0,5},{4,0},{1,4},{5,1},{2,7},{6,2},{3,6},{7,3},{8,13},{12,8},{9,1... | collective-permute-start | bytes 835592 | tf_op jit(solution)/shard_map/ppermute | solution.py:31
  69.4 1.5 %collective-permute-start.13 = (bf16[272,512]{1,0:T(8,128)(2,1)S(1)}, bf16[272,512]{1,0:T(8,128)(2,1)S(1)}, u32[]{:S(2)}, u32[]{:S(2)}) collective-permute-start(bf16[272,512]{1,0:T(8,128)(2,1)S(1)} %multiply_convert_fusion.refs_4_), channel_id=1, source_target_pairs={{0,2},{2,0},{1,3},{3,1},{4,6},{6,4},{5,7},{7,5},{8,10},{10,8},{9,1... | collective-permute-start | bytes 835592 | tf_op jit(solution)/shard_map/ppermute | solution.py:43
  70.9 4.2 %collective-permute-done.12.refs_7_ = bf16[272,512]{1,0:T(8,128)(2,1)S(1)} collective-permute-done((bf16[272,512]{1,0:T(8,128)(2,1)S(1)}, bf16[272,512]{1,0:T(8,128)(2,1)S(1)}, u32[]{:S(2)}, u32[]{:S(2)}) %collective-permute-start.12) | collective-permute-done | bytes 278560 | tf_op jit(solution)/shard_map/ppermute | solution.py:31
  75.1 6.6 %collective-permute-start.16 = (bf16[272,512]{1,0:T(8,128)(2,1)S(1)}, bf16[272,512]{1,0:T(8,128)(2,1)S(1)}, u32[]{:S(2)}, u32[]{:S(2)}) collective-permute-start(bf16[272,512]{1,0:T(8,128)(2,1)S(1)} %collective-permute-done.12.refs_7_), channel_id=1, source_target_pairs={{0,2},{2,0},{1,3},{3,1},{4,6},{6,4},{5,7},{7,5},{8,10},{10,8},{9,1... | collective-permute-start | bytes 835592 | tf_op jit(solution)/shard_map/ppermute | solution.py:43
  81.7 0.0 collective-permute-start.15
  81.7 0.6 collective-permute-start.14
  82.4 0.6 collective-permute-done.16.refs_11_
  82.9 0.4 collective-permute-done.15.refs_10_
  83.3 0.4 collective-permute-done.14.refs_9_
  83.7 11.2 %shard_map.67 = bf16[64,2,8,1024]{3,2,1,0:T(8,128)(2,1)S(1)} custom-call(s32[5]{0:T(128)S(1)} %stack.26.refs_0_.place, bf16[2176,512]{1,0:T(8,128)(2,1)S(1)} %bitcast.32, bf16[2176,1024]{1,0:T(8,128)(2,1)S(1)} %get-tuple-element.43.picked, bf16[2176,1024]{1,0:T(8,128)(2,1)S(1)} %get-tuple-element.44.tangents, f32[128,1024]{1,0:T(8,128)S(1)} %get-tuple-element.45.linears, ...), custom_call_target="tpu_custom_call" | custom-call | flops 6845104128 | bytes 2097152 | tf_op jit(solution)/shard_map/pallas_call | solution.py:219
  94.9 36.2 %all_to_all.5 = bf16[128,8,1024]{2,1,0:T(8,128)(2,1)S(1)} all-to-all(bf16[128,8,1024]{2,1,0:T(8,128)(2,1)S(1)} %bitcast.34), channel_id=1, replica_groups=mesh['x'=4,'y'=4,'zl'=2,'core'=2,'zh'=2] {'x','y','zl','core','zh'}, dimensions={0} | all-to-all | bytes 4194304 | tf_op jit(solution)/shard_map/all_to_all | solution.py:335
  131.1 1.6 %shard_map.68 = f32[1,8,8192]{2,1,0:T(8,128)} custom-call(bf16[16,8,8,1024]{3,2,1,0:T(8,128)(2,1)S(1)} %bitcast.33), custom_call_target="tpu_custom_call" | custom-call | tf_op jit(solution)/shard_map/pallas_call | solution.py:255
  (25 shorter events, 0.3 us)
Async XLA Ops:
  1.0 17.5 %collective-permute-start = (bf16[512,256]{1,0:T(8,128)(2,1)S(1)}, bf16[512,256]{1,0:T(8,128)(2,1)S(1)}, u32[]{:S(2)}, u32[]{:S(2)}) collective-permute-start(bf16[512,256]{1,0:T(8,128)(2,1)S(1)} %dynamic-slice_bitcast_fusion.1), channel_id=1, source_target_pairs={{0,5},{1,4},{4,1},{5,0},{2,7},{3,6},{6,3},{7,2},{8,13},{9,12},{12,... | collective-permute-start | bytes 786440 | tf_op jit(solution)/shard_map/ppermute | solution.py:35
  16.6 1.9 %collective-permute-start.1 = (f32[4,640]{1,0:T(4,128)S(1)}, f32[4,640]{1,0:T(4,128)S(1)}, u32[]{:S(2)}, u32[]{:S(2)}) collective-permute-start(f32[4,640]{1,0:T(4,128)S(1)} %pad_maximum_fusion.3), channel_id=1, source_target_pairs={{0,2},{2,0},{1,3},{3,1},{4,6},{6,4},{5,7},{7,5},{8,10},{10,8},{9,1... | collective-permute-start | bytes 30728 | tf_op jit(solution)/shard_map/ppermute | solution.py:43
  18.5 7.0 %collective-permute-start.2 = (f32[8,640]{1,0:T(8,128)S(1)}, f32[8,640]{1,0:T(8,128)S(1)}, u32[]{:S(2)}, u32[]{:S(2)}) collective-permute-start(f32[8,640]{1,0:T(8,128)S(1)} %pad_maximum_fusion.2), channel_id=1, source_target_pairs={{0,4},{4,0},{1,5},{5,1},{2,6},{6,2},{3,7},{7,3},{8,12},{12,8},{9,1... | collective-permute-start | bytes 61448 | tf_op jit(solution)/shard_map/ppermute | solution.py:300
  20.0 8.8 %collective-permute-start.5 = (bf16[512,256]{1,0:T(8,128)(2,1)S(1)}, bf16[512,256]{1,0:T(8,128)(2,1)}, u32[]{:S(2)}, u32[]{:S(2)}) collective-permute-start(bf16[512,256]{1,0:T(8,128)(2,1)S(1)} %collective-permute-done.refs_6_.refs_0_), channel_id=1, source_target_pairs={{0,32},{32,64},{64,96},{96,0},{1,33},{33,65},{65,97},{97,1},{2,34}... | collective-permute-start | bytes 786440 | tf_op jit(solution)/shard_map/ppermute | solution.py:39
  21.2 7.8 %collective-permute-start.4 = (bf16[512,256]{1,0:T(8,128)(2,1)S(1)}, bf16[512,256]{1,0:T(8,128)(2,1)}, u32[]{:S(2)}, u32[]{:S(2)}) collective-permute-start(bf16[512,256]{1,0:T(8,128)(2,1)S(1)} %collective-permute-done.refs_6_.refs_0_), channel_id=1, source_target_pairs={{0,24},{8,0},{16,8},{24,16},{1,25},{9,1},{17,9},{25,17},{2,26},{10... | collective-permute-start | bytes 786440 | tf_op jit(solution)/shard_map/ppermute | solution.py:39
  24.0 7.1 %collective-permute-start.3 = (bf16[512,256]{1,0:T(8,128)(2,1)S(1)}, bf16[512,256]{1,0:T(8,128)(2,1)}, u32[]{:S(2)}, u32[]{:S(2)}) collective-permute-start(bf16[512,256]{1,0:T(8,128)(2,1)S(1)} %collective-permute-done.refs_6_.refs_0_), channel_id=1, source_target_pairs={{0,96},{32,0},{64,32},{96,64},{1,97},{33,1},{65,33},{97,65},{2,98}... | collective-permute-start | bytes 786440 | tf_op jit(solution)/shard_map/ppermute | solution.py:39
  31.0 7.5 %copy-start = (s32[1,8]{1,0:T(1,128)S(1)}, s32[1,8]{1,0:T(1,128)}, u32[]{:S(2)}) copy-start(s32[1,8]{1,0:T(1,128)} %param.10) | copy-start | bytes 100
  31.0 11.8 %copy-start.1 = (bf16[8,512]{1,0:T(8,128)(2,1)S(1)}, bf16[8,512]{1,0:T(8,128)(2,1)}, u32[]{:S(2)}) copy-start(bf16[8,512]{1,0:T(8,128)(2,1)} %param.7) | copy-start | bytes 24580
  36.8 7.2 %collective-permute-start.6 = (bf16[1088,512]{1,0:T(8,128)(2,1)}, bf16[1088,512]{1,0:T(8,128)(2,1)}, u32[]{:S(2)}, u32[]{:S(2)}) collective-permute-start(bf16[1088,512]{1,0:T(8,128)(2,1)} %shard_map.64), channel_id=1, source_target_pairs={{0,2},{2,0},{1,3},{3,1},{4,6},{6,4},{5,7},{7,5},{8,10},{10,8},{9,1... | collective-permute-start | bytes 3342344 | tf_op jit(solution)/shard_map/ppermute | solution.py:43
  49.0 10.7 %collective-permute-start.7 = (bf16[272,512]{1,0:T(8,128)(2,1)S(1)}, bf16[272,512]{1,0:T(8,128)(2,1)S(1)}, u32[]{:S(2)}, u32[]{:S(2)}) collective-permute-start(bf16[272,512]{1,0:T(8,128)(2,1)S(1)} %get-tuple-element.36), channel_id=1, source_target_pairs={{0,1},{4,5},{1,0},{5,4},{2,3},{6,7},{3,2},{7,6},{8,9},{12,13},{9,8... | collective-permute-start | bytes 835592 | tf_op jit(solution)/shard_map/ppermute | solution.py:31
  50.0 15.2 %collective-permute-start.8 = (bf16[272,512]{1,0:T(8,128)(2,1)S(1)}, bf16[272,512]{1,0:T(8,128)(2,1)S(1)}, u32[]{:S(2)}, u32[]{:S(2)}) collective-permute-start(bf16[272,512]{1,0:T(8,128)(2,1)S(1)} %get-tuple-element.37), channel_id=1, source_target_pairs={{0,4},{4,1},{1,5},{5,0},{2,6},{6,3},{3,7},{7,2},{8,12},{12,9},{9,1... | collective-permute-start | bytes 835592 | tf_op jit(solution)/shard_map/ppermute | solution.py:31
  50.7 14.6 %collective-permute-start.9 = (bf16[272,512]{1,0:T(8,128)(2,1)S(1)}, bf16[272,512]{1,0:T(8,128)(2,1)S(1)}, u32[]{:S(2)}, u32[]{:S(2)}) collective-permute-start(bf16[272,512]{1,0:T(8,128)(2,1)S(1)} %get-tuple-element.38), channel_id=1, source_target_pairs={{0,5},{4,0},{1,4},{5,1},{2,7},{6,2},{3,6},{7,3},{8,13},{12,8},{9,1... | collective-permute-start | bytes 835592 | tf_op jit(solution)/shard_map/ppermute | solution.py:31
  65.4 9.7 %collective-permute-start.12 = (bf16[272,512]{1,0:T(8,128)(2,1)S(1)}, bf16[272,512]{1,0:T(8,128)(2,1)S(1)}, u32[]{:S(2)}, u32[]{:S(2)}) collective-permute-start(bf16[272,512]{1,0:T(8,128)(2,1)S(1)} %multiply_convert_fusion.refs_4_), channel_id=1, source_target_pairs={{0,4},{4,1},{1,5},{5,0},{2,6},{6,3},{3,7},{7,2},{8,12},{12,9},{9,1... | collective-permute-start | bytes 835592 | tf_op jit(solution)/shard_map/ppermute | solution.py:31
  66.9 14.8 %collective-permute-start.11 = (bf16[272,512]{1,0:T(8,128)(2,1)S(1)}, bf16[272,512]{1,0:T(8,128)(2,1)S(1)}, u32[]{:S(2)}, u32[]{:S(2)}) collective-permute-start(bf16[272,512]{1,0:T(8,128)(2,1)S(1)} %multiply_convert_fusion.refs_4_), channel_id=1, source_target_pairs={{0,1},{4,5},{1,0},{5,4},{2,3},{6,7},{3,2},{7,6},{8,9},{12,13},{9,8... | collective-permute-start | bytes 835592 | tf_op jit(solution)/shard_map/ppermute | solution.py:31
  67.5 14.2 %collective-permute-start.10 = (bf16[272,512]{1,0:T(8,128)(2,1)S(1)}, bf16[272,512]{1,0:T(8,128)(2,1)S(1)}, u32[]{:S(2)}, u32[]{:S(2)}) collective-permute-start(bf16[272,512]{1,0:T(8,128)(2,1)S(1)} %multiply_convert_fusion.refs_4_), channel_id=1, source_target_pairs={{0,5},{4,0},{1,4},{5,1},{2,7},{6,2},{3,6},{7,3},{8,13},{12,8},{9,1... | collective-permute-start | bytes 835592 | tf_op jit(solution)/shard_map/ppermute | solution.py:31
  69.4 13.0 %collective-permute-start.13 = (bf16[272,512]{1,0:T(8,128)(2,1)S(1)}, bf16[272,512]{1,0:T(8,128)(2,1)S(1)}, u32[]{:S(2)}, u32[]{:S(2)}) collective-permute-start(bf16[272,512]{1,0:T(8,128)(2,1)S(1)} %multiply_convert_fusion.refs_4_), channel_id=1, source_target_pairs={{0,2},{2,0},{1,3},{3,1},{4,6},{6,4},{5,7},{7,5},{8,10},{10,8},{9,1... | collective-permute-start | bytes 835592 | tf_op jit(solution)/shard_map/ppermute | solution.py:43
  75.1 7.8 %collective-permute-start.16 = (bf16[272,512]{1,0:T(8,128)(2,1)S(1)}, bf16[272,512]{1,0:T(8,128)(2,1)S(1)}, u32[]{:S(2)}, u32[]{:S(2)}) collective-permute-start(bf16[272,512]{1,0:T(8,128)(2,1)S(1)} %collective-permute-done.12.refs_7_), channel_id=1, source_target_pairs={{0,2},{2,0},{1,3},{3,1},{4,6},{6,4},{5,7},{7,5},{8,10},{10,8},{9,1... | collective-permute-start | bytes 835592 | tf_op jit(solution)/shard_map/ppermute | solution.py:43
  81.7 1.6 %collective-permute-start.15 = (bf16[272,512]{1,0:T(8,128)(2,1)S(1)}, bf16[272,512]{1,0:T(8,128)(2,1)S(1)}, u32[]{:S(2)}, u32[]{:S(2)}) collective-permute-start(bf16[272,512]{1,0:T(8,128)(2,1)S(1)} %collective-permute-done.11.refs_6_), channel_id=1, source_target_pairs={{0,2},{2,0},{1,3},{3,1},{4,6},{6,4},{5,7},{7,5},{8,10},{10,8},{9,1... | collective-permute-start | bytes 835592 | tf_op jit(solution)/shard_map/ppermute | solution.py:43
  81.7 2.0 %collective-permute-start.14 = (bf16[272,512]{1,0:T(8,128)(2,1)S(1)}, bf16[272,512]{1,0:T(8,128)(2,1)S(1)}, u32[]{:S(2)}, u32[]{:S(2)}) collective-permute-start(bf16[272,512]{1,0:T(8,128)(2,1)S(1)} %collective-permute-done.10.refs_5_), channel_id=1, source_target_pairs={{0,2},{2,0},{1,3},{3,1},{4,6},{6,4},{5,7},{7,5},{8,10},{10,8},{9,1... | collective-permute-start | bytes 835592 | tf_op jit(solution)/shard_map/ppermute | solution.py:43

commit v6 on v5

--- a/solution.py
+++ b/solution.py
@@ -264,9 +264,54 @@
     )(pieces)
 
 
-def rows_at(array, order, places):
-    picked = [lax.dynamic_slice_in_dim(array, order[k], 1, 0) for k in places]
-    return jnp.concatenate(picked, axis=0)
+def pick_kernel(order, place, samples, directions, targets, target_jac, packed, wanted):
+    def chosen(rows, at):
+        total = jnp.zeros_like(rows[0:1])
+        for j in range(8):
+            total = jnp.where(order[at] == j, rows[j : j + 1], total)
+        return total
+
+    step = pl.program_id(0)
+
+    @pl.when(step == 0)
+    def _():
+        inputs = samples[...].astype(f32)
+        places = directions[...].astype(f32)
+        packed[:, :REDUCED] = jnp.concatenate([chosen(inputs, k) for k in range(MICRO)], axis=0)
+        packed[:, REDUCED:] = jnp.concatenate([chosen(places, k) for k in range(MICRO)], axis=0)
+        outputs = targets[...].astype(f32)
+        own = [chosen(outputs, place[4] * 2 + k) for k in range(2)]
+        wanted[2 * TANGENTS :, :] = jnp.concatenate([*own, jnp.zeros((14, REDUCED), f32)], axis=0)
+
+    wanted[pl.ds(pl.multiple_of(step * TANGENTS, TANGENTS), TANGENTS), :] = target_jac[0].astype(f32)
+
+
+def pick(order, place, samples, directions, targets, jacobian_targets):
+    whole = lambda shape: pl.BlockSpec(shape, lambda i, order, place: (0, 0))
+    return pl.pallas_call(
+        pick_kernel,
+        grid_spec=pltpu.PrefetchScalarGridSpec(
+            num_scalar_prefetch=2,
+            grid=(2,),
+            in_specs=[
+                whole((8, REDUCED)),
+                whole((8, TANGENTS)),
+                whole((8, REDUCED)),
+                pl.BlockSpec(
+                    (1, TANGENTS, REDUCED),
+                    lambda i, order, place: (order[place[4] * 2 + i], 0, 0),
+                ),
+            ],
+            out_specs=[whole((MICRO, REDUCED + TANGENTS)), whole((CHUNK, REDUCED))],
+        ),
+        out_shape=[
+            jax.ShapeDtypeStruct((MICRO, REDUCED + TANGENTS), f32),
+            jax.ShapeDtypeStruct((CHUNK, REDUCED), f32),
+        ],
+        compiler_params=pltpu.CompilerParams(
+            dimension_semantics=("arbitrary",), vmem_limit_bytes=LIMIT
+        ),
+    )(order, place, samples, directions, targets, jacobian_targets)
 
 
 def shards(samples, targets, jacobian_targets, directions, plan, weights):
@@ -284,10 +329,9 @@
     direct = z_facing(quarter)
     own = lax.dynamic_slice_in_dim(weight, mine * COLS, COLS, 1)
 
-    order = plan[0, :MICRO]
-    inputs = rows_at(samples, order, range(MICRO)).astype(f32)
-    chosen = rows_at(directions, order, range(MICRO)).astype(f32)
-    packed = jnp.concatenate([inputs, chosen], axis=1)
+    packed, wanted = pick(
+        plan.reshape(8), place, samples, directions, targets, jacobian_targets
+    )
     swapped = core_swap(packed)
     direct, packed, swapped = lax.optimization_barrier((direct, packed, swapped))
     other = [
@@ -308,15 +352,7 @@
     inputs = jnp.pad(small[:, :, :REDUCED].astype(bf16), ((0, 0), (0, 14), (0, 0)))
     rows = jnp.concatenate([onehot, inputs], axis=1).reshape(2 * GROUP, REDUCED)
 
-    own_order = lax.dynamic_slice_in_dim(order, zh * 2, 2)
-    target_rows = rows_at(targets, own_order, range(2)).astype(f32)
-    target_jac = rows_at(jacobian_targets, own_order, range(2)).reshape(2 * TANGENTS, REDUCED)
-    wanted = jnp.concatenate(
-        [target_jac.astype(f32), jnp.pad(target_rows, ((0, 14), (0, 0)))], axis=0
-    )
-
     from_core = core_swap(forward(place, rows, own, other))
-    from_core, wanted = lax.optimization_barrier((from_core, wanted))
     chunks = forward(place, rows, own, other, from_core)
     chunks, ready = lax.optimization_barrier((chunks, rows))
     got = [z_shift(chunks[d], d) for d in (2, 1, 3)]

time: 133 us -> 120 us (0.902)
  between operations: 11.6 us -> 0.17 us
  waiting for transfers between devices: 16.6 us -> 21.1 us
  Pallas kernels: 30.4 us -> 26 us
    unnamed x5 -> x11, local copies, waits for them, and re-layouts: 0.01 us -> 3.96 us
    pallas_call x2, Pallas kernels: 10.8 us -> 7.58 us  [forward(): pl.pallas_call(lambda *refs: forward_kernel(final, *refs), grid_spec=pltp...]
    ppermute x6, starting transfers between devices: 11.5 us -> 8.48 us  [core_swap(): return lax.ppermute(block, 'core', [(0, 1), (1, 0)])]
    dynamic_slice x5 -> x0, local copies, waits for them, and re-layouts: 2.78 us -> none  [the longest x4 2.71 us: rows_at(): picked = [lax.dynamic_slice_in_dim(array, order[k], 1, 0) for k in places]]
    ppermute x6, waiting for transfers between devices: 9.69 us -> 12.4 us  [z_shift(): lax.ppermute(block, Z, [(z_index(z), z_index((z + d) % 4)) for z in range...]
    ppermute x6, waiting for transfers between devices: 2.19 us -> 4.42 us  [core_swap(): return lax.ppermute(block, 'core', [(0, 1), (1, 0)])]
    slice x2 -> x0, local copies, waits for them, and re-layouts: 2.05 us -> none  [rows_at(): picked = [lax.dynamic_slice_in_dim(array, order[k], 1, 0) for k in places]]
    ppermute x6, starting transfers between devices: 7.89 us -> 9.68 us  [z_shift(): lax.ppermute(block, Z, [(z_index(z), z_index((z + d) % 4)) for z in range...]
  transfers between devices with their start and end apart: 17 -> 17, of which waited for: 9 -> 10; matrix products, arithmetic and copies ran while one was open for 5% -> 2% of each run, Pallas kernels for 5% -> 5%
where the time goes in v6:
time: 120 us; the launch traced here: 119 us
  blocking collectives  36.4 us (30%)
  starting transfers between devices  28.4 us (24%)
  Pallas kernels  26 us (22%)
  waiting for transfers between devices  21.1 us (18%)
  local copies, waits for them, and re-layouts  6.36 us (5%)
    all_to_all x1, blocking collectives, shards(): lax.all_to_all(sent.reshape(128, 8, COLS), AXES, split_axis=0, concat_axi...  36.4 us
    ppermute x6, waiting for transfers between devices, z_shift(): lax.ppermute(block, Z, [(z_index(z), z_index((z + d) % 4)) for z in range...  12.4 us
    pallas_call x1, Pallas kernels, backward(): pl.pallas_call(backward_kernel, grid_spec=pltpu.PrefetchScalarGridSpec(nu...  10.4 us
    ppermute x6, starting transfers between devices, z_shift(): lax.ppermute(block, Z, [(z_index(z), z_index((z + d) % 4)) for z in range...  9.68 us
    ppermute x6, starting transfers between devices, core_swap(): return lax.ppermute(block, 'core', [(0, 1), (1, 0)])  8.48 us
    pallas_call x2, Pallas kernels, forward(): pl.pallas_call(lambda *refs: forward_kernel(final, *refs), grid_spec=pltp...  7.58 us
    pallas_call x1, Pallas kernels, prepare(): pl.pallas_call(prepare_kernel, grid_spec=pltpu.PrefetchScalarGridSpec(num...  5.66 us
    ppermute x3, starting transfers between devices, ring_shift(): return lax.ppermute(block, axis, [(i, (i + d) % 4) for i in range(4)])  5.48 us
  transfers between devices with their start and end apart: 17, of which 10 were waited for; matrix products, arithmetic and copies ran while one was open for 2% of the time, Pallas kernels for 5%

profile of v6, /device:TPU:1, one launch (start us, length us, event | category | flops | bytes accessed | tf_op | source)
XLA Modules:
  0.0 119.3 jit_solution(13226382912522647016)
XLA Ops:
  0.0 1.0 dynamic-slice_bitcast_fusion.1
  1.0 4.7 %collective-permute-start = (bf16[512,256]{1,0:T(8,128)(2,1)S(1)}, bf16[512,256]{1,0:T(8,128)(2,1)S(1)}, u32[]{:S(2)}, u32[]{:S(2)}) collective-permute-start(bf16[512,256]{1,0:T(8,128)(2,1)S(1)} %dynamic-slice_bitcast_fusion.1), channel_id=1, source_target_pairs={{0,5},{1,4},{4,1},{5,0},{2,7},{3,6},{6,3},{7,2},{8,13},{9,12},{12,... | collective-permute-start | bytes 786440 | tf_op jit(solution)/shard_map/ppermute | solution.py:35
  5.6 0.1 stack.26.place.refs_0_
  5.7 1.2 %copy-done = bf16[8,128,512]{2,1,0:T(8,128)(2,1)S(1)} copy-done((bf16[8,128,512]{2,1,0:T(8,128)(2,1)S(1)}, bf16[8,128,512]{2,1,0:T(8,128)(2,1)}, u32[]{:S(2)}) %copy-start) | copy-done | bytes 1048600
  6.9 0.7 copy-done.1
  7.6 0.7 copy-done.2
  8.3 0.7 copy-done.3
  9.0 0.7 copy-done.4
  9.7 0.7 shard_map.64
  10.4 1.0 collective-permute-start.1
  11.4 0.8 collective-permute-done.1
  12.3 0.1 collective-permute-start.2
  12.4 1.3 %dynamic-slice_bitcast_fusion.refs_2_.refs_3_.refs_4_.refs_5_.own = bf16[512,1024]{1,0:T(8,128)(2,1)S(1)} fusion(bf16[1,512,8192]{2,1,0:T(8,128)(2,1)} %param.11, s32[]{:T(128)S(6)} %select_n.63), kind=kLoop, calls=%fused_computation.5 | loop fusion | bytes 2097156 | tf_op jit(solution)/shard_map/dynamic_slice | solution.py:330
  13.7 1.3 %collective-permute-start.5 = (bf16[512,256]{1,0:T(8,128)(2,1)S(1)}, bf16[512,256]{1,0:T(8,128)(2,1)S(1)}, u32[]{:S(2)}, u32[]{:S(2)}) collective-permute-start(bf16[512,256]{1,0:T(8,128)(2,1)S(1)} %collective-permute-done.refs_6_.refs_0_), channel_id=1, source_target_pairs={{0,32},{32,64},{64,96},{96,0},{1,33},{33,65},{65,97},{97,1},{2,34}... | collective-permute-start | bytes 786440 | tf_op jit(solution)/shard_map/ppermute | solution.py:39
  15.0 2.7 %collective-permute-start.4 = (bf16[512,256]{1,0:T(8,128)(2,1)S(1)}, bf16[512,256]{1,0:T(8,128)(2,1)S(1)}, u32[]{:S(2)}, u32[]{:S(2)}) collective-permute-start(bf16[512,256]{1,0:T(8,128)(2,1)S(1)} %collective-permute-done.refs_6_.refs_0_), channel_id=1, source_target_pairs={{0,24},{8,0},{16,8},{24,16},{1,25},{9,1},{17,9},{25,17},{2,26},{10... | collective-permute-start | bytes 786440 | tf_op jit(solution)/shard_map/ppermute | solution.py:39
  17.7 1.5 %collective-permute-start.3 = (bf16[512,256]{1,0:T(8,128)(2,1)S(1)}, bf16[512,256]{1,0:T(8,128)(2,1)S(1)}, u32[]{:S(2)}, u32[]{:S(2)}) collective-permute-start(bf16[512,256]{1,0:T(8,128)(2,1)S(1)} %collective-permute-done.refs_6_.refs_0_), channel_id=1, source_target_pairs={{0,96},{32,0},{64,32},{96,64},{1,97},{33,1},{65,33},{97,65},{2,98}... | collective-permute-start | bytes 786440 | tf_op jit(solution)/shard_map/ppermute | solution.py:39
  19.2 0.0 collective-permute-done.2
  19.4 0.5 fusion.1
  19.9 0.2 fusion.2
  20.1 2.1 %collective-permute-done.5.refs_9_.refs_3_ = bf16[512,256]{1,0:T(8,128)(2,1)S(1)} collective-permute-done((bf16[512,256]{1,0:T(8,128)(2,1)S(1)}, bf16[512,256]{1,0:T(8,128)(2,1)S(1)}, u32[]{:S(2)}, u32[]{:S(2)}) %collective-permute-start.5) | collective-permute-done | bytes 262176 | tf_op jit(solution)/shard_map/ppermute | solution.py:39
  22.2 0.3 collective-permute-done.4.refs_8_.refs_2_
  22.5 1.9 %collective-permute-done.3.refs_7_.refs_1_ = bf16[512,256]{1,0:T(8,128)(2,1)S(1)} collective-permute-done((bf16[512,256]{1,0:T(8,128)(2,1)S(1)}, bf16[512,256]{1,0:T(8,128)(2,1)S(1)}, u32[]{:S(2)}, u32[]{:S(2)}) %collective-permute-start.3) | collective-permute-done | bytes 262176 | tf_op jit(solution)/shard_map/ppermute | solution.py:39
  24.4 3.7 %shard_map.65 = bf16[1088,512]{1,0:T(8,128)(2,1)S(1)} custom-call(s32[5]{0:T(128)S(1)} %stack.26.place.refs_0_, bf16[2176,512]{1,0:T(8,128)(2,1)S(1)} %bitcast.22, bf16[512,1024]{1,0:T(8,128)(2,1)S(1)} %dynamic-slice_bitcast_fusion.refs_2_.refs_3_.refs_4_.refs_5_.own, bf16[512,1024]{1,0:T(8,128)(2,1)S(1)} %dynamic-slice_bitcast_fusion.refs_2_.refs_3_.refs_4_.refs_5_.own, ...), custom_call_target="tpu_custom_call" | custom-call | flops 2281701376 | bytes 2097152 | tf_op jit(solution)/shard_map/pallas_call | solution.py:117
  28.1 2.1 %collective-permute-start.6 = (bf16[1088,512]{1,0:T(8,128)(2,1)S(1)}, bf16[1088,512]{1,0:T(8,128)(2,1)S(1)}, u32[]{:S(2)}, u32[]{:S(2)}) collective-permute-start(bf16[1088,512]{1,0:T(8,128)(2,1)S(1)} %shard_map.65), channel_id=1, source_target_pairs={{0,2},{2,0},{1,3},{3,1},{4,6},{6,4},{5,7},{7,5},{8,10},{10,8},{9,1... | collective-permute-start | bytes 3342344 | tf_op jit(solution)/shard_map/ppermute | solution.py:43
  30.3 2.4 %collective-permute-done.6.refs_10_ = bf16[1088,512]{1,0:T(8,128)(2,1)S(1)} collective-permute-done((bf16[1088,512]{1,0:T(8,128)(2,1)S(1)}, bf16[1088,512]{1,0:T(8,128)(2,1)S(1)}, u32[]{:S(2)}, u32[]{:S(2)}) %collective-permute-start.6) | collective-permute-done | bytes 1114144 | tf_op jit(solution)/shard_map/ppermute | solution.py:43
  32.6 3.8 %shard_map.66 = (f32[272,512]{1,0:T(8,128)S(1)}, bf16[272,512]{1,0:T(8,128)(2,1)S(1)}, bf16[272,512]{1,0:T(8,128)(2,1)S(1)}, bf16[272,512]{1,0:T(8,128)(2,1)S(1)}) custom-call(s32[5]{0:T(128)S(1)} %stack.26.place.refs_0_, bf16[2176,512]{1,0:T(8,128)(2,1)S(1)} %bitcast.23, bf16[512,1024]{1,0:T(8,128)(2,1)S(1)} %dynamic-slice_bitcast_fusion.refs_2_.refs_3_.refs_4_.refs_5_.own, ...), custom_call_target="tpu_custom_call" | custom-call | flops 2281701376 | bytes 2097152 | tf_op jit(solution)/shard_map/pallas_call | solution.py:117
  36.5 3.0 %collective-permute-start.7 = (bf16[272,512]{1,0:T(8,128)(2,1)S(1)}, bf16[272,512]{1,0:T(8,128)(2,1)S(1)}, u32[]{:S(2)}, u32[]{:S(2)}) collective-permute-start(bf16[272,512]{1,0:T(8,128)(2,1)S(1)} %get-tuple-element.36), channel_id=1, source_target_pairs={{0,1},{4,5},{1,0},{5,4},{2,3},{6,7},{3,2},{7,6},{8,9},{12,13},{9,8... | collective-permute-start | bytes 835592 | tf_op jit(solution)/shard_map/ppermute | solution.py:31
  39.5 0.0 collective-permute-start.8
  39.5 2.7 %collective-permute-start.9 = (bf16[272,512]{1,0:T(8,128)(2,1)S(1)}, bf16[272,512]{1,0:T(8,128)(2,1)S(1)}, u32[]{:S(2)}, u32[]{:S(2)}) collective-permute-start(bf16[272,512]{1,0:T(8,128)(2,1)S(1)} %get-tuple-element.38), channel_id=1, source_target_pairs={{0,5},{4,0},{1,4},{5,1},{2,7},{6,2},{3,6},{7,3},{8,13},{12,8},{9,1... | collective-permute-start | bytes 835592 | tf_op jit(solution)/shard_map/ppermute | solution.py:31
  42.2 5.7 %shard_map.67 = (bf16[2176,1024]{1,0:T(8,128)(2,1)S(1)}, bf16[2176,1024]{1,0:T(8,128)(2,1)S(1)}, f32[128,1024]{1,0:T(8,128)S(1)}) custom-call(s32[5]{0:T(128)S(1)} %stack.26.place.refs_0_, bf16[2176,512]{1,0:T(8,128)(2,1)S(1)} %bitcast.24, bf16[512,1024]{1,0:T(8,128)(2,1)S(1)} %dynamic-slice_bitcast_fusion.refs_2_.refs_3_.refs_4_.refs_5_.own, ...), custom_call_target="tpu_custom_call" | custom-call | flops 2281701376 | bytes 2097152 | tf_op jit(solution)/shard_map/pallas_call | solution.py:163
  47.9 4.8 %collective-permute-done.8 = bf16[272,512]{1,0:T(8,128)(2,1)S(1)} collective-permute-done((bf16[272,512]{1,0:T(8,128)(2,1)S(1)}, bf16[272,512]{1,0:T(8,128)(2,1)S(1)}, u32[]{:S(2)}, u32[]{:S(2)}) %collective-permute-start.8) | collective-permute-done | bytes 278560 | tf_op jit(solution)/shard_map/ppermute | solution.py:31
  52.6 0.0 collective-permute-done.9
  52.6 0.2 multiply_convert_fusion.refs_4_
  52.8 1.5 %collective-permute-start.12 = (bf16[272,512]{1,0:T(8,128)(2,1)S(1)}, bf16[272,512]{1,0:T(8,128)(2,1)S(1)}, u32[]{:S(2)}, u32[]{:S(2)}) collective-permute-start(bf16[272,512]{1,0:T(8,128)(2,1)S(1)} %multiply_convert_fusion.refs_4_), channel_id=1, source_target_pairs={{0,4},{4,1},{1,5},{5,0},{2,6},{6,3},{3,7},{7,2},{8,12},{12,9},{9,1... | collective-permute-start | bytes 835592 | tf_op jit(solution)/shard_map/ppermute | solution.py:31
  54.3 1.5 %collective-permute-start.11 = (bf16[272,512]{1,0:T(8,128)(2,1)S(1)}, bf16[272,512]{1,0:T(8,128)(2,1)S(1)}, u32[]{:S(2)}, u32[]{:S(2)}) collective-permute-start(bf16[272,512]{1,0:T(8,128)(2,1)S(1)} %multiply_convert_fusion.refs_4_), channel_id=1, source_target_pairs={{0,1},{4,5},{1,0},{5,4},{2,3},{6,7},{3,2},{7,6},{8,9},{12,13},{9,8... | collective-permute-start | bytes 835592 | tf_op jit(solution)/shard_map/ppermute | solution.py:31
  55.8 1.0 collective-permute-start.10
  56.8 1.6 %collective-permute-start.13 = (bf16[272,512]{1,0:T(8,128)(2,1)S(1)}, bf16[272,512]{1,0:T(8,128)(2,1)S(1)}, u32[]{:S(2)}, u32[]{:S(2)}) collective-permute-start(bf16[272,512]{1,0:T(8,128)(2,1)S(1)} %multiply_convert_fusion.refs_4_), channel_id=1, source_target_pairs={{0,2},{2,0},{1,3},{3,1},{4,6},{6,4},{5,7},{7,5},{8,10},{10,8},{9,1... | collective-permute-start | bytes 835592 | tf_op jit(solution)/shard_map/ppermute | solution.py:43
  58.4 3.4 %collective-permute-done.12.refs_7_ = bf16[272,512]{1,0:T(8,128)(2,1)S(1)} collective-permute-done((bf16[272,512]{1,0:T(8,128)(2,1)S(1)}, bf16[272,512]{1,0:T(8,128)(2,1)S(1)}, u32[]{:S(2)}, u32[]{:S(2)}) %collective-permute-start.12) | collective-permute-done | bytes 278560 | tf_op jit(solution)/shard_map/ppermute | solution.py:31
  61.8 2.0 %collective-permute-start.16 = (bf16[272,512]{1,0:T(8,128)(2,1)S(1)}, bf16[272,512]{1,0:T(8,128)(2,1)S(1)}, u32[]{:S(2)}, u32[]{:S(2)}) collective-permute-start(bf16[272,512]{1,0:T(8,128)(2,1)S(1)} %collective-permute-done.12.refs_7_), channel_id=1, source_target_pairs={{0,2},{2,0},{1,3},{3,1},{4,6},{6,4},{5,7},{7,5},{8,10},{10,8},{9,1... | collective-permute-start | bytes 835592 | tf_op jit(solution)/shard_map/ppermute | solution.py:43
  63.9 4.2 %collective-permute-done.11.refs_6_ = bf16[272,512]{1,0:T(8,128)(2,1)S(1)} collective-permute-done((bf16[272,512]{1,0:T(8,128)(2,1)S(1)}, bf16[272,512]{1,0:T(8,128)(2,1)S(1)}, u32[]{:S(2)}, u32[]{:S(2)}) %collective-permute-start.11) | collective-permute-done | bytes 278560 | tf_op jit(solution)/shard_map/ppermute | solution.py:31
  68.0 1.3 %collective-permute-start.15 = (bf16[272,512]{1,0:T(8,128)(2,1)S(1)}, bf16[272,512]{1,0:T(8,128)(2,1)S(1)}, u32[]{:S(2)}, u32[]{:S(2)}) collective-permute-start(bf16[272,512]{1,0:T(8,128)(2,1)S(1)} %collective-permute-done.11.refs_6_), channel_id=1, source_target_pairs={{0,2},{2,0},{1,3},{3,1},{4,6},{6,4},{5,7},{7,5},{8,10},{10,8},{9,1... | collective-permute-start | bytes 835592 | tf_op jit(solution)/shard_map/ppermute | solution.py:43
  69.4 0.0 collective-permute-done.10.refs_5_
  69.4 0.4 collective-permute-start.14
  69.8 0.8 collective-permute-done.15.refs_10_
  70.6 0.4 collective-permute-done.14.refs_9_
  71.0 10.4 %shard_map.68 = bf16[64,2,8,1024]{3,2,1,0:T(8,128)(2,1)S(1)} custom-call(s32[5]{0:T(128)S(1)} %stack.26.place.refs_0_, bf16[2176,512]{1,0:T(8,128)(2,1)S(1)} %bitcast.25, bf16[2176,1024]{1,0:T(8,128)(2,1)S(1)} %get-tuple-element.43.picked, bf16[2176,1024]{1,0:T(8,128)(2,1)S(1)} %get-tuple-element.44.tangents, f32[128,1024]{1,0:T(8,128)S(1)} %get-tuple-element.45.linears, ...), custom_call_target="tpu_custom_call" | custom-call | flops 6845104128 | bytes 2097152 | tf_op jit(solution)/shard_map/pallas_call | solution.py:219
  81.4 36.4 %all_to_all.5 = bf16[128,8,1024]{2,1,0:T(8,128)(2,1)S(1)} all-to-all(bf16[128,8,1024]{2,1,0:T(8,128)(2,1)S(1)} %bitcast.27), channel_id=1, replica_groups=mesh['x'=4,'y'=4,'zl'=2,'core'=2,'zh'=2] {'x','y','zl','core','zh'}, dimensions={0} | all-to-all | bytes 4194304 | tf_op jit(solution)/shard_map/all_to_all | solution.py:371
  117.7 1.6 %shard_map.69 = f32[1,8,8192]{2,1,0:T(8,128)} custom-call(bf16[16,8,8,1024]{3,2,1,0:T(8,128)(2,1)S(1)} %bitcast.26), custom_call_target="tpu_custom_call" | custom-call | tf_op jit(solution)/shard_map/pallas_call | solution.py:255
  (19 shorter events, 0.2 us)
Async XLA Ops:
  1.0 11.3 %collective-permute-start = (bf16[512,256]{1,0:T(8,128)(2,1)S(1)}, bf16[512,256]{1,0:T(8,128)(2,1)S(1)}, u32[]{:S(2)}, u32[]{:S(2)}) collective-permute-start(bf16[512,256]{1,0:T(8,128)(2,1)S(1)} %dynamic-slice_bitcast_fusion.1), channel_id=1, source_target_pairs={{0,5},{1,4},{4,1},{5,0},{2,7},{3,6},{6,3},{7,2},{8,13},{9,12},{12,... | collective-permute-start | bytes 786440 | tf_op jit(solution)/shard_map/ppermute | solution.py:35
  5.7 1.2 %copy-start = (bf16[8,128,512]{2,1,0:T(8,128)(2,1)S(1)}, bf16[8,128,512]{2,1,0:T(8,128)(2,1)}, u32[]{:S(2)}) copy-start(bf16[8,128,512]{2,1,0:T(8,128)(2,1)} %target_jac.1) | copy-start | bytes 3145732
  6.9 0.7 copy-start.1
  7.6 0.7 copy-start.2
  8.3 0.7 copy-start.3
  9.0 0.7 copy-start.4
  10.4 1.9 %collective-permute-start.1 = (f32[4,640]{1,0:T(4,128)S(1)}, f32[4,640]{1,0:T(4,128)S(1)}, u32[]{:S(2)}, u32[]{:S(2)}) collective-permute-start(f32[4,640]{1,0:T(4,128)S(1)} %get-tuple-element.29), channel_id=1, source_target_pairs={{0,2},{2,0},{1,3},{3,1},{4,6},{6,4},{5,7},{7,5},{8,10},{10,8},{9,1... | collective-permute-start | bytes 30728 | tf_op jit(solution)/shard_map/ppermute | solution.py:43
  12.3 6.9 %collective-permute-start.2 = (f32[8,640]{1,0:T(8,128)S(1)}, f32[8,640]{1,0:T(8,128)S(1)}, u32[]{:S(2)}, u32[]{:S(2)}) collective-permute-start(f32[8,640]{1,0:T(8,128)S(1)} %pad_maximum_fusion.1), channel_id=1, source_target_pairs={{0,4},{4,0},{1,5},{5,1},{2,6},{6,2},{3,7},{7,3},{8,12},{12,8},{9,1... | collective-permute-start | bytes 61448 | tf_op jit(solution)/shard_map/ppermute | solution.py:344
  13.7 8.5 %collective-permute-start.5 = (bf16[512,256]{1,0:T(8,128)(2,1)S(1)}, bf16[512,256]{1,0:T(8,128)(2,1)S(1)}, u32[]{:S(2)}, u32[]{:S(2)}) collective-permute-start(bf16[512,256]{1,0:T(8,128)(2,1)S(1)} %collective-permute-done.refs_6_.refs_0_), channel_id=1, source_target_pairs={{0,32},{32,64},{64,96},{96,0},{1,33},{33,65},{65,97},{97,1},{2,34}... | collective-permute-start | bytes 786440 | tf_op jit(solution)/shard_map/ppermute | solution.py:39
  15.0 7.5 %collective-permute-start.4 = (bf16[512,256]{1,0:T(8,128)(2,1)S(1)}, bf16[512,256]{1,0:T(8,128)(2,1)S(1)}, u32[]{:S(2)}, u32[]{:S(2)}) collective-permute-start(bf16[512,256]{1,0:T(8,128)(2,1)S(1)} %collective-permute-done.refs_6_.refs_0_), channel_id=1, source_target_pairs={{0,24},{8,0},{16,8},{24,16},{1,25},{9,1},{17,9},{25,17},{2,26},{10... | collective-permute-start | bytes 786440 | tf_op jit(solution)/shard_map/ppermute | solution.py:39
  17.7 6.7 %collective-permute-start.3 = (bf16[512,256]{1,0:T(8,128)(2,1)S(1)}, bf16[512,256]{1,0:T(8,128)(2,1)S(1)}, u32[]{:S(2)}, u32[]{:S(2)}) collective-permute-start(bf16[512,256]{1,0:T(8,128)(2,1)S(1)} %collective-permute-done.refs_6_.refs_0_), channel_id=1, source_target_pairs={{0,96},{32,0},{64,32},{96,64},{1,97},{33,1},{65,33},{97,65},{2,98}... | collective-permute-start | bytes 786440 | tf_op jit(solution)/shard_map/ppermute | solution.py:39
  28.1 4.5 %collective-permute-start.6 = (bf16[1088,512]{1,0:T(8,128)(2,1)S(1)}, bf16[1088,512]{1,0:T(8,128)(2,1)S(1)}, u32[]{:S(2)}, u32[]{:S(2)}) collective-permute-start(bf16[1088,512]{1,0:T(8,128)(2,1)S(1)} %shard_map.65), channel_id=1, source_target_pairs={{0,2},{2,0},{1,3},{3,1},{4,6},{6,4},{5,7},{7,5},{8,10},{10,8},{9,1... | collective-permute-start | bytes 3342344 | tf_op jit(solution)/shard_map/ppermute | solution.py:43
  36.5 11.4 %collective-permute-start.7 = (bf16[272,512]{1,0:T(8,128)(2,1)S(1)}, bf16[272,512]{1,0:T(8,128)(2,1)S(1)}, u32[]{:S(2)}, u32[]{:S(2)}) collective-permute-start(bf16[272,512]{1,0:T(8,128)(2,1)S(1)} %get-tuple-element.36), channel_id=1, source_target_pairs={{0,1},{4,5},{1,0},{5,4},{2,3},{6,7},{3,2},{7,6},{8,9},{12,13},{9,8... | collective-permute-start | bytes 835592 | tf_op jit(solution)/shard_map/ppermute | solution.py:31
  39.5 13.1 %collective-permute-start.8 = (bf16[272,512]{1,0:T(8,128)(2,1)S(1)}, bf16[272,512]{1,0:T(8,128)(2,1)S(1)}, u32[]{:S(2)}, u32[]{:S(2)}) collective-permute-start(bf16[272,512]{1,0:T(8,128)(2,1)S(1)} %get-tuple-element.37), channel_id=1, source_target_pairs={{0,4},{4,1},{1,5},{5,0},{2,6},{6,3},{3,7},{7,2},{8,12},{12,9},{9,1... | collective-permute-start | bytes 835592 | tf_op jit(solution)/shard_map/ppermute | solution.py:31
  39.5 13.1 %collective-permute-start.9 = (bf16[272,512]{1,0:T(8,128)(2,1)S(1)}, bf16[272,512]{1,0:T(8,128)(2,1)S(1)}, u32[]{:S(2)}, u32[]{:S(2)}) collective-permute-start(bf16[272,512]{1,0:T(8,128)(2,1)S(1)} %get-tuple-element.38), channel_id=1, source_target_pairs={{0,5},{4,0},{1,4},{5,1},{2,7},{6,2},{3,6},{7,3},{8,13},{12,8},{9,1... | collective-permute-start | bytes 835592 | tf_op jit(solution)/shard_map/ppermute | solution.py:31
  52.8 9.0 %collective-permute-start.12 = (bf16[272,512]{1,0:T(8,128)(2,1)S(1)}, bf16[272,512]{1,0:T(8,128)(2,1)S(1)}, u32[]{:S(2)}, u32[]{:S(2)}) collective-permute-start(bf16[272,512]{1,0:T(8,128)(2,1)S(1)} %multiply_convert_fusion.refs_4_), channel_id=1, source_target_pairs={{0,4},{4,1},{1,5},{5,0},{2,6},{6,3},{3,7},{7,2},{8,12},{12,9},{9,1... | collective-permute-start | bytes 835592 | tf_op jit(solution)/shard_map/ppermute | solution.py:31
  54.3 13.7 %collective-permute-start.11 = (bf16[272,512]{1,0:T(8,128)(2,1)S(1)}, bf16[272,512]{1,0:T(8,128)(2,1)S(1)}, u32[]{:S(2)}, u32[]{:S(2)}) collective-permute-start(bf16[272,512]{1,0:T(8,128)(2,1)S(1)} %multiply_convert_fusion.refs_4_), channel_id=1, source_target_pairs={{0,1},{4,5},{1,0},{5,4},{2,3},{6,7},{3,2},{7,6},{8,9},{12,13},{9,8... | collective-permute-start | bytes 835592 | tf_op jit(solution)/shard_map/ppermute | solution.py:31
  55.8 13.6 %collective-permute-start.10 = (bf16[272,512]{1,0:T(8,128)(2,1)S(1)}, bf16[272,512]{1,0:T(8,128)(2,1)S(1)}, u32[]{:S(2)}, u32[]{:S(2)}) collective-permute-start(bf16[272,512]{1,0:T(8,128)(2,1)S(1)} %multiply_convert_fusion.refs_4_), channel_id=1, source_target_pairs={{0,5},{4,0},{1,4},{5,1},{2,7},{6,2},{3,6},{7,3},{8,13},{12,8},{9,1... | collective-permute-start | bytes 835592 | tf_op jit(solution)/shard_map/ppermute | solution.py:31
  56.8 13.0 %collective-permute-start.13 = (bf16[272,512]{1,0:T(8,128)(2,1)S(1)}, bf16[272,512]{1,0:T(8,128)(2,1)S(1)}, u32[]{:S(2)}, u32[]{:S(2)}) collective-permute-start(bf16[272,512]{1,0:T(8,128)(2,1)S(1)} %multiply_convert_fusion.refs_4_), channel_id=1, source_target_pairs={{0,2},{2,0},{1,3},{3,1},{4,6},{6,4},{5,7},{7,5},{8,10},{10,8},{9,1... | collective-permute-start | bytes 835592 | tf_op jit(solution)/shard_map/ppermute | solution.py:43
  61.8 7.9 %collective-permute-start.16 = (bf16[272,512]{1,0:T(8,128)(2,1)S(1)}, bf16[272,512]{1,0:T(8,128)(2,1)S(1)}, u32[]{:S(2)}, u32[]{:S(2)}) collective-permute-start(bf16[272,512]{1,0:T(8,128)(2,1)S(1)} %collective-permute-done.12.refs_7_), channel_id=1, source_target_pairs={{0,2},{2,0},{1,3},{3,1},{4,6},{6,4},{5,7},{7,5},{8,10},{10,8},{9,1... | collective-permute-start | bytes 835592 | tf_op jit(solution)/shard_map/ppermute | solution.py:43
  68.0 2.5 %collective-permute-start.15 = (bf16[272,512]{1,0:T(8,128)(2,1)S(1)}, bf16[272,512]{1,0:T(8,128)(2,1)S(1)}, u32[]{:S(2)}, u32[]{:S(2)}) collective-permute-start(bf16[272,512]{1,0:T(8,128)(2,1)S(1)} %collective-permute-done.11.refs_6_), channel_id=1, source_target_pairs={{0,2},{2,0},{1,3},{3,1},{4,6},{6,4},{5,7},{7,5},{8,10},{10,8},{9,1... | collective-permute-start | bytes 835592 | tf_op jit(solution)/shard_map/ppermute | solution.py:43
  69.4 1.6 %collective-permute-start.14 = (bf16[272,512]{1,0:T(8,128)(2,1)S(1)}, bf16[272,512]{1,0:T(8,128)(2,1)S(1)}, u32[]{:S(2)}, u32[]{:S(2)}) collective-permute-start(bf16[272,512]{1,0:T(8,128)(2,1)S(1)} %collective-permute-done.10.refs_5_), channel_id=1, source_target_pairs={{0,2},{2,0},{1,3},{3,1},{4,6},{6,4},{5,7},{7,5},{8,10},{10,8},{9,1... | collective-permute-start | bytes 835592 | tf_op jit(solution)/shard_map/ppermute | solution.py:43

commit v7 on v6

--- a/solution.py
+++ b/solution.py
@@ -18,6 +18,8 @@
 GROUP = 4 * CHUNK
 STEP = 2 * CHUNK
 LIMIT = 24 * 2**20
+ORDER = (0, 1, 3, 2)
+EARLY = 6
 jacobian_weight = 32.0
 f32 = jnp.float32
 bf16 = jnp.bfloat16
@@ -62,22 +64,19 @@
     return [pl.BlockSpec((REDUCED, BLOCK), lambda i, place, k=k: (0, place[k])) for k in range(4)]
 
 
-def forward_kernel(final, place, rows, *refs):
+def forward_kernel(final, place, one, two, *refs):
     own, other, refs = refs[:4], refs[4:8], refs[8:]
     if final:
         arrived, refs = refs[0], refs[1:]
     w_first, w_last = refs[-2:]
     outs = refs[:-2]
-
-    @pl.when(pl.program_id(0) == 0)
-    def _():
-        here = place[4] == 0
-        for k in range(4):
-            span = slice(k * BLOCK, (k + 1) * BLOCK)
-            w_first[:, span] = jnp.where(here, own[k][...], other[k][...])
-            w_last[:, span] = jnp.where(here, other[k][...], own[k][...])
-
-    picked = jnp.dot(rows[...], w_first[...], preferred_element_type=f32)
+    here = place[4] == 0
+    for k in range(4):
+        span = slice(k * BLOCK, (k + 1) * BLOCK)
+        w_first[:, span] = jnp.where(here, own[k][...], other[k][...])
+        w_last[:, span] = jnp.where(here, other[k][...], own[k][...])
+    rows = jnp.concatenate([one[...], two[...]], axis=0)
+    picked = jnp.dot(rows, w_first[...], preferred_element_type=f32)
     parts = []
     for c in range(2):
         part = picked[c * CHUNK : (c + 1) * CHUNK]
@@ -91,34 +90,27 @@
         outs[0][...] = total.astype(bf16)
         return
     total = total + arrived[...].astype(f32)
-    for step in range(2):
-
-        @pl.when(pl.program_id(0) == step)
-        def _():
-            for c in range(2):
-                out = outs[2 * step + c]
-                out[...] = total[c * CHUNK : (c + 1) * CHUNK].astype(out.dtype)
-
-
-def forward(place, rows, own, other, arrived=None):
+    for c in range(2):
+        outs[c][...] = total[c * CHUNK : (c + 1) * CHUNK].astype(outs[c].dtype)
+
+
+def forward(place, rows, at, own, other, arrived=None, dtypes=None):
     final = arrived is not None
-    base = 0 if final else 2
-    in_specs = [pl.BlockSpec((STEP, REDUCED), lambda i, place: (i + base, 0)), *own_specs()]
-    in_specs += [whole_spec((REDUCED, BLOCK))] * 4
-    args = [rows, own, own, own, own, *other]
-    out_specs = pl.BlockSpec((STEP, REDUCED), lambda i, place: (i, 0))
-    out_shape = jax.ShapeDtypeStruct((GROUP, REDUCED), bf16)
+    in_specs = [pl.BlockSpec((CHUNK, REDUCED), lambda i, place, a=a: (a, 0)) for a in at]
+    in_specs += own_specs() + [whole_spec((REDUCED, BLOCK))] * 4
+    args = [rows, rows, own, own, own, own, *other]
+    out_specs = whole_spec((STEP, REDUCED))
+    out_shape = jax.ShapeDtypeStruct((STEP, REDUCED), bf16)
     if final:
         in_specs.append(out_specs)
         args.append(arrived)
-        out_specs = [whole_spec((CHUNK, REDUCED))] * 4
-        out_shape = [jax.ShapeDtypeStruct((CHUNK, REDUCED), f32)]
-        out_shape += [jax.ShapeDtypeStruct((CHUNK, REDUCED), bf16)] * 3
+        out_specs = [whole_spec((CHUNK, REDUCED))] * 2
+        out_shape = [jax.ShapeDtypeStruct((CHUNK, REDUCED), dtype) for dtype in dtypes]
     return pl.pallas_call(
         lambda *refs: forward_kernel(final, *refs),
         grid_spec=pltpu.PrefetchScalarGridSpec(
             num_scalar_prefetch=1,
-            grid=(2,),
+            grid=(1,),
             in_specs=in_specs,
             out_specs=out_specs,
             scratch_shapes=[pltpu.VMEM((REDUCED, COLS), bf16)] * 2,
@@ -128,7 +120,7 @@
             dimension_semantics=("arbitrary",), vmem_limit_bytes=LIMIT
         ),
         cost_estimate=pl.CostEstimate(
-            flops=4 * GROUP * REDUCED * COLS, bytes_accessed=4 * REDUCED * COLS, transcendentals=0
+            flops=4 * STEP * REDUCED * COLS, bytes_accessed=4 * REDUCED * COLS, transcendentals=0
         ),
     )(place, *args)
 
@@ -186,11 +178,12 @@
     )(place, rows, own, *other)
 
 
-def backward_kernel(place, rows, picked, tangents, linears, own, *refs):
-    other, misfits, out, cotangents = refs[:4], refs[4:12], refs[12], refs[13]
+def backward_kernel(count, place, rows, picked, tangents, linears, own, *refs):
+    other, misfits, refs = refs[:4], refs[4 : 4 + count], refs[4 + count :]
+    cotangents = refs[-1]
     theirs = piece_of(pl.program_id(0), other)
     w_last = jnp.where(place[4] == 0, theirs, own[...])
-    for c in range(8):
+    for c in range(count):
         span = pl.ds(c * CHUNK, CHUNK)
         back = jnp.dot(misfits[c][...], w_last, preferred_element_type=f32)
         back = back.astype(bf16).astype(f32)
@@ -210,37 +203,57 @@
     whole = jnp.concatenate([m[...] for m in misfits], axis=0)
     last = lax.dot_general(whole, tangents[...], over_rows, preferred_element_type=f32)
     first = lax.dot_general(rows[...], cotangents[...], over_rows, preferred_element_type=f32)
+    if count == EARLY:
+        first_out, last_out = refs[:2]
+        first_out[...] = first
+        last_out[...] = last
+        return
+    first_so_far, last_so_far, out = refs[:3]
+    first = first + first_so_far[...]
+    last = last + last_so_far[...]
     out[:, 0] = first.astype(bf16).reshape(64, 8, BLOCK)
     out[:, 1] = last.astype(bf16).reshape(64, 8, BLOCK)
 
 
-def backward(place, rows, prepared, own, other, misfits):
-    columns = lambda height: pl.BlockSpec((height, BLOCK), lambda j, place: (0, j))
+def backward(place, rows, prepared, own, other, misfits, so_far=None):
+    count = len(misfits)
+    height, block = count * CHUNK, 0 if so_far is None else 3
+    columns = lambda height, at=0: pl.BlockSpec((height, BLOCK), lambda j, place: (at, j))
+    in_specs = [
+        pl.BlockSpec((height, REDUCED), lambda j, place: (block, 0)),
+        columns(height, block),
+        columns(height, block),
+        columns(16 * count, block),
+        pl.BlockSpec((REDUCED, BLOCK), lambda j, place: (0, place[j])),
+        *[whole_spec((REDUCED, BLOCK))] * 4,
+        *[whole_spec((CHUNK, REDUCED))] * count,
+    ]
+    args = [rows, *prepared, own, *other, *misfits]
+    if so_far is None:
+        out_specs = [columns(REDUCED)] * 2
+        out_shape = [jax.ShapeDtypeStruct((REDUCED, COLS), f32)] * 2
+    else:
+        in_specs += [columns(REDUCED)] * 2
+        args += so_far
+        out_specs = pl.BlockSpec((64, 2, 8, BLOCK), lambda j, place: (0, 0, 0, place[j]))
+        out_shape = jax.ShapeDtypeStruct((64, 2, 8, COLS), bf16)
     return pl.pallas_call(
-        backward_kernel,
+        lambda *refs: backward_kernel(count, *refs),
         grid_spec=pltpu.PrefetchScalarGridSpec(
             num_scalar_prefetch=1,
             grid=(4,),
-            in_specs=[
-                whole_spec((2 * GROUP, REDUCED)),
-                columns(2 * GROUP),
-                columns(2 * GROUP),
-                columns(128),
-                pl.BlockSpec((REDUCED, BLOCK), lambda j, place: (0, place[j])),
-                *[whole_spec((REDUCED, BLOCK))] * 4,
-                *[whole_spec((CHUNK, REDUCED))] * 8,
-            ],
-            out_specs=pl.BlockSpec((64, 2, 8, BLOCK), lambda j, place: (0, 0, 0, place[j])),
-            scratch_shapes=[pltpu.VMEM((2 * GROUP, BLOCK), bf16)],
-        ),
-        out_shape=jax.ShapeDtypeStruct((64, 2, 8, COLS), bf16),
+            in_specs=in_specs,
+            out_specs=out_specs,
+            scratch_shapes=[pltpu.VMEM((height, BLOCK), bf16)],
+        ),
+        out_shape=out_shape,
         compiler_params=pltpu.CompilerParams(
             dimension_semantics=("arbitrary",), vmem_limit_bytes=LIMIT
         ),
         cost_estimate=pl.CostEstimate(
-            flops=12 * GROUP * REDUCED * COLS, bytes_accessed=4 * REDUCED * COLS, transcendentals=0
-        ),
-    )(place, rows, *prepared, own, *other, *misfits)
+            flops=6 * height * REDUCED * COLS, bytes_accessed=4 * REDUCED * COLS, transcendentals=0
+        ),
+    )(place, *args)
 
 
 def total_kernel(pieces, out):
@@ -320,20 +333,20 @@
     z = zh * 2 + zl
     kind = (at_x + 2 * at_y) % 4
     weight = weights[0]
-    mine = (zl * 2 + core) * 2 + zh
+    share = (zl * 2 + core) * 2 + zh
     theirs = ((1 - zl) * 2 + core) * 2 + (1 - zh)
     turn = [(kind + k) % 4 for k in range(4)]
     place = jnp.stack(turn + [zh]).astype(jnp.int32)
 
     quarter = lax.dynamic_slice_in_dim(weight, theirs * COLS + kind * BLOCK, BLOCK, 1)
     direct = z_facing(quarter)
-    own = lax.dynamic_slice_in_dim(weight, mine * COLS, COLS, 1)
+    own = lax.dynamic_slice_in_dim(weight, share * COLS, COLS, 1)
 
     packed, wanted = pick(
         plan.reshape(8), place, samples, directions, targets, jacobian_targets
     )
     swapped = core_swap(packed)
-    direct, packed, swapped = lax.optimization_barrier((direct, packed, swapped))
+    direct, packed, swapped, own = lax.optimization_barrier((direct, packed, swapped, own))
     other = [
         direct,
         ring_shift(direct, "x", 3),
@@ -346,28 +359,38 @@
     high = jnp.where(zl == 0, beside, pair).reshape(2, 2, 2, REDUCED + TANGENTS)
     small = jnp.stack([low, high], axis=2).reshape(2, 4, 2, REDUCED + TANGENTS)
     small = lax.dynamic_slice_in_dim(jnp.concatenate([small, small], axis=1), z, 4, 1)
+    small = jnp.concatenate([small[:, d : d + 1] for d in ORDER], axis=1).swapaxes(0, 1)
     small = small.reshape(8, 2, REDUCED + TANGENTS)
     chosen = small[:, :, REDUCED:].reshape(8, 2 * TANGENTS).astype(jnp.int32)
     onehot = (chosen[:, :, None] == jnp.arange(REDUCED, dtype=jnp.int32)).astype(bf16)
     inputs = jnp.pad(small[:, :, :REDUCED].astype(bf16), ((0, 0), (0, 14), (0, 0)))
     rows = jnp.concatenate([onehot, inputs], axis=1).reshape(2 * GROUP, REDUCED)
 
-    from_core = core_swap(forward(place, rows, own, other))
-    chunks = forward(place, rows, own, other, from_core)
-    chunks, ready = lax.optimization_barrier((chunks, rows))
-    got = [z_shift(chunks[d], d) for d in (2, 1, 3)]
+    pairs = ((6, 2), (4, 0))
+    arrived = []
+    for one, two in pairs:
+        arrived.append(core_swap(forward(place, rows, (one + 1, two + 1), own, other)))
+    ahead = forward(place, rows, pairs[0], own, other, arrived[0], (bf16, bf16))
+    ahead, second = lax.optimization_barrier((ahead, arrived[1]))
+    got = [z_shift(ahead[0], 2), z_shift(ahead[1], 1)]
+    three, total = forward(place, rows, pairs[1], own, other, second, (bf16, f32))
+    got.append(z_shift(three, 3))
+    total, ready = lax.optimization_barrier((total, rows))
     prepared = prepare(place, ready, own, other)
     got, prepared = lax.optimization_barrier((got, prepared))
-    total = chunks[0]
     for g in got:
         total = total + g.astype(f32)
     scale = jnp.where(jnp.arange(CHUNK)[:, None] < 2 * TANGENTS, jacobian_weight, 1.0)
     misfit = (scale * (total - wanted)).astype(bf16)
-    near = [misfit, None, None, None]
-    for d in (2, 1, 3):
-        near[d] = z_shift(misfit, 4 - d)
-    misfits = near + [core_swap(m) for m in near]
-    sent = backward(place, rows, prepared, own, other, misfits)
+    near, early = [misfit], []
+    for d in ORDER[1:]:
+        near.append(z_shift(misfit, 4 - d))
+    for part in near[:3]:
+        early += [part, core_swap(part)]
+    so_far = backward(place, rows, prepared, own, other, early)
+    near[3], so_far = lax.optimization_barrier((near[3], so_far))
+    late = [near[3], core_swap(near[3])]
+    sent = backward(place, rows, prepared, own, other, late, so_far)
     pieces = lax.all_to_all(
         sent.reshape(128, 8, COLS), AXES, split_axis=0, concat_axis=0, tiled=True
     )

time: 120 us -> 114 us (0.950)
  waiting for transfers between devices: 21.1 us -> 14.8 us
  Pallas kernels: 26 us -> 29.8 us
  starting transfers between devices: 28.4 us -> 25.2 us
    ppermute x6, waiting for transfers between devices: 12.4 us -> 8.48 us  [z_shift(): lax.ppermute(block, Z, [(z_index(z), z_index((z + d) % 4)) for z in range...]
    pallas_call x1 -> x2, Pallas kernels: 10.4 us -> 13.8 us  [backward(): pl.pallas_call(lambda *refs: backward_kernel(count, *refs), grid_spec=plt...]
    ppermute x6 -> x7, waiting for transfers between devices: 4.42 us -> 1.59 us  [core_swap(): return lax.ppermute(block, 'core', [(0, 1), (1, 0)])]
    ppermute x6 -> x7, starting transfers between devices: 8.48 us -> 6 us  [core_swap(): return lax.ppermute(block, 'core', [(0, 1), (1, 0)])]
    pallas_call x2 -> x4, Pallas kernels: 7.58 us -> 8 us  [forward(): pl.pallas_call(lambda *refs: forward_kernel(final, *refs), grid_spec=pltp...]
  transfers between devices with their start and end apart: 17 -> 18, of which waited for: 10 -> 7; matrix products, arithmetic and copies ran while one was open for 2% -> 2% of each run, Pallas kernels for 5% -> 18%
where the time goes in v7:
time: 114 us
  blocking collectives  36.5 us (32%)
  Pallas kernels  29.8 us (26%)
  starting transfers between devices  25.2 us (22%)
  waiting for transfers between devices  14.8 us (13%)
  local copies, waits for them, and re-layouts  6.37 us (6%)
    all_to_all x1, blocking collectives, shards(): lax.all_to_all(sent.reshape(128, 8, COLS), AXES, split_axis=0, concat_axi...  36.5 us
    pallas_call x2, Pallas kernels, backward(): pl.pallas_call(lambda *refs: backward_kernel(count, *refs), grid_spec=plt...  13.8 us
    ppermute x6, starting transfers between devices, z_shift(): lax.ppermute(block, Z, [(z_index(z), z_index((z + d) % 4)) for z in range...  8.98 us
    ppermute x6, waiting for transfers between devices, z_shift(): lax.ppermute(block, Z, [(z_index(z), z_index((z + d) % 4)) for z in range...  8.48 us
    pallas_call x4, Pallas kernels, forward(): pl.pallas_call(lambda *refs: forward_kernel(final, *refs), grid_spec=pltp...  8 us
    ppermute x7, starting transfers between devices, core_swap(): return lax.ppermute(block, 'core', [(0, 1), (1, 0)])  6 us
    pallas_call x1, Pallas kernels, prepare(): pl.pallas_call(prepare_kernel, grid_spec=pltpu.PrefetchScalarGridSpec(num...  5.64 us
    ppermute x3, starting transfers between devices, ring_shift(): return lax.ppermute(block, axis, [(i, (i + d) % 4) for i in range(4)])  5.48 us
  transfers between devices with their start and end apart: 18, of which 7 were waited for; matrix products, arithmetic and copies ran while one was open for 2% of the time, Pallas kernels for 18%

profile of v7, /device:TPU:1, one launch (start us, length us, event | category | flops | bytes accessed | tf_op | source)
XLA Modules:
  0.0 114.0 jit_solution(4879751991314024207)
XLA Ops:
  0.0 1.0 dynamic-slice_bitcast_fusion.1
  1.0 4.7 %collective-permute-start = (bf16[512,256]{1,0:T(8,128)(2,1)S(1)}, bf16[512,256]{1,0:T(8,128)(2,1)S(1)}, u32[]{:S(2)}, u32[]{:S(2)}) collective-permute-start(bf16[512,256]{1,0:T(8,128)(2,1)S(1)} %dynamic-slice_bitcast_fusion.1), channel_id=1, source_target_pairs={{0,5},{1,4},{4,1},{5,0},{2,7},{3,6},{6,3},{7,2},{8,13},{9,12},{12,... | collective-permute-start | bytes 786440 | tf_op jit(solution)/shard_map/ppermute | solution.py:37
  5.6 0.1 stack.26.place.refs_0_
  5.7 1.2 %copy-done = bf16[8,128,512]{2,1,0:T(8,128)(2,1)S(1)} copy-done((bf16[8,128,512]{2,1,0:T(8,128)(2,1)S(1)}, bf16[8,128,512]{2,1,0:T(8,128)(2,1)}, u32[]{:S(2)}) %copy-start) | copy-done | bytes 1048600
  6.9 0.7 copy-done.1
  7.6 0.7 copy-done.2
  8.3 0.7 copy-done.3
  9.0 0.7 copy-done.4
  9.7 0.7 shard_map.64
  10.4 1.0 collective-permute-start.1
  11.4 1.3 %dynamic-slice_bitcast_fusion.refs_3_.refs_4_.refs_5_.refs_6_.own = bf16[512,1024]{1,0:T(8,128)(2,1)S(1)} fusion(bf16[1,512,8192]{2,1,0:T(8,128)(2,1)} %param.11, s32[]{:T(128)S(6)} %select_n.60), kind=kLoop, calls=%fused_computation.5 | loop fusion | bytes 2097156 | tf_op jit(solution)/shard_map/dynamic_slice | solution.py:343
  12.7 0.0 collective-permute-done.1
  12.8 0.1 collective-permute-start.2
  12.9 1.3 %collective-permute-start.5 = (bf16[512,256]{1,0:T(8,128)(2,1)S(1)}, bf16[512,256]{1,0:T(8,128)(2,1)S(1)}, u32[]{:S(2)}, u32[]{:S(2)}) collective-permute-start(bf16[512,256]{1,0:T(8,128)(2,1)S(1)} %collective-permute-done.refs_7_.refs_0_.refs_6_), channel_id=1, source_target_pairs={{0,32},{32,64},{64,96},{96,0},{1,33},{33,65},{65,97},{97,1},{2,34}... | collective-permute-start | bytes 786440 | tf_op jit(solution)/shard_map/ppermute | solution.py:41
  14.2 2.7 %collective-permute-start.4 = (bf16[512,256]{1,0:T(8,128)(2,1)S(1)}, bf16[512,256]{1,0:T(8,128)(2,1)S(1)}, u32[]{:S(2)}, u32[]{:S(2)}) collective-permute-start(bf16[512,256]{1,0:T(8,128)(2,1)S(1)} %collective-permute-done.refs_7_.refs_0_.refs_6_), channel_id=1, source_target_pairs={{0,24},{8,0},{16,8},{24,16},{1,25},{9,1},{17,9},{25,17},{2,26},{10... | collective-permute-start | bytes 786440 | tf_op jit(solution)/shard_map/ppermute | solution.py:41
  16.9 1.5 %collective-permute-start.3 = (bf16[512,256]{1,0:T(8,128)(2,1)S(1)}, bf16[512,256]{1,0:T(8,128)(2,1)S(1)}, u32[]{:S(2)}, u32[]{:S(2)}) collective-permute-start(bf16[512,256]{1,0:T(8,128)(2,1)S(1)} %collective-permute-done.refs_7_.refs_0_.refs_6_), channel_id=1, source_target_pairs={{0,96},{32,0},{64,32},{96,64},{1,97},{33,1},{65,33},{97,65},{2,98}... | collective-permute-start | bytes 786440 | tf_op jit(solution)/shard_map/ppermute | solution.py:41
  18.6 0.5 fusion.1
  19.1 0.2 fusion.2
  19.4 2.5 %collective-permute-done.5.refs_10_.refs_3_.refs_9_ = bf16[512,256]{1,0:T(8,128)(2,1)S(1)} collective-permute-done((bf16[512,256]{1,0:T(8,128)(2,1)S(1)}, bf16[512,256]{1,0:T(8,128)(2,1)S(1)}, u32[]{:S(2)}, u32[]{:S(2)}) %collective-permute-start.5) | collective-permute-done | bytes 262176 | tf_op jit(solution)/shard_map/ppermute | solution.py:41
  21.9 0.3 collective-permute-done.4.refs_9_.refs_2_.refs_8_
  22.2 1.9 %collective-permute-done.3.refs_8_.refs_1_.refs_7_ = bf16[512,256]{1,0:T(8,128)(2,1)S(1)} collective-permute-done((bf16[512,256]{1,0:T(8,128)(2,1)S(1)}, bf16[512,256]{1,0:T(8,128)(2,1)S(1)}, u32[]{:S(2)}, u32[]{:S(2)}) %collective-permute-start.3) | collective-permute-done | bytes 262176 | tf_op jit(solution)/shard_map/ppermute | solution.py:41
  24.1 2.0 %shard_map.65 = bf16[544,512]{1,0:T(8,128)(2,1)S(1)} custom-call(s32[5]{0:T(128)S(1)} %stack.26.place.refs_0_, bf16[2176,512]{1,0:T(8,128)(2,1)S(1)} %bitcast.24, bf16[2176,512]{1,0:T(8,128)(2,1)S(1)} %bitcast.25, bf16[512,1024]{1,0:T(8,128)(2,1)S(1)} %dynamic-slice_bitcast_fusion.refs_3_.refs_4_.refs_5_.refs_6_.own, ...), custom_call_target="tpu_custom_call" | custom-call | flops 1140850688 | bytes 2097152 | tf_op jit(solution)/shard_map/pallas_call | solution.py:109
  26.1 1.6 %collective-permute-start.6 = (bf16[544,512]{1,0:T(8,128)(2,1)S(1)}, bf16[544,512]{1,0:T(8,128)(2,1)S(1)}, u32[]{:S(2)}, u32[]{:S(2)}) collective-permute-start(bf16[544,512]{1,0:T(8,128)(2,1)S(1)} %shard_map.65), channel_id=1, source_target_pairs={{0,2},{2,0},{1,3},{3,1},{4,6},{6,4},{5,7},{7,5},{8,10},{10,8},{9,1... | collective-permute-start | bytes 1671176 | tf_op jit(solution)/shard_map/ppermute | solution.py:45
  27.7 2.0 %shard_map.67 = bf16[544,512]{1,0:T(8,128)(2,1)S(1)} custom-call(s32[5]{0:T(128)S(1)} %stack.26.place.refs_0_, bf16[2176,512]{1,0:T(8,128)(2,1)S(1)} %bitcast.26, bf16[2176,512]{1,0:T(8,128)(2,1)S(1)} %bitcast.27, bf16[512,1024]{1,0:T(8,128)(2,1)S(1)} %dynamic-slice_bitcast_fusion.refs_3_.refs_4_.refs_5_.refs_6_.own, ...), custom_call_target="tpu_custom_call" | custom-call | flops 1140850688 | bytes 2097152 | tf_op jit(solution)/shard_map/pallas_call | solution.py:109
  29.7 0.1 collective-permute-start.7
  29.8 0.0 collective-permute-done.6.refs_11_
  29.8 2.0 %shard_map.66 = (bf16[272,512]{1,0:T(8,128)(2,1)S(1)}, bf16[272,512]{1,0:T(8,128)(2,1)S(1)}) custom-call(s32[5]{0:T(128)S(1)} %stack.26.place.refs_0_, bf16[2176,512]{1,0:T(8,128)(2,1)S(1)} %bitcast.28, bf16[2176,512]{1,0:T(8,128)(2,1)S(1)} %bitcast.29, bf16[512,1024]{1,0:T(8,128)(2,1)S(1)} %dynamic-slice_bitcast_fusion.refs_3_.refs_4_.refs_5_.refs_6_.own, ...), custom_call_target="tpu_custom_call" | custom-call | flops 1140850688 | bytes 2097152 | tf_op jit(solution)/shard_map/pallas_call | solution.py:109
  31.8 0.0 collective-permute-done.7.refs_11_
  31.8 2.4 %collective-permute-start.8 = (bf16[272,512]{1,0:T(8,128)(2,1)S(1)}, bf16[272,512]{1,0:T(8,128)(2,1)S(1)}, u32[]{:S(2)}, u32[]{:S(2)}) collective-permute-start(bf16[272,512]{1,0:T(8,128)(2,1)S(1)} %get-tuple-element.41), channel_id=1, source_target_pairs={{0,1},{4,5},{1,0},{5,4},{2,3},{6,7},{3,2},{7,6},{8,9},{12,13},{9,8... | collective-permute-start | bytes 835592 | tf_op jit(solution)/shard_map/ppermute | solution.py:33
  34.3 2.0 %shard_map.68 = (bf16[272,512]{1,0:T(8,128)(2,1)S(1)}, f32[272,512]{1,0:T(8,128)S(1)}) custom-call(s32[5]{0:T(128)S(1)} %stack.26.place.refs_0_, bf16[2176,512]{1,0:T(8,128)(2,1)S(1)} %bitcast.30, bf16[2176,512]{1,0:T(8,128)(2,1)S(1)} %bitcast.31, bf16[512,1024]{1,0:T(8,128)(2,1)S(1)} %dynamic-slice_bitcast_fusion.refs_3_.refs_4_.refs_5_.refs_6_.own, ...), custom_call_target="tpu_custom_call" | custom-call | flops 1140850688 | bytes 2097152 | tf_op jit(solution)/shard_map/pallas_call | solution.py:109
  36.3 2.8 %collective-permute-start.10 = (bf16[272,512]{1,0:T(8,128)(2,1)S(1)}, bf16[272,512]{1,0:T(8,128)(2,1)S(1)}, u32[]{:S(2)}, u32[]{:S(2)}) collective-permute-start(bf16[272,512]{1,0:T(8,128)(2,1)S(1)} %get-tuple-element.44), channel_id=1, source_target_pairs={{0,5},{4,0},{1,4},{5,1},{2,7},{6,2},{3,6},{7,3},{8,13},{12,8},{9,1... | collective-permute-start | bytes 835592 | tf_op jit(solution)/shard_map/ppermute | solution.py:33
  39.1 5.6 %shard_map.69 = (bf16[2176,1024]{1,0:T(8,128)(2,1)S(1)}, bf16[2176,1024]{1,0:T(8,128)(2,1)S(1)}, f32[128,1024]{1,0:T(8,128)S(1)}) custom-call(s32[5]{0:T(128)S(1)} %stack.26.place.refs_0_, bf16[2176,512]{1,0:T(8,128)(2,1)S(1)} %bitcast.32, bf16[512,1024]{1,0:T(8,128)(2,1)S(1)} %dynamic-slice_bitcast_fusion.refs_3_.refs_4_.refs_5_.refs_6_.own, ...), custom_call_target="tpu_custom_call" | custom-call | flops 2281701376 | bytes 2097152 | tf_op jit(solution)/shard_map/pallas_call | solution.py:155
  44.7 3.3 %collective-permute-done.9 = bf16[272,512]{1,0:T(8,128)(2,1)S(1)} collective-permute-done((bf16[272,512]{1,0:T(8,128)(2,1)S(1)}, bf16[272,512]{1,0:T(8,128)(2,1)S(1)}, u32[]{:S(2)}, u32[]{:S(2)}) %collective-permute-start.9) | collective-permute-done | bytes 278560 | tf_op jit(solution)/shard_map/ppermute | solution.py:33
  48.0 0.2 multiply_convert_fusion.refs_10_
  48.2 1.4 %collective-permute-start.15 = (bf16[272,512]{1,0:T(8,128)(2,1)S(1)}, bf16[272,512]{1,0:T(8,128)(2,1)S(1)}, u32[]{:S(2)}, u32[]{:S(2)}) collective-permute-start(bf16[272,512]{1,0:T(8,128)(2,1)S(1)} %multiply_convert_fusion.refs_10_), channel_id=1, source_target_pairs={{0,4},{4,1},{1,5},{5,0},{2,6},{6,3},{3,7},{7,2},{8,12},{12,9},{9,1... | collective-permute-start | bytes 835592 | tf_op jit(solution)/shard_map/ppermute | solution.py:33
  49.6 1.3 %collective-permute-start.13 = (bf16[272,512]{1,0:T(8,128)(2,1)S(1)}, bf16[272,512]{1,0:T(8,128)(2,1)S(1)}, u32[]{:S(2)}, u32[]{:S(2)}) collective-permute-start(bf16[272,512]{1,0:T(8,128)(2,1)S(1)} %multiply_convert_fusion.refs_10_), channel_id=1, source_target_pairs={{0,5},{4,0},{1,4},{5,1},{2,7},{6,2},{3,6},{7,3},{8,13},{12,8},{9,1... | collective-permute-start | bytes 835592 | tf_op jit(solution)/shard_map/ppermute | solution.py:33
  50.9 1.1 collective-permute-start.12
  52.0 5.2 %collective-permute-done.15.refs_14_ = bf16[272,512]{1,0:T(8,128)(2,1)S(1)} collective-permute-done((bf16[272,512]{1,0:T(8,128)(2,1)S(1)}, bf16[272,512]{1,0:T(8,128)(2,1)S(1)}, u32[]{:S(2)}, u32[]{:S(2)}) %collective-permute-start.15) | collective-permute-done | bytes 278560 | tf_op jit(solution)/shard_map/ppermute | solution.py:33
  57.2 1.3 %collective-permute-start.16 = (bf16[272,512]{1,0:T(8,128)(2,1)S(1)}, bf16[272,512]{1,0:T(8,128)(2,1)S(1)}, u32[]{:S(2)}, u32[]{:S(2)}) collective-permute-start(bf16[272,512]{1,0:T(8,128)(2,1)S(1)} %collective-permute-done.15.refs_14_), channel_id=1, source_target_pairs={{0,2},{2,0},{1,3},{3,1},{4,6},{6,4},{5,7},{7,5},{8,10},{10,8},{9,1... | collective-permute-start | bytes 835592 | tf_op jit(solution)/shard_map/ppermute | solution.py:45
  58.5 0.2 collective-permute-start.14
  58.7 1.0 collective-permute-start.11
  59.7 0.4 collective-permute-done.14.refs_13_
  60.1 8.4 %shard_map.70 = (f32[512,1024]{1,0:T(8,128)S(1)}, f32[512,1024]{1,0:T(8,128)S(1)}) custom-call(s32[5]{0:T(128)S(1)} %stack.26.place.refs_0_, bf16[2176,512]{1,0:T(8,128)(2,1)S(1)} %bitcast.33, bf16[2176,1024]{1,0:T(8,128)(2,1)S(1)} %get-tuple-element.50.refs_2_, bf16[2176,1024]{1,0:T(8,128)(2,1)S(1)} %get-tuple-element.51.refs_3_, ...), custom_call_target="tpu_custom_call" | custom-call | flops 5133828096 | bytes 2097152 | tf_op jit(solution)/shard_map/pallas_call | solution.py:240
  68.6 0.7 collective-permute-start.17
  69.3 1.2 %collective-permute-done.17.refs_11_ = bf16[272,512]{1,0:T(8,128)(2,1)S(1)} collective-permute-done((bf16[272,512]{1,0:T(8,128)(2,1)S(1)}, bf16[272,512]{1,0:T(8,128)(2,1)S(1)}, u32[]{:S(2)}, u32[]{:S(2)}) %collective-permute-start.17) | collective-permute-done | bytes 278560 | tf_op jit(solution)/shard_map/ppermute | solution.py:45
  70.4 5.4 %shard_map.71 = bf16[64,2,8,1024]{3,2,1,0:T(8,128)(2,1)S(1)} custom-call(s32[5]{0:T(128)S(1)} %stack.26.place.refs_0_, bf16[2176,512]{1,0:T(8,128)(2,1)S(1)} %bitcast.34, bf16[2176,1024]{1,0:T(8,128)(2,1)S(1)} %get-tuple-element.50.refs_2_, bf16[2176,1024]{1,0:T(8,128)(2,1)S(1)} %get-tuple-element.51.refs_3_, f32[128,1024]{1,0:T(8,128)S(1)} %get-tuple-element.52.refs_4_, ...), custom_call_target="tpu_custom_call" | custom-call | flops 1711276032 | bytes 2097152 | tf_op jit(solution)/shard_map/pallas_call | solution.py:240
  75.8 36.5 %all_to_all.5 = bf16[128,8,1024]{2,1,0:T(8,128)(2,1)S(1)} all-to-all(bf16[128,8,1024]{2,1,0:T(8,128)(2,1)S(1)} %bitcast.35), channel_id=1, replica_groups=mesh['x'=4,'y'=4,'zl'=2,'core'=2,'zh'=2] {'x','y','zl','core','zh'}, dimensions={0} | all-to-all | bytes 4194304 | tf_op jit(solution)/shard_map/all_to_all | solution.py:394
  112.4 1.6 %shard_map.72 = f32[1,8,8192]{2,1,0:T(8,128)} custom-call(bf16[16,8,8,1024]{3,2,1,0:T(8,128)(2,1)S(1)} %bitcast.36), custom_call_target="tpu_custom_call" | custom-call | tf_op jit(solution)/shard_map/pallas_call | solution.py:268
  (28 shorter events, 0.2 us)
Async XLA Ops:
  1.0 11.8 %collective-permute-start = (bf16[512,256]{1,0:T(8,128)(2,1)S(1)}, bf16[512,256]{1,0:T(8,128)(2,1)S(1)}, u32[]{:S(2)}, u32[]{:S(2)}) collective-permute-start(bf16[512,256]{1,0:T(8,128)(2,1)S(1)} %dynamic-slice_bitcast_fusion.1), channel_id=1, source_target_pairs={{0,5},{1,4},{4,1},{5,0},{2,7},{3,6},{6,3},{7,2},{8,13},{9,12},{12,... | collective-permute-start | bytes 786440 | tf_op jit(solution)/shard_map/ppermute | solution.py:37
  5.7 1.2 %copy-start = (bf16[8,128,512]{2,1,0:T(8,128)(2,1)S(1)}, bf16[8,128,512]{2,1,0:T(8,128)(2,1)}, u32[]{:S(2)}) copy-start(bf16[8,128,512]{2,1,0:T(8,128)(2,1)} %target_jac.1) | copy-start | bytes 3145732
  6.9 0.7 copy-start.1
  7.6 0.7 copy-start.2
  8.3 0.7 copy-start.3
  9.0 0.7 copy-start.4
  10.4 2.3 %collective-permute-start.1 = (f32[4,640]{1,0:T(4,128)S(1)}, f32[4,640]{1,0:T(4,128)S(1)}, u32[]{:S(2)}, u32[]{:S(2)}) collective-permute-start(f32[4,640]{1,0:T(4,128)S(1)} %get-tuple-element.35), channel_id=1, source_target_pairs={{0,2},{2,0},{1,3},{3,1},{4,6},{6,4},{5,7},{7,5},{8,10},{10,8},{9,1... | collective-permute-start | bytes 30728 | tf_op jit(solution)/shard_map/ppermute | solution.py:45
  12.8 5.6 %collective-permute-start.2 = (f32[8,640]{1,0:T(8,128)S(1)}, f32[8,640]{1,0:T(8,128)S(1)}, u32[]{:S(2)}, u32[]{:S(2)}) collective-permute-start(f32[8,640]{1,0:T(8,128)S(1)} %pad_maximum_fusion.1), channel_id=1, source_target_pairs={{0,4},{4,0},{1,5},{5,1},{2,6},{6,2},{3,7},{7,3},{8,12},{12,8},{9,1... | collective-permute-start | bytes 61448 | tf_op jit(solution)/shard_map/ppermute | solution.py:357
  12.9 9.0 %collective-permute-start.5 = (bf16[512,256]{1,0:T(8,128)(2,1)S(1)}, bf16[512,256]{1,0:T(8,128)(2,1)S(1)}, u32[]{:S(2)}, u32[]{:S(2)}) collective-permute-start(bf16[512,256]{1,0:T(8,128)(2,1)S(1)} %collective-permute-done.refs_7_.refs_0_.refs_6_), channel_id=1, source_target_pairs={{0,32},{32,64},{64,96},{96,0},{1,33},{33,65},{65,97},{97,1},{2,34}... | collective-permute-start | bytes 786440 | tf_op jit(solution)/shard_map/ppermute | solution.py:41
  14.2 8.0 %collective-permute-start.4 = (bf16[512,256]{1,0:T(8,128)(2,1)S(1)}, bf16[512,256]{1,0:T(8,128)(2,1)S(1)}, u32[]{:S(2)}, u32[]{:S(2)}) collective-permute-start(bf16[512,256]{1,0:T(8,128)(2,1)S(1)} %collective-permute-done.refs_7_.refs_0_.refs_6_), channel_id=1, source_target_pairs={{0,24},{8,0},{16,8},{24,16},{1,25},{9,1},{17,9},{25,17},{2,26},{10... | collective-permute-start | bytes 786440 | tf_op jit(solution)/shard_map/ppermute | solution.py:41
  16.9 7.2 %collective-permute-start.3 = (bf16[512,256]{1,0:T(8,128)(2,1)S(1)}, bf16[512,256]{1,0:T(8,128)(2,1)S(1)}, u32[]{:S(2)}, u32[]{:S(2)}) collective-permute-start(bf16[512,256]{1,0:T(8,128)(2,1)S(1)} %collective-permute-done.refs_7_.refs_0_.refs_6_), channel_id=1, source_target_pairs={{0,96},{32,0},{64,32},{96,64},{1,97},{33,1},{65,33},{97,65},{2,98}... | collective-permute-start | bytes 786440 | tf_op jit(solution)/shard_map/ppermute | solution.py:41
  26.1 3.7 %collective-permute-start.6 = (bf16[544,512]{1,0:T(8,128)(2,1)S(1)}, bf16[544,512]{1,0:T(8,128)(2,1)S(1)}, u32[]{:S(2)}, u32[]{:S(2)}) collective-permute-start(bf16[544,512]{1,0:T(8,128)(2,1)S(1)} %shard_map.65), channel_id=1, source_target_pairs={{0,2},{2,0},{1,3},{3,1},{4,6},{6,4},{5,7},{7,5},{8,10},{10,8},{9,1... | collective-permute-start | bytes 1671176 | tf_op jit(solution)/shard_map/ppermute | solution.py:45
  29.7 2.1 %collective-permute-start.7 = (bf16[544,512]{1,0:T(8,128)(2,1)S(1)}, bf16[544,512]{1,0:T(8,128)(2,1)S(1)}, u32[]{:S(2)}, u32[]{:S(2)}) collective-permute-start(bf16[544,512]{1,0:T(8,128)(2,1)S(1)} %shard_map.67), channel_id=1, source_target_pairs={{0,2},{2,0},{1,3},{3,1},{4,6},{6,4},{5,7},{7,5},{8,10},{10,8},{9,1... | collective-permute-start | bytes 1671176 | tf_op jit(solution)/shard_map/ppermute | solution.py:45
  31.8 12.9 %collective-permute-start.8 = (bf16[272,512]{1,0:T(8,128)(2,1)S(1)}, bf16[272,512]{1,0:T(8,128)(2,1)S(1)}, u32[]{:S(2)}, u32[]{:S(2)}) collective-permute-start(bf16[272,512]{1,0:T(8,128)(2,1)S(1)} %get-tuple-element.41), channel_id=1, source_target_pairs={{0,1},{4,5},{1,0},{5,4},{2,3},{6,7},{3,2},{7,6},{8,9},{12,13},{9,8... | collective-permute-start | bytes 835592 | tf_op jit(solution)/shard_map/ppermute | solution.py:33
  34.3 13.7 %collective-permute-start.9 = (bf16[272,512]{1,0:T(8,128)(2,1)S(1)}, bf16[272,512]{1,0:T(8,128)(2,1)S(1)}, u32[]{:S(2)}, u32[]{:S(2)}) collective-permute-start(bf16[272,512]{1,0:T(8,128)(2,1)S(1)} %get-tuple-element.42), channel_id=1, source_target_pairs={{0,4},{4,1},{1,5},{5,0},{2,6},{6,3},{3,7},{7,2},{8,12},{12,9},{9,1... | collective-permute-start | bytes 835592 | tf_op jit(solution)/shard_map/ppermute | solution.py:33
  36.3 11.7 %collective-permute-start.10 = (bf16[272,512]{1,0:T(8,128)(2,1)S(1)}, bf16[272,512]{1,0:T(8,128)(2,1)S(1)}, u32[]{:S(2)}, u32[]{:S(2)}) collective-permute-start(bf16[272,512]{1,0:T(8,128)(2,1)S(1)} %get-tuple-element.44), channel_id=1, source_target_pairs={{0,5},{4,0},{1,4},{5,1},{2,7},{6,2},{3,6},{7,3},{8,13},{12,8},{9,1... | collective-permute-start | bytes 835592 | tf_op jit(solution)/shard_map/ppermute | solution.py:33
  48.2 9.0 %collective-permute-start.15 = (bf16[272,512]{1,0:T(8,128)(2,1)S(1)}, bf16[272,512]{1,0:T(8,128)(2,1)S(1)}, u32[]{:S(2)}, u32[]{:S(2)}) collective-permute-start(bf16[272,512]{1,0:T(8,128)(2,1)S(1)} %multiply_convert_fusion.refs_10_), channel_id=1, source_target_pairs={{0,4},{4,1},{1,5},{5,0},{2,6},{6,3},{3,7},{7,2},{8,12},{12,9},{9,1... | collective-permute-start | bytes 835592 | tf_op jit(solution)/shard_map/ppermute | solution.py:33
  49.6 8.9 %collective-permute-start.13 = (bf16[272,512]{1,0:T(8,128)(2,1)S(1)}, bf16[272,512]{1,0:T(8,128)(2,1)S(1)}, u32[]{:S(2)}, u32[]{:S(2)}) collective-permute-start(bf16[272,512]{1,0:T(8,128)(2,1)S(1)} %multiply_convert_fusion.refs_10_), channel_id=1, source_target_pairs={{0,5},{4,0},{1,4},{5,1},{2,7},{6,2},{3,6},{7,3},{8,13},{12,8},{9,1... | collective-permute-start | bytes 835592 | tf_op jit(solution)/shard_map/ppermute | solution.py:33
  50.9 8.8 %collective-permute-start.12 = (bf16[272,512]{1,0:T(8,128)(2,1)S(1)}, bf16[272,512]{1,0:T(8,128)(2,1)S(1)}, u32[]{:S(2)}, u32[]{:S(2)}) collective-permute-start(bf16[272,512]{1,0:T(8,128)(2,1)S(1)} %multiply_convert_fusion.refs_10_), channel_id=1, source_target_pairs={{0,2},{2,0},{1,3},{3,1},{4,6},{6,4},{5,7},{7,5},{8,10},{10,8},{9,1... | collective-permute-start | bytes 835592 | tf_op jit(solution)/shard_map/ppermute | solution.py:45
  57.2 2.5 %collective-permute-start.16 = (bf16[272,512]{1,0:T(8,128)(2,1)S(1)}, bf16[272,512]{1,0:T(8,128)(2,1)S(1)}, u32[]{:S(2)}, u32[]{:S(2)}) collective-permute-start(bf16[272,512]{1,0:T(8,128)(2,1)S(1)} %collective-permute-done.15.refs_14_), channel_id=1, source_target_pairs={{0,2},{2,0},{1,3},{3,1},{4,6},{6,4},{5,7},{7,5},{8,10},{10,8},{9,1... | collective-permute-start | bytes 835592 | tf_op jit(solution)/shard_map/ppermute | solution.py:45
  58.5 1.6 %collective-permute-start.14 = (bf16[272,512]{1,0:T(8,128)(2,1)S(1)}, bf16[272,512]{1,0:T(8,128)(2,1)S(1)}, u32[]{:S(2)}, u32[]{:S(2)}) collective-permute-start(bf16[272,512]{1,0:T(8,128)(2,1)S(1)} %collective-permute-done.13.refs_12_), channel_id=1, source_target_pairs={{0,2},{2,0},{1,3},{3,1},{4,6},{6,4},{5,7},{7,5},{8,10},{10,8},{9,1... | collective-permute-start | bytes 835592 | tf_op jit(solution)/shard_map/ppermute | solution.py:45
  58.7 9.9 %collective-permute-start.11 = (bf16[272,512]{1,0:T(8,128)(2,1)S(1)}, bf16[272,512]{1,0:T(8,128)(2,1)S(1)}, u32[]{:S(2)}, u32[]{:S(2)}) collective-permute-start(bf16[272,512]{1,0:T(8,128)(2,1)S(1)} %multiply_convert_fusion.refs_10_), channel_id=1, source_target_pairs={{0,1},{4,5},{1,0},{5,4},{2,3},{6,7},{3,2},{7,6},{8,9},{12,13},{9,8... | collective-permute-start | bytes 835592 | tf_op jit(solution)/shard_map/ppermute | solution.py:33
  68.6 1.9 %collective-permute-start.17 = (bf16[272,512]{1,0:T(8,128)(2,1)S(1)}, bf16[272,512]{1,0:T(8,128)(2,1)S(1)}, u32[]{:S(2)}, u32[]{:S(2)}) collective-permute-start(bf16[272,512]{1,0:T(8,128)(2,1)S(1)} %collective-permute-done.11.refs_10_), channel_id=1, source_target_pairs={{0,2},{2,0},{1,3},{3,1},{4,6},{6,4},{5,7},{7,5},{8,10},{10,8},{9,1... | collective-permute-start | bytes 835592 | tf_op jit(solution)/shard_map/ppermute | solution.py:45

commit v8 on v7

--- a/solution.py
+++ b/solution.py
@@ -18,8 +18,8 @@
 GROUP = 4 * CHUNK
 STEP = 2 * CHUNK
 LIMIT = 24 * 2**20
-ORDER = (0, 1, 3, 2)
-EARLY = 6
+PLACES = (0, 4, 1, 3, 5, 7, 2, 6)
+EARLY = 4
 jacobian_weight = 32.0
 f32 = jnp.float32
 bf16 = jnp.bfloat16
@@ -178,73 +178,80 @@
     )(place, rows, own, *other)
 
 
-def backward_kernel(count, place, rows, picked, tangents, linears, own, *refs):
-    other, misfits, refs = refs[:4], refs[4 : 4 + count], refs[4 + count :]
-    cotangents = refs[-1]
-    theirs = piece_of(pl.program_id(0), other)
-    w_last = jnp.where(place[4] == 0, theirs, own[...])
-    for c in range(count):
-        span = pl.ds(c * CHUNK, CHUNK)
-        back = jnp.dot(misfits[c][...], w_last, preferred_element_type=f32)
-        back = back.astype(bf16).astype(f32)
-        _, first, second = slopes(linears[pl.ds(c * 16, 16), :])
-        joint = back[: 2 * TANGENTS] * picked[pl.ds(c * CHUNK, 2 * TANGENTS), :].astype(f32)
-        projected = jnp.concatenate(
-            [
-                jnp.sum(joint[:TANGENTS], axis=0, keepdims=True),
-                jnp.sum(joint[TANGENTS:], axis=0, keepdims=True),
-                jnp.zeros((14, BLOCK), f32),
-            ],
-            axis=0,
+def backward_kernel(count, place, rows, picked, tangents, linears, *refs):
+    own, other, misfits, refs = refs[:4], refs[4:8], refs[8 : 8 + count], refs[8 + count :]
+    w_last, cotangents = refs[-2:]
+    outs = refs[:-2]
+    here = place[4] == 0
+    for k in range(4):
+        w_last[:, k * BLOCK : (k + 1) * BLOCK] = jnp.where(here, other[k][...], own[k][...])
+    whole = jnp.concatenate([m[...] for m in misfits], axis=0)
+    for c in range(0, count, 2):
+        back = jnp.dot(
+            whole[c * CHUNK : (c + 2) * CHUNK], w_last[...], preferred_element_type=f32
         )
-        before = back[2 * TANGENTS :] * first + second * projected
-        cotangents[span, :] = jnp.concatenate(per_row(back, first) + [before], axis=0).astype(bf16)
+        parts = []
+        for e in range(2):
+            part = back[e * CHUNK : (e + 1) * CHUNK].astype(bf16).astype(f32)
+            _, first, second = slopes(linears[(c + e) * 16 : (c + e + 1) * 16, :])
+            start = (c + e) * CHUNK
+            joint = part[: 2 * TANGENTS] * picked[start : start + 2 * TANGENTS, :].astype(f32)
+            projected = jnp.concatenate(
+                [
+                    jnp.sum(joint[:TANGENTS], axis=0, keepdims=True),
+                    jnp.sum(joint[TANGENTS:], axis=0, keepdims=True),
+                    jnp.zeros((14, COLS), f32),
+                ],
+                axis=0,
+            )
+            before = part[2 * TANGENTS :] * first + second * projected
+            parts += per_row(part, first) + [before]
+        cotangents[c * CHUNK : (c + 2) * CHUNK, :] = jnp.concatenate(parts, axis=0).astype(bf16)
     over_rows = (((0,), (0,)), ((), ()))
-    whole = jnp.concatenate([m[...] for m in misfits], axis=0)
     last = lax.dot_general(whole, tangents[...], over_rows, preferred_element_type=f32)
     first = lax.dot_general(rows[...], cotangents[...], over_rows, preferred_element_type=f32)
-    if count == EARLY:
-        first_out, last_out = refs[:2]
-        first_out[...] = first
-        last_out[...] = last
+    if len(outs) == 2:
+        outs[0][...] = first
+        outs[1][...] = last
         return
-    first_so_far, last_so_far, out = refs[:3]
-    first = first + first_so_far[...]
-    last = last + last_so_far[...]
-    out[:, 0] = first.astype(bf16).reshape(64, 8, BLOCK)
-    out[:, 1] = last.astype(bf16).reshape(64, 8, BLOCK)
+    first_so_far, last_so_far, out = outs
+    out[:, 0] = (first + first_so_far[...]).astype(bf16).reshape(64, 8, COLS)
+    out[:, 1] = (last + last_so_far[...]).astype(bf16).reshape(64, 8, COLS)
 
 
 def backward(place, rows, prepared, own, other, misfits, so_far=None):
     count = len(misfits)
-    height, block = count * CHUNK, 0 if so_far is None else 3
-    columns = lambda height, at=0: pl.BlockSpec((height, BLOCK), lambda j, place: (at, j))
+    height, block = count * CHUNK, 0 if so_far is None else 1
+    columns = lambda height, at=0: pl.BlockSpec((height, COLS), lambda j, place: (at, 0))
     in_specs = [
         pl.BlockSpec((height, REDUCED), lambda j, place: (block, 0)),
         columns(height, block),
         columns(height, block),
         columns(16 * count, block),
-        pl.BlockSpec((REDUCED, BLOCK), lambda j, place: (0, place[j])),
+        *own_specs(),
         *[whole_spec((REDUCED, BLOCK))] * 4,
         *[whole_spec((CHUNK, REDUCED))] * count,
     ]
-    args = [rows, *prepared, own, *other, *misfits]
+    args = [rows, *prepared, own, own, own, own, *other, *misfits]
     if so_far is None:
         out_specs = [columns(REDUCED)] * 2
         out_shape = [jax.ShapeDtypeStruct((REDUCED, COLS), f32)] * 2
     else:
         in_specs += [columns(REDUCED)] * 2
         args += so_far
-        out_specs = pl.BlockSpec((64, 2, 8, BLOCK), lambda j, place: (0, 0, 0, place[j]))
+        out_specs = whole_spec((64, 2, 8, COLS))
         out_shape = jax.ShapeDtypeStruct((64, 2, 8, COLS), bf16)
     return pl.pallas_call(
         lambda *refs: backward_kernel(count, *refs),
         grid_spec=pltpu.PrefetchScalarGridSpec(
             num_scalar_prefetch=1,
-            grid=(4,),
+            grid=(1,),
             in_specs=in_specs,
             out_specs=out_specs,
-            scratch_shapes=[pltpu.VMEM((height, BLOCK), bf16)],
+            scratch_shapes=[
+                pltpu.VMEM((REDUCED, COLS), bf16),
+                pltpu.VMEM((height, COLS), bf16),
+            ],
         ),
         out_shape=out_shape,
         compiler_params=pltpu.CompilerParams(
@@ -258,10 +265,13 @@
 
 def total_kernel(pieces, out):
     for u in range(2):
-        total = pieces[0, u].astype(f32)
-        for k in range(1, 16):
-            total = total + pieces[k, u].astype(f32)
-        out[0, :, u * COLS : (u + 1) * COLS] = total
+        for block in range(4):
+            total = jnp.zeros((8, BLOCK), f32)
+            for k in range(16):
+                at = (block - (k // 4 + 2 * (k % 4))) % 4 * BLOCK
+                total = total + pieces[k, u, :, at : at + BLOCK].astype(f32)
+            start = u * COLS + block * BLOCK
+            out[0, :, start : start + BLOCK] = total
 
 
 def total_of(pieces):
@@ -359,17 +369,19 @@
     high = jnp.where(zl == 0, beside, pair).reshape(2, 2, 2, REDUCED + TANGENTS)
     small = jnp.stack([low, high], axis=2).reshape(2, 4, 2, REDUCED + TANGENTS)
     small = lax.dynamic_slice_in_dim(jnp.concatenate([small, small], axis=1), z, 4, 1)
-    small = jnp.concatenate([small[:, d : d + 1] for d in ORDER], axis=1).swapaxes(0, 1)
     small = small.reshape(8, 2, REDUCED + TANGENTS)
+    small = jnp.concatenate([small[p : p + 1] for p in PLACES], axis=0)
     chosen = small[:, :, REDUCED:].reshape(8, 2 * TANGENTS).astype(jnp.int32)
     onehot = (chosen[:, :, None] == jnp.arange(REDUCED, dtype=jnp.int32)).astype(bf16)
     inputs = jnp.pad(small[:, :, :REDUCED].astype(bf16), ((0, 0), (0, 14), (0, 0)))
     rows = jnp.concatenate([onehot, inputs], axis=1).reshape(2 * GROUP, REDUCED)
 
-    pairs = ((6, 2), (4, 0))
+    at = PLACES.index
+    pairs = ((2, 1), (3, 0))
     arrived = []
     for one, two in pairs:
-        arrived.append(core_swap(forward(place, rows, (one + 1, two + 1), own, other)))
+        arrived.append(core_swap(forward(place, rows, (at(4 + one), at(4 + two)), own, other)))
+    pairs = [(at(one), at(two)) for one, two in pairs]
     ahead = forward(place, rows, pairs[0], own, other, arrived[0], (bf16, bf16))
     ahead, second = lax.optimization_barrier((ahead, arrived[1]))
     got = [z_shift(ahead[0], 2), z_shift(ahead[1], 1)]
@@ -382,14 +394,15 @@
         total = total + g.astype(f32)
     scale = jnp.where(jnp.arange(CHUNK)[:, None] < 2 * TANGENTS, jacobian_weight, 1.0)
     misfit = (scale * (total - wanted)).astype(bf16)
-    near, early = [misfit], []
-    for d in ORDER[1:]:
-        near.append(z_shift(misfit, 4 - d))
-    for part in near[:3]:
-        early += [part, core_swap(part)]
-    so_far = backward(place, rows, prepared, own, other, early)
-    near[3], so_far = lax.optimization_barrier((near[3], so_far))
-    late = [near[3], core_swap(near[3])]
+    parts = {0: misfit}
+    for d in (1, 3, 2):
+        parts[d] = z_shift(misfit, 4 - d)
+    for d in (0, 1, 3):
+        parts[4 + d] = core_swap(parts[d])
+    so_far = backward(place, rows, prepared, own, other, [parts[p] for p in PLACES[:EARLY]])
+    parts[2], so_far = lax.optimization_barrier((parts[2], so_far))
+    parts[6] = core_swap(parts[2])
+    late = [parts[p] for p in PLACES[EARLY:]]
     sent = backward(place, rows, prepared, own, other, late, so_far)
     pieces = lax.all_to_all(
         sent.reshape(128, 8, COLS), AXES, split_axis=0, concat_axis=0, tiled=True

time: 114 us -> 115 us (level)
  blocking collectives: 36.5 us -> 41.5 us
  Pallas kernels: 29.8 us -> 25.5 us
  waiting for transfers between devices: 14.8 us -> 16.6 us
  starting transfers between devices: 25.2 us -> 23.7 us
    all_to_all x1, blocking collectives: 36.5 us -> 41.5 us  [shards(): lax.all_to_all(sent.reshape(128, 8, COLS), AXES, split_axis=0, concat_axi...]
    pallas_call x2, Pallas kernels: 13.8 us -> 9.55 us  [backward(): pl.pallas_call(lambda *refs: backward_kernel(count, *refs), grid_spec=plt...]
    ppermute x6, waiting for transfers between devices: 8.48 us -> 10.4 us  [z_shift(): lax.ppermute(block, Z, [(z_index(z), z_index((z + d) % 4)) for z in range...]
    ppermute x7, starting transfers between devices: 6 us -> 4.77 us  [core_swap(): return lax.ppermute(block, 'core', [(0, 1), (1, 0)])]
    unnamed x11 -> x18, local copies, waits for them, and re-layouts: 3.96 us -> 4.02 us
  transfers between devices with their start and end apart: 18 -> 18, of which waited for: 7 -> 9; matrix products, arithmetic and copies ran while one was open for 2% -> 2% of each run, Pallas kernels for 18% -> 15%
where the time goes in v8:
time: 115 us
  blocking collectives  41.5 us (36%)
  Pallas kernels  25.5 us (22%)
  starting transfers between devices  23.7 us (21%)
  waiting for transfers between devices  16.6 us (14%)
  local copies, waits for them, and re-layouts  6.42 us (6%)
    all_to_all x1, blocking collectives, shards(): lax.all_to_all(sent.reshape(128, 8, COLS), AXES, split_axis=0, concat_axi...  41.5 us
    ppermute x6, waiting for transfers between devices, z_shift(): lax.ppermute(block, Z, [(z_index(z), z_index((z + d) % 4)) for z in range...  10.4 us
    pallas_call x2, Pallas kernels, backward(): pl.pallas_call(lambda *refs: backward_kernel(count, *refs), grid_spec=plt...  9.55 us
    ppermute x6, starting transfers between devices, z_shift(): lax.ppermute(block, Z, [(z_index(z), z_index((z + d) % 4)) for z in range...  8.68 us
    pallas_call x4, Pallas kernels, forward(): pl.pallas_call(lambda *refs: forward_kernel(final, *refs), grid_spec=pltp...  8 us
    pallas_call x1, Pallas kernels, prepare(): pl.pallas_call(prepare_kernel, grid_spec=pltpu.PrefetchScalarGridSpec(num...  5.64 us
    ppermute x3, starting transfers between devices, ring_shift(): return lax.ppermute(block, axis, [(i, (i + d) % 4) for i in range(4)])  5.48 us
    ppermute x7, starting transfers between devices, core_swap(): return lax.ppermute(block, 'core', [(0, 1), (1, 0)])  4.77 us
  transfers between devices with their start and end apart: 18, of which 9 were waited for; matrix products, arithmetic and copies ran while one was open for 2% of the time, Pallas kernels for 15%

profile of v8, /device:TPU:1, one launch (start us, length us, event | category | flops | bytes accessed | tf_op | source)
XLA Modules:
  0.0 115.0 jit_solution(2125736884592827425)
XLA Ops:
  0.0 1.0 dynamic-slice_bitcast_fusion.1
  1.0 4.7 %collective-permute-start = (bf16[512,256]{1,0:T(8,128)(2,1)S(1)}, bf16[512,256]{1,0:T(8,128)(2,1)S(1)}, u32[]{:S(2)}, u32[]{:S(2)}) collective-permute-start(bf16[512,256]{1,0:T(8,128)(2,1)S(1)} %dynamic-slice_bitcast_fusion.1), channel_id=1, source_target_pairs={{0,5},{1,4},{4,1},{5,0},{2,7},{3,6},{6,3},{7,2},{8,13},{9,12},{12,... | collective-permute-start | bytes 786440 | tf_op jit(solution)/shard_map/ppermute | solution.py:37
  5.6 0.1 stack.26.place.refs_0_
  5.7 1.2 %copy-done = bf16[8,128,512]{2,1,0:T(8,128)(2,1)S(1)} copy-done((bf16[8,128,512]{2,1,0:T(8,128)(2,1)S(1)}, bf16[8,128,512]{2,1,0:T(8,128)(2,1)}, u32[]{:S(2)}) %copy-start) | copy-done | bytes 1048600
  6.9 0.7 copy-done.1
  7.6 0.7 copy-done.2
  8.3 0.7 copy-done.3
  9.0 0.7 copy-done.4
  9.7 0.7 shard_map.64
  10.4 1.0 collective-permute-start.1
  11.4 1.3 %dynamic-slice_bitcast_fusion.refs_3_.refs_4_.refs_5_.refs_6_.own.refs_7_.refs_8_ = bf16[512,1024]{1,0:T(8,128)(2,1)S(1)} fusion(bf16[1,512,8192]{2,1,0:T(8,128)(2,1)} %param.11, s32[]{:T(128)S(6)} %select_n.60), kind=kLoop, calls=%fused_computation.5 | loop fusion | bytes 2097156 | tf_op jit(solution)/shard_map/dynamic_slice | solution.py:353
  12.7 0.0 collective-permute-done.1
  12.8 0.1 collective-permute-start.2
  12.9 1.3 %collective-permute-start.5 = (bf16[512,256]{1,0:T(8,128)(2,1)S(1)}, bf16[512,256]{1,0:T(8,128)(2,1)S(1)}, u32[]{:S(2)}, u32[]{:S(2)}) collective-permute-start(bf16[512,256]{1,0:T(8,128)(2,1)S(1)} %collective-permute-done.refs_7_.refs_0_.refs_9_), channel_id=1, source_target_pairs={{0,32},{32,64},{64,96},{96,0},{1,33},{33,65},{65,97},{97,1},{2,34}... | collective-permute-start | bytes 786440 | tf_op jit(solution)/shard_map/ppermute | solution.py:41
  14.2 2.7 %collective-permute-start.4 = (bf16[512,256]{1,0:T(8,128)(2,1)S(1)}, bf16[512,256]{1,0:T(8,128)(2,1)S(1)}, u32[]{:S(2)}, u32[]{:S(2)}) collective-permute-start(bf16[512,256]{1,0:T(8,128)(2,1)S(1)} %collective-permute-done.refs_7_.refs_0_.refs_9_), channel_id=1, source_target_pairs={{0,24},{8,0},{16,8},{24,16},{1,25},{9,1},{17,9},{25,17},{2,26},{10... | collective-permute-start | bytes 786440 | tf_op jit(solution)/shard_map/ppermute | solution.py:41
  16.9 1.5 %collective-permute-start.3 = (bf16[512,256]{1,0:T(8,128)(2,1)S(1)}, bf16[512,256]{1,0:T(8,128)(2,1)S(1)}, u32[]{:S(2)}, u32[]{:S(2)}) collective-permute-start(bf16[512,256]{1,0:T(8,128)(2,1)S(1)} %collective-permute-done.refs_7_.refs_0_.refs_9_), channel_id=1, source_target_pairs={{0,96},{32,0},{64,32},{96,64},{1,97},{33,1},{65,33},{97,65},{2,98}... | collective-permute-start | bytes 786440 | tf_op jit(solution)/shard_map/ppermute | solution.py:41
  18.6 0.5 fusion.1
  19.2 0.2 fusion.2
  19.4 2.5 %collective-permute-done.5.refs_10_.refs_3_.refs_12_ = bf16[512,256]{1,0:T(8,128)(2,1)S(1)} collective-permute-done((bf16[512,256]{1,0:T(8,128)(2,1)S(1)}, bf16[512,256]{1,0:T(8,128)(2,1)S(1)}, u32[]{:S(2)}, u32[]{:S(2)}) %collective-permute-start.5) | collective-permute-done | bytes 262176 | tf_op jit(solution)/shard_map/ppermute | solution.py:41
  21.9 0.3 collective-permute-done.4.refs_9_.refs_2_.refs_11_
  22.2 1.9 %collective-permute-done.3.refs_8_.refs_1_.refs_10_ = bf16[512,256]{1,0:T(8,128)(2,1)S(1)} collective-permute-done((bf16[512,256]{1,0:T(8,128)(2,1)S(1)}, bf16[512,256]{1,0:T(8,128)(2,1)S(1)}, u32[]{:S(2)}, u32[]{:S(2)}) %collective-permute-start.3) | collective-permute-done | bytes 262176 | tf_op jit(solution)/shard_map/ppermute | solution.py:41
  24.1 2.0 %shard_map.65 = bf16[544,512]{1,0:T(8,128)(2,1)S(1)} custom-call(s32[5]{0:T(128)S(1)} %stack.26.place.refs_0_, bf16[2176,512]{1,0:T(8,128)(2,1)S(1)} %bitcast.22, bf16[2176,512]{1,0:T(8,128)(2,1)S(1)} %bitcast.23, bf16[512,1024]{1,0:T(8,128)(2,1)S(1)} %dynamic-slice_bitcast_fusion.refs_3_.refs_4_.refs_5_.refs_6_.own.refs_7_.refs_8_, ...), custom_call_target="tpu_custom_call" | custom-call | flops 1140850688 | bytes 2097152 | tf_op jit(solution)/shard_map/pallas_call | solution.py:109
  26.1 1.6 %collective-permute-start.6 = (bf16[544,512]{1,0:T(8,128)(2,1)S(1)}, bf16[544,512]{1,0:T(8,128)(2,1)S(1)}, u32[]{:S(2)}, u32[]{:S(2)}) collective-permute-start(bf16[544,512]{1,0:T(8,128)(2,1)S(1)} %shard_map.65), channel_id=1, source_target_pairs={{0,2},{2,0},{1,3},{3,1},{4,6},{6,4},{5,7},{7,5},{8,10},{10,8},{9,1... | collective-permute-start | bytes 1671176 | tf_op jit(solution)/shard_map/ppermute | solution.py:45
  27.7 2.0 %shard_map.67 = bf16[544,512]{1,0:T(8,128)(2,1)S(1)} custom-call(s32[5]{0:T(128)S(1)} %stack.26.place.refs_0_, bf16[2176,512]{1,0:T(8,128)(2,1)S(1)} %bitcast.24, bf16[2176,512]{1,0:T(8,128)(2,1)S(1)} %bitcast.25, bf16[512,1024]{1,0:T(8,128)(2,1)S(1)} %dynamic-slice_bitcast_fusion.refs_3_.refs_4_.refs_5_.refs_6_.own.refs_7_.refs_8_, ...), custom_call_target="tpu_custom_call" | custom-call | flops 1140850688 | bytes 2097152 | tf_op jit(solution)/shard_map/pallas_call | solution.py:109
  29.7 0.1 collective-permute-start.7
  29.8 2.0 %shard_map.66 = (bf16[272,512]{1,0:T(8,128)(2,1)S(1)}, bf16[272,512]{1,0:T(8,128)(2,1)S(1)}) custom-call(s32[5]{0:T(128)S(1)} %stack.26.place.refs_0_, bf16[2176,512]{1,0:T(8,128)(2,1)S(1)} %bitcast.26, bf16[2176,512]{1,0:T(8,128)(2,1)S(1)} %bitcast.27, bf16[512,1024]{1,0:T(8,128)(2,1)S(1)} %dynamic-slice_bitcast_fusion.refs_3_.refs_4_.refs_5_.refs_6_.own.refs_7_.refs_8_, ...), custom_call_target="tpu_custom_call" | custom-call | flops 1140850688 | bytes 2097152 | tf_op jit(solution)/shard_map/pallas_call | solution.py:109
  31.8 2.4 %collective-permute-start.8 = (bf16[272,512]{1,0:T(8,128)(2,1)S(1)}, bf16[272,512]{1,0:T(8,128)(2,1)S(1)}, u32[]{:S(2)}, u32[]{:S(2)}) collective-permute-start(bf16[272,512]{1,0:T(8,128)(2,1)S(1)} %get-tuple-element.41), channel_id=1, source_target_pairs={{0,1},{4,5},{1,0},{5,4},{2,3},{6,7},{3,2},{7,6},{8,9},{12,13},{9,8... | collective-permute-start | bytes 835592 | tf_op jit(solution)/shard_map/ppermute | solution.py:33
  34.3 2.0 %shard_map.68 = (bf16[272,512]{1,0:T(8,128)(2,1)S(1)}, f32[272,512]{1,0:T(8,128)S(1)}) custom-call(s32[5]{0:T(128)S(1)} %stack.26.place.refs_0_, bf16[2176,512]{1,0:T(8,128)(2,1)S(1)} %bitcast.28, bf16[2176,512]{1,0:T(8,128)(2,1)S(1)} %bitcast.29, bf16[512,1024]{1,0:T(8,128)(2,1)S(1)} %dynamic-slice_bitcast_fusion.refs_3_.refs_4_.refs_5_.refs_6_.own.refs_7_.refs_8_, ...), custom_call_target="tpu_custom_call" | custom-call | flops 1140850688 | bytes 2097152 | tf_op jit(solution)/shard_map/pallas_call | solution.py:109
  36.3 2.8 %collective-permute-start.10 = (bf16[272,512]{1,0:T(8,128)(2,1)S(1)}, bf16[272,512]{1,0:T(8,128)(2,1)S(1)}, u32[]{:S(2)}, u32[]{:S(2)}) collective-permute-start(bf16[272,512]{1,0:T(8,128)(2,1)S(1)} %get-tuple-element.44), channel_id=1, source_target_pairs={{0,5},{4,0},{1,4},{5,1},{2,7},{6,2},{3,6},{7,3},{8,13},{12,8},{9,1... | collective-permute-start | bytes 835592 | tf_op jit(solution)/shard_map/ppermute | solution.py:33
  39.1 5.6 %shard_map.69 = (bf16[2176,1024]{1,0:T(8,128)(2,1)S(1)}, bf16[2176,1024]{1,0:T(8,128)(2,1)S(1)}, f32[128,1024]{1,0:T(8,128)S(1)}) custom-call(s32[5]{0:T(128)S(1)} %stack.26.place.refs_0_, bf16[2176,512]{1,0:T(8,128)(2,1)S(1)} %bitcast.30, bf16[512,1024]{1,0:T(8,128)(2,1)S(1)} %dynamic-slice_bitcast_fusion.refs_3_.refs_4_.refs_5_.refs_6_.own.refs_7_.refs_8_, ...), custom_call_target="tpu_custom_call" | custom-call | flops 2281701376 | bytes 2097152 | tf_op jit(solution)/shard_map/pallas_call | solution.py:155
  44.7 3.3 %collective-permute-done.9 = bf16[272,512]{1,0:T(8,128)(2,1)S(1)} collective-permute-done((bf16[272,512]{1,0:T(8,128)(2,1)S(1)}, bf16[272,512]{1,0:T(8,128)(2,1)S(1)}, u32[]{:S(2)}, u32[]{:S(2)}) %collective-permute-start.9) | collective-permute-done | bytes 278560 | tf_op jit(solution)/shard_map/ppermute | solution.py:33
  48.0 0.2 multiply_convert_fusion.refs_13_
  48.2 0.6 collective-permute-start.16
  48.7 1.4 %collective-permute-start.13 = (bf16[272,512]{1,0:T(8,128)(2,1)S(1)}, bf16[272,512]{1,0:T(8,128)(2,1)S(1)}, u32[]{:S(2)}, u32[]{:S(2)}) collective-permute-start(bf16[272,512]{1,0:T(8,128)(2,1)S(1)} %multiply_convert_fusion.refs_13_), channel_id=1, source_target_pairs={{0,4},{4,1},{1,5},{5,0},{2,6},{6,3},{3,7},{7,2},{8,12},{12,9},{9,1... | collective-permute-start | bytes 835592 | tf_op jit(solution)/shard_map/ppermute | solution.py:33
  50.1 1.3 %collective-permute-start.11 = (bf16[272,512]{1,0:T(8,128)(2,1)S(1)}, bf16[272,512]{1,0:T(8,128)(2,1)S(1)}, u32[]{:S(2)}, u32[]{:S(2)}) collective-permute-start(bf16[272,512]{1,0:T(8,128)(2,1)S(1)} %multiply_convert_fusion.refs_13_), channel_id=1, source_target_pairs={{0,5},{4,0},{1,4},{5,1},{2,7},{6,2},{3,6},{7,3},{8,13},{12,8},{9,1... | collective-permute-start | bytes 835592 | tf_op jit(solution)/shard_map/ppermute | solution.py:33
  51.4 0.8 collective-permute-start.15
  52.2 5.9 %collective-permute-done.13.refs_16_ = bf16[272,512]{1,0:T(8,128)(2,1)S(1)} collective-permute-done((bf16[272,512]{1,0:T(8,128)(2,1)S(1)}, bf16[272,512]{1,0:T(8,128)(2,1)S(1)}, u32[]{:S(2)}, u32[]{:S(2)}) %collective-permute-start.13) | collective-permute-done | bytes 278560 | tf_op jit(solution)/shard_map/ppermute | solution.py:33
  58.1 4.7 %shard_map.70 = (f32[512,1024]{1,0:T(8,128)S(1)}, f32[512,1024]{1,0:T(8,128)S(1)}) custom-call(s32[5]{0:T(128)S(1)} %stack.26.place.refs_0_, bf16[2176,512]{1,0:T(8,128)(2,1)S(1)} %bitcast.31, bf16[2176,1024]{1,0:T(8,128)(2,1)S(1)} %get-tuple-element.50.refs_2_, bf16[2176,1024]{1,0:T(8,128)(2,1)S(1)} %get-tuple-element.51.refs_3_, ...), custom_call_target="tpu_custom_call" | custom-call | flops 3422552064 | bytes 2097152 | tf_op jit(solution)/shard_map/pallas_call | solution.py:244
  62.8 1.3 %collective-permute-done.15.refs_15_ = bf16[272,512]{1,0:T(8,128)(2,1)S(1)} collective-permute-done((bf16[272,512]{1,0:T(8,128)(2,1)S(1)}, bf16[272,512]{1,0:T(8,128)(2,1)S(1)}, u32[]{:S(2)}, u32[]{:S(2)}) %collective-permute-start.15) | collective-permute-done | bytes 278560 | tf_op jit(solution)/shard_map/ppermute | solution.py:33
  64.1 0.9 collective-permute-start.14
  65.0 0.0 collective-permute-start.12
  65.0 0.5 collective-permute-start.17
  65.5 0.7 collective-permute-done.14.refs_14_
  66.2 0.4 collective-permute-done.12.refs_13_
  66.6 0.4 collective-permute-done.17.refs_16_
  67.0 4.8 %shard_map.71 = bf16[64,2,8,1024]{3,2,1,0:T(8,128)(2,1)S(1)} custom-call(s32[5]{0:T(128)S(1)} %stack.26.place.refs_0_, bf16[2176,512]{1,0:T(8,128)(2,1)S(1)} %bitcast.32, bf16[2176,1024]{1,0:T(8,128)(2,1)S(1)} %get-tuple-element.50.refs_2_, bf16[2176,1024]{1,0:T(8,128)(2,1)S(1)} %get-tuple-element.51.refs_3_, f32[128,1024]{1,0:T(8,128)S(1)} %get-tuple-element.52.refs_4_, ...), custom_call_target="tpu_custom_call" | custom-call | flops 3422552064 | bytes 2097152 | tf_op jit(solution)/shard_map/pallas_call | solution.py:244
  71.8 41.5 %all_to_all.5 = bf16[128,8,1024]{2,1,0:T(8,128)(2,1)S(1)} all-to-all(bf16[128,8,1024]{2,1,0:T(8,128)(2,1)S(1)} %bitcast.34), channel_id=1, replica_groups=mesh['x'=4,'y'=4,'zl'=2,'core'=2,'zh'=2] {'x','y','zl','core','zh'}, dimensions={0} | all-to-all | bytes 4194304 | tf_op jit(solution)/shard_map/all_to_all | solution.py:407
  113.3 1.6 %shard_map.72 = f32[1,8,8192]{2,1,0:T(8,128)} custom-call(bf16[16,8,8,1024]{3,2,1,0:T(8,128)(2,1)S(1)} %bitcast.33), custom_call_target="tpu_custom_call" | custom-call | tf_op jit(solution)/shard_map/pallas_call | solution.py:278
  (32 shorter events, 0.2 us)
Async XLA Ops:
  1.0 11.8 %collective-permute-start = (bf16[512,256]{1,0:T(8,128)(2,1)S(1)}, bf16[512,256]{1,0:T(8,128)(2,1)S(1)}, u32[]{:S(2)}, u32[]{:S(2)}) collective-permute-start(bf16[512,256]{1,0:T(8,128)(2,1)S(1)} %dynamic-slice_bitcast_fusion.1), channel_id=1, source_target_pairs={{0,5},{1,4},{4,1},{5,0},{2,7},{3,6},{6,3},{7,2},{8,13},{9,12},{12,... | collective-permute-start | bytes 786440 | tf_op jit(solution)/shard_map/ppermute | solution.py:37
  5.7 1.2 %copy-start = (bf16[8,128,512]{2,1,0:T(8,128)(2,1)S(1)}, bf16[8,128,512]{2,1,0:T(8,128)(2,1)}, u32[]{:S(2)}) copy-start(bf16[8,128,512]{2,1,0:T(8,128)(2,1)} %target_jac.1) | copy-start | bytes 3145732
  6.9 0.7 copy-start.1
  7.6 0.7 copy-start.2
  8.3 0.7 copy-start.3
  9.0 0.7 copy-start.4
  10.4 2.3 %collective-permute-start.1 = (f32[4,640]{1,0:T(4,128)S(1)}, f32[4,640]{1,0:T(4,128)S(1)}, u32[]{:S(2)}, u32[]{:S(2)}) collective-permute-start(f32[4,640]{1,0:T(4,128)S(1)} %get-tuple-element.35), channel_id=1, source_target_pairs={{0,2},{2,0},{1,3},{3,1},{4,6},{6,4},{5,7},{7,5},{8,10},{10,8},{9,1... | collective-permute-start | bytes 30728 | tf_op jit(solution)/shard_map/ppermute | solution.py:45
  12.8 5.6 %collective-permute-start.2 = (f32[8,640]{1,0:T(8,128)S(1)}, f32[8,640]{1,0:T(8,128)S(1)}, u32[]{:S(2)}, u32[]{:S(2)}) collective-permute-start(f32[8,640]{1,0:T(8,128)S(1)} %pad_maximum_fusion.1), channel_id=1, source_target_pairs={{0,4},{4,0},{1,5},{5,1},{2,6},{6,2},{3,7},{7,3},{8,12},{12,8},{9,1... | collective-permute-start | bytes 61448 | tf_op jit(solution)/shard_map/ppermute | solution.py:367
  12.9 9.0 %collective-permute-start.5 = (bf16[512,256]{1,0:T(8,128)(2,1)S(1)}, bf16[512,256]{1,0:T(8,128)(2,1)S(1)}, u32[]{:S(2)}, u32[]{:S(2)}) collective-permute-start(bf16[512,256]{1,0:T(8,128)(2,1)S(1)} %collective-permute-done.refs_7_.refs_0_.refs_9_), channel_id=1, source_target_pairs={{0,32},{32,64},{64,96},{96,0},{1,33},{33,65},{65,97},{97,1},{2,34}... | collective-permute-start | bytes 786440 | tf_op jit(solution)/shard_map/ppermute | solution.py:41
  14.2 8.0 %collective-permute-start.4 = (bf16[512,256]{1,0:T(8,128)(2,1)S(1)}, bf16[512,256]{1,0:T(8,128)(2,1)S(1)}, u32[]{:S(2)}, u32[]{:S(2)}) collective-permute-start(bf16[512,256]{1,0:T(8,128)(2,1)S(1)} %collective-permute-done.refs_7_.refs_0_.refs_9_), channel_id=1, source_target_pairs={{0,24},{8,0},{16,8},{24,16},{1,25},{9,1},{17,9},{25,17},{2,26},{10... | collective-permute-start | bytes 786440 | tf_op jit(solution)/shard_map/ppermute | solution.py:41
  16.9 7.2 %collective-permute-start.3 = (bf16[512,256]{1,0:T(8,128)(2,1)S(1)}, bf16[512,256]{1,0:T(8,128)(2,1)S(1)}, u32[]{:S(2)}, u32[]{:S(2)}) collective-permute-start(bf16[512,256]{1,0:T(8,128)(2,1)S(1)} %collective-permute-done.refs_7_.refs_0_.refs_9_), channel_id=1, source_target_pairs={{0,96},{32,0},{64,32},{96,64},{1,97},{33,1},{65,33},{97,65},{2,98}... | collective-permute-start | bytes 786440 | tf_op jit(solution)/shard_map/ppermute | solution.py:41
  26.1 3.7 %collective-permute-start.6 = (bf16[544,512]{1,0:T(8,128)(2,1)S(1)}, bf16[544,512]{1,0:T(8,128)(2,1)S(1)}, u32[]{:S(2)}, u32[]{:S(2)}) collective-permute-start(bf16[544,512]{1,0:T(8,128)(2,1)S(1)} %shard_map.65), channel_id=1, source_target_pairs={{0,2},{2,0},{1,3},{3,1},{4,6},{6,4},{5,7},{7,5},{8,10},{10,8},{9,1... | collective-permute-start | bytes 1671176 | tf_op jit(solution)/shard_map/ppermute | solution.py:45
  29.7 2.1 %collective-permute-start.7 = (bf16[544,512]{1,0:T(8,128)(2,1)S(1)}, bf16[544,512]{1,0:T(8,128)(2,1)S(1)}, u32[]{:S(2)}, u32[]{:S(2)}) collective-permute-start(bf16[544,512]{1,0:T(8,128)(2,1)S(1)} %shard_map.67), channel_id=1, source_target_pairs={{0,2},{2,0},{1,3},{3,1},{4,6},{6,4},{5,7},{7,5},{8,10},{10,8},{9,1... | collective-permute-start | bytes 1671176 | tf_op jit(solution)/shard_map/ppermute | solution.py:45
  31.8 12.9 %collective-permute-start.8 = (bf16[272,512]{1,0:T(8,128)(2,1)S(1)}, bf16[272,512]{1,0:T(8,128)(2,1)S(1)}, u32[]{:S(2)}, u32[]{:S(2)}) collective-permute-start(bf16[272,512]{1,0:T(8,128)(2,1)S(1)} %get-tuple-element.41), channel_id=1, source_target_pairs={{0,1},{4,5},{1,0},{5,4},{2,3},{6,7},{3,2},{7,6},{8,9},{12,13},{9,8... | collective-permute-start | bytes 835592 | tf_op jit(solution)/shard_map/ppermute | solution.py:33
  34.3 13.7 %collective-permute-start.9 = (bf16[272,512]{1,0:T(8,128)(2,1)S(1)}, bf16[272,512]{1,0:T(8,128)(2,1)S(1)}, u32[]{:S(2)}, u32[]{:S(2)}) collective-permute-start(bf16[272,512]{1,0:T(8,128)(2,1)S(1)} %get-tuple-element.42), channel_id=1, source_target_pairs={{0,4},{4,1},{1,5},{5,0},{2,6},{6,3},{3,7},{7,2},{8,12},{12,9},{9,1... | collective-permute-start | bytes 835592 | tf_op jit(solution)/shard_map/ppermute | solution.py:33
  36.3 11.7 %collective-permute-start.10 = (bf16[272,512]{1,0:T(8,128)(2,1)S(1)}, bf16[272,512]{1,0:T(8,128)(2,1)S(1)}, u32[]{:S(2)}, u32[]{:S(2)}) collective-permute-start(bf16[272,512]{1,0:T(8,128)(2,1)S(1)} %get-tuple-element.44), channel_id=1, source_target_pairs={{0,5},{4,0},{1,4},{5,1},{2,7},{6,2},{3,6},{7,3},{8,13},{12,8},{9,1... | collective-permute-start | bytes 835592 | tf_op jit(solution)/shard_map/ppermute | solution.py:33
  48.2 4.1 %collective-permute-start.16 = (bf16[272,512]{1,0:T(8,128)(2,1)S(1)}, bf16[272,512]{1,0:T(8,128)(2,1)S(1)}, u32[]{:S(2)}, u32[]{:S(2)}) collective-permute-start(bf16[272,512]{1,0:T(8,128)(2,1)S(1)} %multiply_convert_fusion.refs_13_), channel_id=1, source_target_pairs={{0,2},{2,0},{1,3},{3,1},{4,6},{6,4},{5,7},{7,5},{8,10},{10,8},{9,1... | collective-permute-start | bytes 835592 | tf_op jit(solution)/shard_map/ppermute | solution.py:45
  48.7 9.3 %collective-permute-start.13 = (bf16[272,512]{1,0:T(8,128)(2,1)S(1)}, bf16[272,512]{1,0:T(8,128)(2,1)S(1)}, u32[]{:S(2)}, u32[]{:S(2)}) collective-permute-start(bf16[272,512]{1,0:T(8,128)(2,1)S(1)} %multiply_convert_fusion.refs_13_), channel_id=1, source_target_pairs={{0,4},{4,1},{1,5},{5,0},{2,6},{6,3},{3,7},{7,2},{8,12},{12,9},{9,1... | collective-permute-start | bytes 835592 | tf_op jit(solution)/shard_map/ppermute | solution.py:33
  50.1 8.0 %collective-permute-start.11 = (bf16[272,512]{1,0:T(8,128)(2,1)S(1)}, bf16[272,512]{1,0:T(8,128)(2,1)S(1)}, u32[]{:S(2)}, u32[]{:S(2)}) collective-permute-start(bf16[272,512]{1,0:T(8,128)(2,1)S(1)} %multiply_convert_fusion.refs_13_), channel_id=1, source_target_pairs={{0,5},{4,0},{1,4},{5,1},{2,7},{6,2},{3,6},{7,3},{8,13},{12,8},{9,1... | collective-permute-start | bytes 835592 | tf_op jit(solution)/shard_map/ppermute | solution.py:33
  51.4 12.7 %collective-permute-start.15 = (bf16[272,512]{1,0:T(8,128)(2,1)S(1)}, bf16[272,512]{1,0:T(8,128)(2,1)S(1)}, u32[]{:S(2)}, u32[]{:S(2)}) collective-permute-start(bf16[272,512]{1,0:T(8,128)(2,1)S(1)} %multiply_convert_fusion.refs_13_), channel_id=1, source_target_pairs={{0,1},{4,5},{1,0},{5,4},{2,3},{6,7},{3,2},{7,6},{8,9},{12,13},{9,8... | collective-permute-start | bytes 835592 | tf_op jit(solution)/shard_map/ppermute | solution.py:33
  64.1 2.1 %collective-permute-start.14 = (bf16[272,512]{1,0:T(8,128)(2,1)S(1)}, bf16[272,512]{1,0:T(8,128)(2,1)S(1)}, u32[]{:S(2)}, u32[]{:S(2)}) collective-permute-start(bf16[272,512]{1,0:T(8,128)(2,1)S(1)} %collective-permute-done.13.refs_16_), channel_id=1, source_target_pairs={{0,2},{2,0},{1,3},{3,1},{4,6},{6,4},{5,7},{7,5},{8,10},{10,8},{9,1... | collective-permute-start | bytes 835592 | tf_op jit(solution)/shard_map/ppermute | solution.py:45
  65.0 1.6 %collective-permute-start.12 = (bf16[272,512]{1,0:T(8,128)(2,1)S(1)}, bf16[272,512]{1,0:T(8,128)(2,1)S(1)}, u32[]{:S(2)}, u32[]{:S(2)}) collective-permute-start(bf16[272,512]{1,0:T(8,128)(2,1)S(1)} %collective-permute-done.11.refs_15_), channel_id=1, source_target_pairs={{0,2},{2,0},{1,3},{3,1},{4,6},{6,4},{5,7},{7,5},{8,10},{10,8},{9,1... | collective-permute-start | bytes 835592 | tf_op jit(solution)/shard_map/ppermute | solution.py:45
  65.0 2.0 %collective-permute-start.17 = (bf16[272,512]{1,0:T(8,128)(2,1)S(1)}, bf16[272,512]{1,0:T(8,128)(2,1)S(1)}, u32[]{:S(2)}, u32[]{:S(2)}) collective-permute-start(bf16[272,512]{1,0:T(8,128)(2,1)S(1)} %collective-permute-done.15.refs_15_), channel_id=1, source_target_pairs={{0,2},{2,0},{1,3},{3,1},{4,6},{6,4},{5,7},{7,5},{8,10},{10,8},{9,1... | collective-permute-start | bytes 835592 | tf_op jit(solution)/shard_map/ppermute | solution.py:45
